TPU v7x, 32 devices: a whole 2x2x4 slice. The times are simulated.
32 devices in a mesh: blk: 8 (over z, y), band: 4 (over x, core).
Axes of the slice: x: 2, y: 2, z: 4, core: 2. Of those that a mesh axis runs over, the one named last changes fastest.
Arguments:
- grid_nodes: bfloat16 [16384, 512], P(('blk', 'band')), may hold values from -6 to 6
- enc_edges: bfloat16 [32768, 512], P(('blk', 'band')), may hold values from -6 to 6
- enc_sender: int32 [32768], P(('blk', 'band')), may hold values from 0 to 511, as said below
- enc_slot: int32 [32768], P(('blk', 'band')), may hold values from 0 to 511
- enc_slot_node: int32 [32, 512], P(('blk', 'band')), may hold values from 0 to 639
- mesh_nodes: bfloat16 [5120, 512], P('blk'), may hold values from -6 to 6
- mesh_edges: bfloat16 [32768, 512], P(('blk', 'band')), may hold values from -6 to 6
- mesh_sender: int32 [32768], P(('blk', 'band')), may hold values from 0 to 63
- mesh_receiver: int32 [32768], P(('blk', 'band')), may hold values from 0 to 639
- mesh_send_node: int32 [32, 64], P(('blk', 'band')), may hold values from 0 to 639
- grid_weights: bfloat16 [2, 512, 512], replicated, may hold values from -0.25 to 0.25
- enc_edge_weights: bfloat16 [4, 512, 512], replicated, may hold values from -0.25 to 0.25
- enc_node_weights: bfloat16 [3, 512, 512], replicated, may hold values from -0.25 to 0.25
- proc_edge_weights: bfloat16 [4, 512, 512], replicated, may hold values from -0.25 to 0.25
- proc_node_weights: bfloat16 [3, 512, 512], replicated, may hold values from -0.25 to 0.25
- biases: float32 [5, 2, 512], replicated, may hold values from -3 to 3
- gains: float32 [5, 512], replicated, may hold values from 0.5 to 1.5
Outputs:
- grid_out: bfloat16 [16384, 512], P(('blk', 'band'))
- mesh_out: bfloat16 [5120, 512], P(('blk', 'band'))
Inputs may be any that keep to these rules, and one draw needn't show every extreme that they name: `enc_sender`: within each device's 1024 edges the values never fall, and every one of the device's 512 grid rows is a sender.
All inputs are finite; a program needn't handle non-finite values.
Results may differ from a plain program's by a relative error of at most 0.014.
Values may be sent and summed in bfloat16 or wider, within the bound.
No kernel may reach another device: no remote copies, remote signals or barrier semaphores. Data moves between devices by JAX's collectives and lax.ppermute only.
A program may use at most 64 MiB of HBM per device.

v0:
```python
import jax
import jax.numpy as jnp
from jax import lax
from jax.sharding import PartitionSpec as P

NEIGH = 8
CAP = 64


def shifted(block, axis, distance):
    devices = range(lax.axis_size(axis))
    route = [((i - distance) % len(devices), i) for i in devices]
    return lax.ppermute(block, axis, route)


def layer_norm(values, gain_row):
    center = values - jnp.mean(values, axis=-1, keepdims=True)
    spread = jnp.mean(center * center, axis=-1, keepdims=True)
    return center * lax.rsqrt(spread + 1e-05) * gain_row


def dense_tail(first_layer, second_weight, bias_pair, gain_row):
    hidden = jax.nn.silu(first_layer + bias_pair[0]).astype(jnp.bfloat16)
    second = jnp.dot(hidden, second_weight, preferred_element_type=jnp.float32) + bias_pair[1]
    return layer_norm(second, gain_row)


def project(node_rows, weight):
    return jnp.dot(node_rows, weight, preferred_element_type=jnp.float32)


def one_hot_sum(targets, row_count, messages):
    selector = (
        lax.broadcasted_iota(jnp.int32, (row_count, targets.shape[0]), 0) == targets[None, :]
    ).astype(jnp.bfloat16)
    return jnp.dot(selector, messages, preferred_element_type=jnp.float32)


def per_device(
    grid_nodes,
    enc_edges,
    enc_sender,
    enc_slot,
    enc_slot_node,
    mesh_nodes,
    mesh_edges,
    mesh_sender,
    mesh_receiver,
    mesh_send_node,
    grid_weights,
    enc_edge_weights,
    enc_node_weights,
    proc_edge_weights,
    proc_node_weights,
    biases,
    gains,
):
    band_index = lax.axis_index("band")
    patch_rows = mesh_nodes.shape[0]
    share_rows = patch_rows // lax.axis_size("band")
    width = mesh_nodes.shape[1]
    middle = NEIGH // 2
    slot_nodes = enc_slot_node[0]
    sender_nodes = mesh_send_node[0]
    receiver_keys = project(jnp.take(mesh_nodes, slot_nodes, axis=0), enc_edge_weights[2]).astype(
        jnp.bfloat16
    )
    receiver_keys = receiver_keys.reshape(NEIGH, CAP, width)
    key_pieces = []
    for window in range(NEIGH):
        if window == middle:
            key_pieces.append(receiver_keys[window])
        else:
            key_pieces.append(shifted(receiver_keys[window], "blk", middle - window))
    arrived_keys = jnp.concatenate(key_pieces, axis=0)
    sender_proj = project(grid_nodes, enc_edge_weights[1])
    edge_first = (
        project(enc_edges, enc_edge_weights[0])
        + jnp.take(sender_proj, enc_sender, axis=0)
        + jnp.take(arrived_keys, enc_slot, axis=0).astype(jnp.float32)
    )
    enc_message = dense_tail(edge_first, enc_edge_weights[3], biases[1], gains[1]).astype(
        jnp.bfloat16
    )
    slot_sums = one_hot_sum(enc_slot, slot_nodes.shape[0], enc_message).reshape(NEIGH, CAP, width)
    sum_pieces = []
    for window in range(NEIGH):
        if window == middle:
            sum_pieces.append(slot_sums[window])
        else:
            sum_pieces.append(
                shifted(slot_sums[window].astype(jnp.bfloat16), "blk", window - middle).astype(
                    jnp.float32
                )
            )
    landed = jnp.concatenate(sum_pieces, axis=0)
    partial_sums = jax.ops.segment_sum(landed, slot_nodes, num_segments=patch_rows)
    grid_first = project(grid_nodes, grid_weights[0])
    grid_out = (
        grid_nodes.astype(jnp.float32)
        + dense_tail(grid_first, grid_weights[1], biases[0], gains[0])
    ).astype(jnp.bfloat16)
    enc_share = lax.psum_scatter(
        partial_sums.astype(jnp.bfloat16), "band", scatter_dimension=0, tiled=True
    )
    own_nodes = lax.dynamic_slice_in_dim(mesh_nodes, band_index * share_rows, share_rows, 0)
    node_first = project(own_nodes, enc_node_weights[0]) + project(enc_share, enc_node_weights[1])
    own_mid = (
        own_nodes.astype(jnp.float32)
        + dense_tail(node_first, enc_node_weights[2], biases[2], gains[2])
    ).astype(jnp.bfloat16)
    sender_share = project(own_mid, proc_edge_weights[1]).astype(jnp.bfloat16)
    target_share = project(own_mid, proc_edge_weights[2]).astype(jnp.bfloat16)
    sender_keys, target_keys = (
        lax.all_gather(sender_share, "band", axis=0, tiled=True),
        lax.all_gather(target_share, "band", axis=0, tiled=True),
    )
    sender_rows = jnp.take(sender_keys, sender_nodes, axis=0)
    arrived_senders = lax.all_to_all(sender_rows, "blk", split_axis=0, concat_axis=0, tiled=True)
    mesh_first = (
        project(mesh_edges, proc_edge_weights[0])
        + jnp.take(arrived_senders, mesh_sender, axis=0).astype(jnp.float32)
        + jnp.take(target_keys, mesh_receiver, axis=0).astype(jnp.float32)
    )
    proc_message = dense_tail(mesh_first, proc_edge_weights[3], biases[3], gains[3]).astype(
        jnp.bfloat16
    )
    receiver_sums = one_hot_sum(mesh_receiver, patch_rows, proc_message)
    proc_share = lax.psum_scatter(
        receiver_sums.astype(jnp.bfloat16), "band", scatter_dimension=0, tiled=True
    )
    final_first = project(own_mid, proc_node_weights[0]) + project(proc_share, proc_node_weights[1])
    mesh_out = (
        own_mid.astype(jnp.float32)
        + dense_tail(final_first, proc_node_weights[2], biases[4], gains[4])
    ).astype(jnp.bfloat16)
    return (grid_out, mesh_out)


def solution(mesh):
    in_specs = (
        P(("blk", "band"), None),
        P(("blk", "band"), None),
        P(("blk", "band")),
        P(("blk", "band")),
        P(("blk", "band"), None),
        P("blk", None),
        P(("blk", "band"), None),
        P(("blk", "band")),
        P(("blk", "band")),
        P(("blk", "band"), None),
        P(),
        P(),
        P(),
        P(),
        P(),
        P(),
        P(),
    )
    out_specs = (P(("blk", "band"), None), P(("blk", "band"), None))
    return jax.shard_map(
        per_device, mesh=mesh, in_specs=in_specs, out_specs=out_specs, check_vma=False
    )
```

profile of v0, /device:TPU:0, one launch (start us, length us, event | category | flops | bytes accessed | tf_op | source)
XLA Modules:
  0.0 172.9 jit_solution(15231473944220760289)
XLA Ops:
  8.7 3.2 %gather_fusion.1 = bf16[512,512]{1,0:T(8,128)(2,1)S(1)} fusion(bf16[640,512]{1,0:T(8,128)(2,1)} %param.22, s32[1024]{0:T(1024)S(1)} %pad_clamp_fusion.1), kind=kCustom, calls=%fused_computation.1 | custom fusion | bytes 1050624 | tf_op jit(solution)/shard_map/jit(_take)/gather | solution.py:65
  13.5 4.1 %collective-permute-start = (bf16[64,512]{1,0:T(8,128)(2,1)S(1)}, bf16[64,512]{1,0:T(8,128)(2,1)S(1)}, u32[]{:S(2)}, u32[]{:S(2)}) collective-permute-start(bf16[64,512]{1,0:T(8,128)(2,1)S(1)} %get-tuple-element.20), channel_id=1, source_target_pairs={{16,0},{20,4},{24,8},{28,12},{0,16},{4,20},{8,24},{12,28},{17,1},{... | collective-permute-start | bytes 196616 | tf_op jit(solution)/shard_map/ppermute | solution.py:13
  17.7 2.5 %collective-permute-start.1 = (bf16[64,512]{1,0:T(8,128)(2,1)S(1)}, bf16[64,512]{1,0:T(8,128)(2,1)S(1)}, u32[]{:S(2)}, u32[]{:S(2)}) collective-permute-start(bf16[64,512]{1,0:T(8,128)(2,1)S(1)} %get-tuple-element.19), channel_id=1, source_target_pairs={{20,0},{24,4},{28,8},{0,12},{4,16},{8,20},{12,24},{16,28},{21,1},{... | collective-permute-start | bytes 196616 | tf_op jit(solution)/shard_map/ppermute | solution.py:13
  22.6 5.5 %collective-permute-done.1 = bf16[64,512]{1,0:T(8,128)(2,1)S(1)} collective-permute-done((bf16[64,512]{1,0:T(8,128)(2,1)S(1)}, bf16[64,512]{1,0:T(8,128)(2,1)S(1)}, u32[]{:S(2)}, u32[]{:S(2)}) %collective-permute-start.1) | collective-permute-done | bytes 65568 | tf_op jit(solution)/shard_map/ppermute | solution.py:13
  29.4 4.9 %gather_fusion = f32[1024,512]{1,0:T(8,128)} fusion(f32[512,512]{1,0:T(8,128)S(1)} %fusion.40, s32[1024]{0:T(1024)S(1)} %get-tuple-element.48), kind=kCustom, calls=%fused_computation | custom fusion | bytes 4198400 | tf_op jit(solution)/shard_map/jit(_take)/gather | solution.py:79
  38.5 2.2 %collective-permute-done.6 = bf16[64,512]{1,0:T(8,128)(2,1)S(1)} collective-permute-done((bf16[64,512]{1,0:T(8,128)(2,1)S(1)}, bf16[64,512]{1,0:T(8,128)(2,1)S(1)}, u32[]{:S(2)}, u32[]{:S(2)}) %collective-permute-start.6) | collective-permute-done | bytes 65568 | tf_op jit(solution)/shard_map/ppermute | solution.py:13
  40.7 5.1 %gather_fusion.2 = bf16[1024,512]{1,0:T(8,128)(2,1)} fusion(bf16[512,512]{1,0:T(8,128)(2,1)S(1)} %constant_dynamic-update-slice_fusion, s32[1024]{0:T(1024)S(1)} %get-tuple-element.49), kind=kCustom, calls=%fused_computation.2 | custom fusion | bytes 2101248 | tf_op jit(solution)/shard_map/jit(_take)/gather | solution.py:80
  45.8 3.8 %add_reduce_fusion.1 = (f32[1024]{0:T(1024)S(1)}, f32[1024,512]{0,1:T(8,128)S(1)}) fusion(f32[512]{0:T(512)S(1)} %bitcast.121, bf16[4,512,512]{2,1,0:T(8,128)(2,1)} %param.28, f32[1024,512]{1,0:T(8,128)} %gather_fusion, f32[512]{0:T(512)S(1)} %bitcast.136, bf16[1024,512]{1,0:T(8,128)(2,1)} %gather_fusion.2, pred[1024]{0:T(1024)(128)(4,1)S(1)} %get-tuple-element.52, ...), kind=kOutput, calls=%fused_computation.18 | convolution fusion | flops 1080556544 | bytes 7350272 | tf_op jit(solution)/shard_map/dot_general | solution.py:24
  52.3 3.7 %collective-permute-start.8 = (bf16[64,512]{1,0:T(8,128)(2,1)S(1)}, bf16[64,512]{1,0:T(8,128)(2,1)S(1)}, u32[]{:S(2)}, u32[]{:S(2)}) collective-permute-start(bf16[64,512]{1,0:T(8,128)(2,1)S(1)} %get-tuple-element.11), channel_id=1, source_target_pairs={{12,0},{16,4},{20,8},{24,12},{28,16},{0,20},{4,24},{8,28},{13,1},{... | collective-permute-start | bytes 196616 | tf_op jit(solution)/shard_map/ppermute | solution.py:13
  56.1 2.5 %collective-permute-start.9 = (bf16[64,512]{1,0:T(8,128)(2,1)S(1)}, bf16[64,512]{1,0:T(8,128)(2,1)S(1)}, u32[]{:S(2)}, u32[]{:S(2)}) collective-permute-start(bf16[64,512]{1,0:T(8,128)(2,1)S(1)} %get-tuple-element.10), channel_id=1, source_target_pairs={{8,0},{12,4},{16,8},{20,12},{24,16},{28,20},{0,24},{4,28},{9,1},{1... | collective-permute-start | bytes 196616 | tf_op jit(solution)/shard_map/ppermute | solution.py:13
  58.7 1.9 %collective-permute-start.11 = (bf16[64,512]{1,0:T(8,128)(2,1)S(1)}, bf16[64,512]{1,0:T(8,128)(2,1)S(1)}, u32[]{:S(2)}, u32[]{:S(2)}) collective-permute-start(bf16[64,512]{1,0:T(8,128)(2,1)S(1)} %get-tuple-element.8), channel_id=1, source_target_pairs={{28,0},{0,4},{4,8},{8,12},{12,16},{16,20},{20,24},{24,28},{29,1},{... | collective-permute-start | bytes 196616 | tf_op jit(solution)/shard_map/ppermute | solution.py:13
  70.2 4.6 %scatter_custom_fusion = f32[640,512]{1,0:T(8,128)S(1)} fusion(s32[512]{0:T(512)} %bitcast.126, f32[512,512]{1,0:T(8,128)} %convert_dynamic-update-slice_fusion, f32[]{:T(128)} %constant.105.clone.1), kind=kCustom, calls=%fused_computation.53 | custom fusion | flops 262144 | bytes 1311232 | tf_op jit(solution)/shard_map/scatter-add | solution.py:97
  78.4 18.2 %reduce-scatter.3.cloned.1.call-done = bf16[160,512]{1,0:T(8,128)(2,1)} async-done(((bf16[640,512]{1,0:T(8,128)(2,1)}), bf16[160,512]{1,0:T(8,128)(2,1)}) %reduce-scatter.3.cloned.1.call-update) | async-done | bytes 163856 | tf_op jit(solution)/shard_map/reduce_scatter | solution.py:103
  96.6 1.8 %fusion.114 = (f32[160]{0:T(256)S(1)}, f32[160,512]{1,0:T(8,128)S(1)}) fusion(f32[512]{0:T(512)S(1)} %bitcast.133, bf16[3,512,512]{2,1,0:T(8,128)(2,1)} %param.29, f32[160,512]{1,0:T(8,128)S(1)} %fusion.44, bf16[160,512]{1,0:T(8,128)(2,1)} %reduce-scatter.3.cloned.1.call-done, f32[512]{0:T(512)S(1)} %bitcast.134), kind=kOutput, calls=%fused_computation.173 | convolution fusion | flops 168509280 | bytes 1872512 | tf_op jit(solution)/shard_map/dot_general | solution.py:24
  101.5 7.3 %all_gather.6 = bf16[640,512]{1,0:T(8,128)(2,1)S(1)} all-gather(bf16[160,512]{1,0:T(8,128)(2,1)S(1)} %convolution_convert_fusion.2), channel_id=1, replica_groups=mesh['blk'=8,'band'=4] {'band'}, dimensions={0}, use_global_device_ids=true | all-gather | bytes 819200 | tf_op jit(solution)/shard_map/all_gather | solution.py:115
  110.2 5.5 %all-to-all-start = ((bf16[8,8,512]{2,1,0:T(8,128)(2,1)}), bf16[8,8,512]{2,1,0:T(8,128)(2,1)S(1)}, u32[]{:S(2)}, u32[]{:S(2)}) async-start(bf16[8,8,512]{2,1,0:T(8,128)(2,1)} %bitcast_select_fusion), calls=%async_computation.1 | async-start | bytes 131072 | tf_op jit(solution)/shard_map/all_to_all | solution.py:119
  115.8 7.9 %all_gather.7 = bf16[640,512]{1,0:T(8,128)(2,1)S(1)} all-gather(bf16[160,512]{1,0:T(8,128)(2,1)S(1)} %convolution_convert_fusion.1), channel_id=1, replica_groups=mesh['blk'=8,'band'=4] {'band'}, dimensions={0}, use_global_device_ids=true | all-gather | bytes 819200 | tf_op jit(solution)/shard_map/all_gather | solution.py:116
  123.7 5.0 %gather_fusion.5 = bf16[1024,512]{1,0:T(8,128)(2,1)} fusion(bf16[640,512]{1,0:T(8,128)(2,1)S(1)} %all_gather.7, s32[1024]{0:T(1024)S(1)} %get-tuple-element.51), kind=kCustom, calls=%fused_computation.5 | custom fusion | bytes 2101248 | tf_op jit(solution)/shard_map/jit(_take)/gather | solution.py:123
  128.7 5.1 %gather_fusion.4 = bf16[1024,512]{1,0:T(8,128)(2,1)} fusion(bf16[64,512]{1,0:T(8,128)(2,1)S(1)} %bitcast.114, s32[1024]{0:T(1024)S(1)} %get-tuple-element.50), kind=kCustom, calls=%fused_computation.4 | custom fusion | bytes 2101248 | tf_op jit(solution)/shard_map/jit(_take)/gather | solution.py:122
  133.8 3.8 %add_reduce_fusion = (f32[1024]{0:T(1024)S(1)}, f32[1024,512]{0,1:T(8,128)S(1)}) fusion(f32[512]{0:T(512)S(1)} %bitcast.117, bf16[4,512,512]{2,1,0:T(8,128)(2,1)} %param.30, bf16[1024,512]{1,0:T(8,128)(2,1)} %param.23, f32[512]{0:T(512)S(1)} %bitcast.132, bf16[1024,512]{1,0:T(8,128)(2,1)} %gather_fusion.5, bf16[1024,512]{1,0:T(8,128)(2,1)} %gather_fusion.4, ...), kind=kOutput, calls=%fused_computation.17 | convolution fusion | flops 1081080832 | bytes 6301696 | tf_op jit(solution)/shard_map/dot_general | solution.py:24
  138.0 1.9 %fusion.2 = bf16[640,512]{1,0:T(8,128)(2,1)} fusion(s32[1024]{0:T(1024)S(1)} %copy-done.8, f32[1024,512]{0,1:T(8,128)S(1)} %get-tuple-element.45, f32[512]{0:T(512)S(1)} %bitcast.131, f32[1024]{0:T(1024)S(1)} %add_rsqrt_fusion, f32[1024]{0:T(1024)S(1)} %broadcast_multiply_fusion, f32[512]{0:T(512)S(1)} %bitcast.119), kind=kOutput, calls=%fused_computation.21 | convolution fusion | flops 674693120 | bytes 2768896 | tf_op jit(solution)/shard_map/dot_general | solution.py:36
  139.9 2.4 %fusion.108 = (f32[512]{0:T(512)S(1)}, f32[512,512]{0,1:T(8,128)S(1)}) fusion(f32[512]{0:T(512)S(1)} %bitcast.129, bf16[2,512,512]{2,1,0:T(8,128)(2,1)} %param.27, bf16[512,512]{1,0:T(8,128)(2,1)} %param.17, f32[512]{0:T(512)S(1)} %bitcast.130), kind=kOutput, calls=%fused_computation.171 | convolution fusion | flops 538967552 | bytes 2627584 | tf_op jit(solution)/shard_map/dot_general | solution.py:24
  145.3 17.9 %reduce-scatter.5.cloned.1.call-done = bf16[160,512]{1,0:T(8,128)(2,1)} async-done(((bf16[640,512]{1,0:T(8,128)(2,1)}), bf16[160,512]{1,0:T(8,128)(2,1)}) %reduce-scatter.5.cloned.1.call-update) | async-done | bytes 163856 | tf_op jit(solution)/shard_map/reduce_scatter | solution.py:129
  163.2 1.8 %fusion.119 = (f32[160]{0:T(256)S(1)}, f32[160,512]{1,0:T(8,128)S(1)}) fusion(f32[512]{0:T(512)S(1)} %bitcast.128, bf16[3,512,512]{2,1,0:T(8,128)(2,1)} %param.31, f32[160,512]{1,0:T(8,128)S(1)} %fusion.34, bf16[160,512]{1,0:T(8,128)(2,1)} %reduce-scatter.5.cloned.1.call-done, f32[512]{0:T(512)S(1)} %bitcast.127), kind=kOutput, calls=%fused_computation.174 | convolution fusion | flops 168509280 | bytes 1872512 | tf_op jit(solution)/shard_map/dot_general | solution.py:24
  (111 shorter events, 35.7 us)
Async XLA Ops:
  7.2 38.7 %copy-start = (bf16[1024,512]{1,0:T(8,128)(2,1)S(1)}, bf16[1024,512]{1,0:T(8,128)(2,1)}, u32[]{:S(2)}) copy-start(bf16[1024,512]{1,0:T(8,128)(2,1)} %param.18) | copy-start | bytes 3145732
  7.2 89.5 %reduce-scatter.3.cloned.1.call-start = ((), (), s32[]{:S(2)}) async-start(), calls=%async_computation.3 | async-start | bytes 819200 | tf_op jit(solution)/shard_map/reduce_scatter | solution.py:103
  11.9 10.7 %copy-start.9 = (f32[5,512]{1,0:T(8,128)S(1)}, f32[5,512]{1,0:T(8,128)}, u32[]{:S(2)}) copy-start(f32[5,512]{1,0:T(8,128)} %param.33) | copy-start | bytes 30724
  11.9 10.7 %copy-start.5 = (s32[1024]{0:T(1024)S(1)}, s32[1024]{0:T(1024)}, u32[]{:S(2)}) copy-start(s32[1024]{0:T(1024)} %param.19) | copy-start | bytes 12292
  11.9 10.7 %copy-start.6 = (s32[1024]{0:T(1024)S(1)}, s32[1024]{0:T(1024)}, u32[]{:S(2)}) copy-start(s32[1024]{0:T(1024)} %param.20) | copy-start | bytes 12292
  13.5 9.1 %collective-permute-start = (bf16[64,512]{1,0:T(8,128)(2,1)S(1)}, bf16[64,512]{1,0:T(8,128)(2,1)S(1)}, u32[]{:S(2)}, u32[]{:S(2)}) collective-permute-start(bf16[64,512]{1,0:T(8,128)(2,1)S(1)} %get-tuple-element.20), channel_id=1, source_target_pairs={{16,0},{20,4},{24,8},{28,12},{0,16},{4,20},{8,24},{12,28},{17,1},{... | collective-permute-start | bytes 196616 | tf_op jit(solution)/shard_map/ppermute | solution.py:13
  17.7 10.4 %collective-permute-start.1 = (bf16[64,512]{1,0:T(8,128)(2,1)S(1)}, bf16[64,512]{1,0:T(8,128)(2,1)S(1)}, u32[]{:S(2)}, u32[]{:S(2)}) collective-permute-start(bf16[64,512]{1,0:T(8,128)(2,1)S(1)} %get-tuple-element.19), channel_id=1, source_target_pairs={{20,0},{24,4},{28,8},{0,12},{4,16},{8,20},{12,24},{16,28},{21,1},{... | collective-permute-start | bytes 196616 | tf_op jit(solution)/shard_map/ppermute | solution.py:13
  20.2 7.9 %collective-permute-start.2 = (bf16[64,512]{1,0:T(8,128)(2,1)S(1)}, bf16[64,512]{1,0:T(8,128)(2,1)S(1)}, u32[]{:S(2)}, u32[]{:S(2)}) collective-permute-start(bf16[64,512]{1,0:T(8,128)(2,1)S(1)} %get-tuple-element.18), channel_id=1, source_target_pairs={{24,0},{28,4},{0,8},{4,12},{8,16},{12,20},{16,24},{20,28},{25,1},{... | collective-permute-start | bytes 196616 | tf_op jit(solution)/shard_map/ppermute | solution.py:13
  20.2 7.9 %collective-permute-start.3 = (bf16[64,512]{1,0:T(8,128)(2,1)S(1)}, bf16[64,512]{1,0:T(8,128)(2,1)S(1)}, u32[]{:S(2)}, u32[]{:S(2)}) collective-permute-start(bf16[64,512]{1,0:T(8,128)(2,1)S(1)} %get-tuple-element.17), channel_id=1, source_target_pairs={{28,0},{0,4},{4,8},{8,12},{12,16},{16,20},{20,24},{24,28},{29,1},{... | collective-permute-start | bytes 196616 | tf_op jit(solution)/shard_map/ppermute | solution.py:13
  28.2 8.7 %collective-permute-start.4 = (bf16[64,512]{1,0:T(8,128)(2,1)S(1)}, bf16[64,512]{1,0:T(8,128)(2,1)S(1)}, u32[]{:S(2)}, u32[]{:S(2)}) collective-permute-start(bf16[64,512]{1,0:T(8,128)(2,1)S(1)} %get-tuple-element.15), channel_id=1, source_target_pairs={{4,0},{8,4},{12,8},{16,12},{20,16},{24,20},{28,24},{0,28},{5,1},{9... | collective-permute-start | bytes 196616 | tf_op jit(solution)/shard_map/ppermute | solution.py:13
  34.3 4.3 %collective-permute-start.5 = (bf16[64,512]{1,0:T(8,128)(2,1)S(1)}, bf16[64,512]{1,0:T(8,128)(2,1)S(1)}, u32[]{:S(2)}, u32[]{:S(2)}) collective-permute-start(bf16[64,512]{1,0:T(8,128)(2,1)S(1)} %get-tuple-element.14), channel_id=1, source_target_pairs={{8,0},{12,4},{16,8},{20,12},{24,16},{28,20},{0,24},{4,28},{9,1},{1... | collective-permute-start | bytes 196616 | tf_op jit(solution)/shard_map/ppermute | solution.py:13
  35.6 5.2 %collective-permute-start.6 = (bf16[64,512]{1,0:T(8,128)(2,1)S(1)}, bf16[64,512]{1,0:T(8,128)(2,1)S(1)}, u32[]{:S(2)}, u32[]{:S(2)}) collective-permute-start(bf16[64,512]{1,0:T(8,128)(2,1)S(1)} %get-tuple-element.13), channel_id=1, source_target_pairs={{12,0},{16,4},{20,8},{24,12},{28,16},{0,20},{4,24},{8,28},{13,1},{... | collective-permute-start | bytes 196616 | tf_op jit(solution)/shard_map/ppermute | solution.py:13
  51.0 9.6 %collective-permute-start.7 = (bf16[64,512]{1,0:T(8,128)(2,1)S(1)}, bf16[64,512]{1,0:T(8,128)(2,1)S(1)}, u32[]{:S(2)}, u32[]{:S(2)}) collective-permute-start(bf16[64,512]{1,0:T(8,128)(2,1)S(1)} %get-tuple-element.12), channel_id=1, source_target_pairs={{16,0},{20,4},{24,8},{28,12},{0,16},{4,20},{8,24},{12,28},{17,1},{... | collective-permute-start | bytes 196616 | tf_op jit(solution)/shard_map/ppermute | solution.py:13
  52.3 9.0 %collective-permute-start.8 = (bf16[64,512]{1,0:T(8,128)(2,1)S(1)}, bf16[64,512]{1,0:T(8,128)(2,1)S(1)}, u32[]{:S(2)}, u32[]{:S(2)}) collective-permute-start(bf16[64,512]{1,0:T(8,128)(2,1)S(1)} %get-tuple-element.11), channel_id=1, source_target_pairs={{12,0},{16,4},{20,8},{24,12},{28,16},{0,20},{4,24},{8,28},{13,1},{... | collective-permute-start | bytes 196616 | tf_op jit(solution)/shard_map/ppermute | solution.py:13
  56.1 7.6 %collective-permute-start.9 = (bf16[64,512]{1,0:T(8,128)(2,1)S(1)}, bf16[64,512]{1,0:T(8,128)(2,1)S(1)}, u32[]{:S(2)}, u32[]{:S(2)}) collective-permute-start(bf16[64,512]{1,0:T(8,128)(2,1)S(1)} %get-tuple-element.10), channel_id=1, source_target_pairs={{8,0},{12,4},{16,8},{20,12},{24,16},{28,20},{0,24},{4,28},{9,1},{1... | collective-permute-start | bytes 196616 | tf_op jit(solution)/shard_map/ppermute | solution.py:13
  58.6 5.7 %collective-permute-start.10 = (bf16[64,512]{1,0:T(8,128)(2,1)S(1)}, bf16[64,512]{1,0:T(8,128)(2,1)S(1)}, u32[]{:S(2)}, u32[]{:S(2)}) collective-permute-start(bf16[64,512]{1,0:T(8,128)(2,1)S(1)} %get-tuple-element.9), channel_id=1, source_target_pairs={{4,0},{8,4},{12,8},{16,12},{20,16},{24,20},{28,24},{0,28},{5,1},{9... | collective-permute-start | bytes 196616 | tf_op jit(solution)/shard_map/ppermute | solution.py:13
  58.7 7.7 %collective-permute-start.11 = (bf16[64,512]{1,0:T(8,128)(2,1)S(1)}, bf16[64,512]{1,0:T(8,128)(2,1)S(1)}, u32[]{:S(2)}, u32[]{:S(2)}) collective-permute-start(bf16[64,512]{1,0:T(8,128)(2,1)S(1)} %get-tuple-element.8), channel_id=1, source_target_pairs={{28,0},{0,4},{4,8},{8,12},{12,16},{16,20},{20,24},{24,28},{29,1},{... | collective-permute-start | bytes 196616 | tf_op jit(solution)/shard_map/ppermute | solution.py:13
  60.6 6.5 %collective-permute-start.12 = (bf16[64,512]{1,0:T(8,128)(2,1)S(1)}, bf16[64,512]{1,0:T(8,128)(2,1)S(1)}, u32[]{:S(2)}, u32[]{:S(2)}) collective-permute-start(bf16[64,512]{1,0:T(8,128)(2,1)S(1)} %get-tuple-element.7), channel_id=1, source_target_pairs={{24,0},{28,4},{0,8},{4,12},{8,16},{12,20},{16,24},{20,28},{25,1},{... | collective-permute-start | bytes 196616 | tf_op jit(solution)/shard_map/ppermute | solution.py:13
  61.3 8.3 %collective-permute-start.13 = (bf16[64,512]{1,0:T(8,128)(2,1)S(1)}, bf16[64,512]{1,0:T(8,128)(2,1)S(1)}, u32[]{:S(2)}, u32[]{:S(2)}) collective-permute-start(bf16[64,512]{1,0:T(8,128)(2,1)S(1)} %get-tuple-element.6), channel_id=1, source_target_pairs={{20,0},{24,4},{28,8},{0,12},{4,16},{8,20},{12,24},{16,28},{21,1},{... | collective-permute-start | bytes 196616 | tf_op jit(solution)/shard_map/ppermute | solution.py:13
  67.9 9.2 %copy-start.7 = (s32[1024]{0:T(1024)S(1)}, s32[1024]{0:T(1024)}, u32[]{:S(2)}) copy-start(s32[1024]{0:T(1024)} %param.24) | copy-start | bytes 12292
  67.9 9.2 %copy-start.8 = (s32[1024]{0:T(1024)S(1)}, s32[1024]{0:T(1024)}, u32[]{:S(2)}) copy-start(s32[1024]{0:T(1024)} %param.25) | copy-start | bytes 12292
  67.9 9.3 %copy-start.1 = (bf16[640,512]{1,0:T(8,128)(2,1)S(1)}, bf16[640,512]{1,0:T(8,128)(2,1)}, u32[]{:S(2)}) copy-start(bf16[640,512]{1,0:T(8,128)(2,1)} %param.22) | copy-start | bytes 1966084
  110.2 18.5 %all-to-all-start = ((bf16[8,8,512]{2,1,0:T(8,128)(2,1)}), bf16[8,8,512]{2,1,0:T(8,128)(2,1)S(1)}, u32[]{:S(2)}, u32[]{:S(2)}) async-start(bf16[8,8,512]{2,1,0:T(8,128)(2,1)} %bitcast_select_fusion), calls=%async_computation.1 | async-start | bytes 131072 | tf_op jit(solution)/shard_map/all_to_all | solution.py:119
  115.7 47.5 %reduce-scatter.5.cloned.1.call-start = ((), (), s32[]{:S(2)}) async-start(), calls=%async_computation.4 | async-start | bytes 819200 | tf_op jit(solution)/shard_map/reduce_scatter | solution.py:129
  (4 other events, 29.3 us)
Sparse Core Ops, SparseCore 0:
  75.9 20.7 reduce-scatter.2
  140.0 23.1 reduce-scatter.4
where the time goes:
time: 174 us; the launch traced here: 173 us
  waiting for transfers between devices  48.1 us (28%)
  starting transfers between devices  28.2 us (16%)
  local copies, waits for them, and re-layouts  26.6 us (15%)
  matrix products  24.8 us (14%)
  other arithmetic  15.5 us (9%)
  blocking collectives  15.2 us (9%)
  between operations  14.5 us (8%)
    ppermute x14, starting transfers between devices, shifted(): return lax.ppermute(block, axis, route)  22.6 us
    reduce_scatter x1, waiting for transfers between devices, per_device(): lax.psum_scatter(partial_sums.astype(jnp.bfloat16), 'band', scatter_dimen...  18.2 us
    reduce_scatter x1, waiting for transfers between devices, per_device(): lax.psum_scatter(receiver_sums.astype(jnp.bfloat16), 'band', scatter_dime...  17.9 us
    dot_general x5, matrix products, dense_tail(): jnp.dot(hidden, second_weight, preferred_element_type=jnp.float32)  13.7 us
    ppermute x14, waiting for transfers between devices, shifted(): return lax.ppermute(block, axis, route)  11.9 us
    dot_general x6, matrix products, project(): return jnp.dot(node_rows, weight, preferred_element_type=jnp.float32)  8.22 us
    all_gather x1, blocking collectives, per_device(): lax.all_gather(target_share, 'band', axis=0, tiled=True)  7.9 us
    all_gather x1, blocking collectives, per_device(): lax.all_gather(sender_share, 'band', axis=0, tiled=True)  7.32 us
  transfers between devices with their start and end apart: 17, of which 7 were waited for; matrix products, arithmetic and copies ran while one was open for 14% of the time, Pallas kernels for 0%

commit v1 on v0

v1 whole, which is shorter than its diff:
```python
import jax
import jax.numpy as jnp
from jax import lax
from jax.sharding import PartitionSpec as P


NEIGH = 8
BF16 = jnp.bfloat16
F32 = jnp.float32


def layer_norm(values, gain_row):
    center = values - jnp.mean(values, axis=-1, keepdims=True)
    spread = jnp.mean(center * center, axis=-1, keepdims=True)
    return center * lax.rsqrt(spread + 1e-05) * gain_row


def dense_tail(first_layer, second_weight, bias_pair, gain_row):
    hidden = jax.nn.silu(first_layer + bias_pair[0]).astype(BF16)
    second = project(hidden, second_weight) + bias_pair[1]
    return layer_norm(second, gain_row)


def project(node_rows, weight):
    return jnp.dot(node_rows, weight, preferred_element_type=F32)


def pick_rows(indices, table):
    hot = (indices[:, None] == lax.broadcasted_iota(jnp.int32, (1, table.shape[0]), 1)).astype(BF16)
    return project(hot, table)


def sum_rows(indices, row_count, rows):
    hot = (lax.broadcasted_iota(jnp.int32, (row_count, 1), 0) == indices[None, :]).astype(BF16)
    return project(hot, rows)


def swap(rows, axis, mask):
    return lax.ppermute(rows, axis, [(i, i ^ mask) for i in range(lax.axis_size(axis))])


def window_exchange(blocks, back):
    blk_count = lax.axis_size("blk")
    pieces = []
    for window in range(NEIGH):
        if blk_count == NEIGH:
            pieces.append(swap(blocks[window], "blk", window) if window else blocks[0])
        else:
            distance = window - NEIGH // 2
            distance = distance if back else -distance
            route = [((i - distance) % blk_count, i) for i in range(blk_count)]
            pieces.append(lax.ppermute(blocks[window], "blk", route) if distance else blocks[window])
    return jnp.concatenate(pieces, axis=0)


def body(
    grid_nodes,
    enc_edges,
    enc_sender,
    enc_slot,
    enc_slot_node,
    mesh_nodes,
    mesh_edges,
    mesh_sender,
    mesh_receiver,
    mesh_send_node,
    grid_weights,
    enc_edge_weights,
    enc_node_weights,
    proc_edge_weights,
    proc_node_weights,
    biases,
    gains,
):
    blk_count, band_count = lax.axis_size("blk"), lax.axis_size("band")
    blk_index, band_index = lax.axis_index("blk"), lax.axis_index("band")
    patch_rows, width = mesh_nodes.shape
    share_rows = patch_rows // band_count
    slots = enc_slot_node.shape[1]
    cap = slots // NEIGH
    mcap = mesh_send_node.shape[1] // blk_count

    slot_nodes = enc_slot_node.reshape(NEIGH, cap)
    slot_place = enc_slot
    if blk_count == NEIGH:
        masks = jnp.arange(NEIGH)
        slot_nodes = jnp.take(slot_nodes, (blk_index - (blk_index ^ masks) + NEIGH // 2) % NEIGH, axis=0)
        patch = (blk_index + enc_slot // cap - NEIGH // 2) % NEIGH
        slot_place = (patch ^ blk_index) * cap + enc_slot % cap
    slot_nodes = slot_nodes.reshape(slots)

    slot_rows = pick_rows(slot_nodes, mesh_nodes).astype(BF16)
    slot_keys = project(slot_rows, enc_edge_weights[2]).astype(BF16).reshape(NEIGH, cap, width)
    arrived_keys = window_exchange(slot_keys, False)

    sender_rows = pick_rows(enc_sender, grid_nodes).astype(BF16)
    edge_part = project(enc_edges, enc_edge_weights[0]) + project(sender_rows, enc_edge_weights[1])
    grid_out = (
        grid_nodes.astype(F32)
        + dense_tail(project(grid_nodes, grid_weights[0]), grid_weights[1], biases[0], gains[0])
    ).astype(BF16)

    edge_first = edge_part + pick_rows(slot_place, arrived_keys)
    enc_message = dense_tail(edge_first, enc_edge_weights[3], biases[1], gains[1]).astype(BF16)
    slot_sums = sum_rows(slot_place, slots, enc_message).astype(BF16).reshape(NEIGH, cap, width)
    landed = window_exchange(slot_sums, True)
    partial_sums = sum_rows(slot_nodes, patch_rows, landed)

    low = band_index % 2
    quarters = partial_sums.reshape(band_count // 2, 2, share_rows, width)
    kept = lax.dynamic_index_in_dim(quarters, low, 1, False)
    given = lax.dynamic_index_in_dim(quarters, 1 - low, 1, False).astype(BF16)
    half = (kept + swap(given, "band", 1).astype(F32)).astype(BF16)
    mask = 2
    while mask < band_count:
        half = (half.astype(F32) + swap(half, "band", mask).astype(F32)).astype(BF16)
        mask *= 2
    half_rows = patch_rows // 2
    enc_total = half.reshape(half_rows, width)
    own_nodes = lax.dynamic_index_in_dim(
        mesh_nodes.reshape(band_count // 2, 2, share_rows, width), low, 1, False
    ).reshape(half_rows, width)
    node_first = project(own_nodes, enc_node_weights[0]) + project(enc_total, enc_node_weights[1])
    half_mid = (
        own_nodes.astype(F32) + dense_tail(node_first, enc_node_weights[2], biases[2], gains[2])
    ).astype(BF16)
    other_mid = swap(half_mid, "band", 1)
    all_mid = jnp.concatenate([half_mid, other_mid], axis=0)

    def mid_place(node):
        share = node // share_rows
        return ((share % 2) ^ low) * half_rows + (share // 2) * share_rows + node % share_rows

    send_nodes = jnp.take(mesh_send_node.reshape(blk_count, mcap), blk_index ^ jnp.arange(blk_count), axis=0)
    wanted = pick_rows(mid_place(send_nodes.reshape(-1)), all_mid).astype(BF16)
    senders = project(wanted, proc_edge_weights[1]).astype(BF16).reshape(blk_count, mcap, width)
    mask = 1
    while mask < blk_count:
        view = senders.reshape(blk_count // (2 * mask), 2, mask * mcap, width)
        got = swap(view[:, 1], "blk", mask)
        senders = jnp.stack([view[:, 0], got], axis=1)
        mask *= 2
    arrived_senders = senders.reshape(blk_count * mcap, width)
    sender_place = ((mesh_sender // mcap) ^ blk_index) * mcap + mesh_sender % mcap

    target_keys = project(all_mid, proc_edge_weights[2]).astype(BF16)
    mesh_first = (
        project(mesh_edges, proc_edge_weights[0])
        + pick_rows(sender_place, arrived_senders)
        + pick_rows(mid_place(mesh_receiver), target_keys)
    )
    proc_message = dense_tail(mesh_first, proc_edge_weights[3], biases[3], gains[3]).astype(BF16)
    shares = sum_rows(mesh_receiver, patch_rows, proc_message)
    shares = shares.reshape(band_count, share_rows, width)
    place, mask = band_index, 1
    while mask < band_count:
        pairs = shares.reshape(-1, 2, share_rows, width)
        kept = lax.dynamic_index_in_dim(pairs, place % 2, 1, False)
        given = lax.dynamic_index_in_dim(pairs, 1 - place % 2, 1, False).astype(BF16)
        shares = kept + swap(given, "band", mask).astype(F32)
        place, mask = place // 2, mask * 2
    proc_total = shares.reshape(share_rows, width).astype(BF16)
    own_mid = lax.dynamic_index_in_dim(
        half_mid.reshape(band_count // 2, share_rows, width), band_index // 2, 0, False
    )
    final_first = project(own_mid, proc_node_weights[0]) + project(proc_total, proc_node_weights[1])
    mesh_out = (
        own_mid.astype(F32) + dense_tail(final_first, proc_node_weights[2], biases[4], gains[4])
    ).astype(BF16)
    return (grid_out, mesh_out)


def solution(mesh):
    rows = P(("blk", "band"), None)
    flat = P(("blk", "band"))
    in_specs = (rows, rows, flat, flat, rows, P("blk", None), rows, flat, flat, rows) + (P(),) * 7
    return jax.shard_map(
        body, mesh=mesh, in_specs=in_specs, out_specs=(rows, rows), check_vma=False
    )
```

time: 174 us -> 128 us (0.74)
  waiting for transfers between devices: 48.1 us -> 24.8 us
  blocking collectives: 15.2 us -> 0 us
  matrix products: 24.8 us -> 38.3 us
  between operations: 14.5 us -> 1.17 us
  local copies, waits for them, and re-layouts: 26.6 us -> 18.4 us
    reduce_scatter x2 -> x0, waiting for transfers between devices: 36.1 us -> none  [the longest x1 18.2 us: per_device(): lax.psum_scatter(partial_sums.astype(jnp.bfloat16), 'band', scatter_dimen...]
    gather x6 -> x2, local copies, waits for them, and re-layouts: 24 us -> 1.11 us  [the longest x1 0.55 us: body(): jnp.take(slot_nodes, (blk_index - (blk_index ^ masks) + NEIGH // 2) % NEI...]
    all_gather x2 -> x0, blocking collectives: 15.2 us -> none  [the longest x1 7.9 us: per_device(): lax.all_gather(target_share, 'band', axis=0, tiled=True)]
    dot_general x13 -> x16, matrix products: 24.8 us -> 38.3 us  [project(): return jnp.dot(node_rows, weight, preferred_element_type=F32)]
    ppermute x14 -> x22, waiting for transfers between devices: 11.9 us -> 24.8 us  [swap(): lax.ppermute(rows, axis, [(i, i ^ mask) for i in range(lax.axis_size(axis...]
    unnamed x32 -> x78, local copies, waits for them, and re-layouts: 2.48 us -> 11.8 us
    ppermute x14 -> x22, starting transfers between devices: 22.6 us -> 28.5 us  [swap(): lax.ppermute(rows, axis, [(i, i ^ mask) for i in range(lax.axis_size(axis...]
    all_to_all x1 -> x0, starting transfers between devices: 5.52 us -> none  [per_device(): lax.all_to_all(sender_rows, 'blk', split_axis=0, concat_axis=0, tiled=True)]
  transfers between devices with their start and end apart: 17 -> 22, of which waited for: 7 -> 10; matrix products, arithmetic and copies ran while one was open for 14% -> 29% of each run, Pallas kernels for 0% -> 0%
where the time goes in v1:
time: 128 us; the launch traced here: 127 us
  matrix products  38.3 us (30%)
  starting transfers between devices  28.5 us (22%)
  waiting for transfers between devices  24.8 us (19%)
  local copies, waits for them, and re-layouts  18.4 us (14%)
  other arithmetic  16.4 us (13%)
    dot_general x16, matrix products, project(): return jnp.dot(node_rows, weight, preferred_element_type=F32)  38.3 us
    ppermute x22, starting transfers between devices, swap(): lax.ppermute(rows, axis, [(i, i ^ mask) for i in range(lax.axis_size(axis...  28.5 us
    ppermute x22, waiting for transfers between devices, swap(): lax.ppermute(rows, axis, [(i, i ^ mask) for i in range(lax.axis_size(axis...  24.8 us
    unnamed x78, local copies, waits for them, and re-layouts  11.8 us
    reduce_sum x5, other arithmetic, layer_norm(): spread = jnp.mean(center * center, axis=-1, keepdims=True)  4.78 us
    unnamed x2, other arithmetic  3.12 us
  transfers between devices with their start and end apart: 22, of which 10 were waited for; matrix products, arithmetic and copies ran while one was open for 29% of the time, Pallas kernels for 0%

profile of v1, /device:TPU:0, one launch (start us, length us, event | category | flops | bytes accessed | tf_op | source)
XLA Modules:
  0.0 127.5 jit_solution(6523162450814526311)
XLA Ops:
  3.9 2.2 %convolution_convert_fusion.1 = bf16[512,512]{1,0:T(8,128)(2,1)S(1)} fusion(bf16[640,512]{1,0:T(8,128)(2,1)} %param.22, s32[512]{0:T(512)S(1)} %select_n.194, bf16[4,512,512]{2,1,0:T(8,128)(2,1)} %param.28), kind=kOutput, calls=%fused_computation.34 | convolution fusion | flops 604831744 | bytes 1705984 | tf_op jit(solution)/shard_map/dot_general | solution.py:25
  6.8 3.0 %collective-permute-start = (bf16[64,512]{1,0:T(8,128)(2,1)}, bf16[64,512]{1,0:T(8,128)(2,1)}, u32[]{:S(2)}, u32[]{:S(2)}) collective-permute-start(bf16[64,512]{1,0:T(8,128)(2,1)} %get-tuple-element.20), channel_id=1, source_target_pairs={{0,4},{4,0},{8,12},{12,8},{16,20},{20,16},{24,28},{28,24},{1,5},{5... | collective-permute-start | bytes 196616 | tf_op jit(solution)/shard_map/ppermute | solution.py:39
  11.4 3.0 %collective-permute-start.3 = (bf16[64,512]{1,0:T(8,128)(2,1)S(1)}, bf16[64,512]{1,0:T(8,128)(2,1)}, u32[]{:S(2)}, u32[]{:S(2)}) collective-permute-start(bf16[64,512]{1,0:T(8,128)(2,1)S(1)} %get-tuple-element.17), channel_id=1, source_target_pairs={{0,16},{4,20},{8,24},{12,28},{16,0},{20,4},{24,8},{28,12},{1,17},{... | collective-permute-start | bytes 196616 | tf_op jit(solution)/shard_map/ppermute | solution.py:39
  23.2 3.9 %fusion.6 = f32[1024,512]{1,0:T(8,128)} fusion(bf16[512,512]{1,0:T(8,128)(2,1)} %param.17, s32[1024]{0:T(1024)} %param.19, bf16[4,512,512]{2,1,0:T(8,128)(2,1)} %param.28), kind=kOutput, calls=%fused_computation.21 | convolution fusion | flops 1074790400 | bytes 3149824 | tf_op jit(solution)/shard_map/dot_general | solution.py:25
  29.7 3.6 %collective-permute-start.5 = (bf16[64,512]{1,0:T(8,128)(2,1)S(1)}, bf16[64,512]{1,0:T(8,128)(2,1)S(1)}, u32[]{:S(2)}, u32[]{:S(2)}) collective-permute-start(bf16[64,512]{1,0:T(8,128)(2,1)S(1)} %get-tuple-element.15), channel_id=1, source_target_pairs={{0,24},{4,28},{8,16},{12,20},{16,8},{20,12},{24,0},{28,4},{1,25},{... | collective-permute-start | bytes 196616 | tf_op jit(solution)/shard_map/ppermute | solution.py:39
  42.4 4.8 %add_reduce_fusion.1 = (f32[1024]{0:T(1024)S(1)}, f32[1024,512]{0,1:T(8,128)}) fusion(f32[512]{0:T(512)} %bitcast.168, bf16[4,512,512]{2,1,0:T(8,128)(2,1)} %param.28, f32[1024,512]{1,0:T(8,128)S(1)} %fusion.54, f32[1024,512]{1,0:T(8,128)} %fusion.6, bf16[512,512]{1,0:T(8,128)(2,1)} %constant_dynamic-update-slice_fusion, f32[512]{0:T(512)} %bitcast.179, ...), kind=kOutput, calls=%fused_computation.19 | convolution fusion | flops 1079507968 | bytes 7352320 | tf_op jit(solution)/shard_map/dot_general | solution.py:25
  47.2 2.1 %multiply_reduce_fusion.1 = f32[1024]{0:T(1024)S(1)} fusion(f32[1024,512]{0,1:T(8,128)} %get-tuple-element.48, f32[1024]{0:T(1024)S(1)} %broadcast_multiply_fusion.1, f32[512]{0:T(512)S(1)} %bitcast.169), kind=kLoop, calls=%fused_computation.10 | loop fusion | flops 2096128 | bytes 2107392 | tf_op jit(solution)/shard_map/reduce_sum | solution.py:14
  52.1 2.2 %collective-permute-start.9 = (bf16[64,512]{1,0:T(8,128)(2,1)S(1)}, bf16[64,512]{1,0:T(8,128)(2,1)S(1)}, u32[]{:S(2)}, u32[]{:S(2)}) collective-permute-start(bf16[64,512]{1,0:T(8,128)(2,1)S(1)} %get-tuple-element.10), channel_id=1, source_target_pairs={{0,12},{4,8},{8,4},{12,0},{16,28},{20,24},{24,20},{28,16},{1,13},{... | collective-permute-start | bytes 196616 | tf_op jit(solution)/shard_map/ppermute | solution.py:39
  54.3 2.0 %collective-permute-start.10 = (bf16[64,512]{1,0:T(8,128)(2,1)S(1)}, bf16[64,512]{1,0:T(8,128)(2,1)S(1)}, u32[]{:S(2)}, u32[]{:S(2)}) collective-permute-start(bf16[64,512]{1,0:T(8,128)(2,1)S(1)} %get-tuple-element.9), channel_id=1, source_target_pairs={{0,16},{4,20},{8,24},{12,28},{16,0},{20,4},{24,8},{28,12},{1,17},{... | collective-permute-start | bytes 196616 | tf_op jit(solution)/shard_map/ppermute | solution.py:39
  57.9 3.6 %collective-permute-start.12 = (bf16[64,512]{1,0:T(8,128)(2,1)S(1)}, bf16[64,512]{1,0:T(8,128)(2,1)S(1)}, u32[]{:S(2)}, u32[]{:S(2)}) collective-permute-start(bf16[64,512]{1,0:T(8,128)(2,1)S(1)} %get-tuple-element.7), channel_id=1, source_target_pairs={{0,24},{4,28},{8,16},{12,20},{16,8},{20,12},{24,0},{28,4},{1,25},{... | collective-permute-start | bytes 196616 | tf_op jit(solution)/shard_map/ppermute | solution.py:39
  63.0 2.8 %collective-permute-done.11 = bf16[64,512]{1,0:T(8,128)(2,1)S(1)} collective-permute-done((bf16[64,512]{1,0:T(8,128)(2,1)S(1)}, bf16[64,512]{1,0:T(8,128)(2,1)S(1)}, u32[]{:S(2)}, u32[]{:S(2)}) %collective-permute-start.11) | collective-permute-done | bytes 65568 | tf_op jit(solution)/shard_map/ppermute | solution.py:39
  65.9 2.7 %collective-permute-done.13 = bf16[64,512]{1,0:T(8,128)(2,1)S(1)} collective-permute-done((bf16[64,512]{1,0:T(8,128)(2,1)S(1)}, bf16[64,512]{1,0:T(8,128)(2,1)S(1)}, u32[]{:S(2)}, u32[]{:S(2)}) %collective-permute-start.13) | collective-permute-done | bytes 65568 | tf_op jit(solution)/shard_map/ppermute | solution.py:39
  69.3 2.2 %fusion.56 = f32[320,512]{1,0:T(8,128)} fusion(bf16[320,512]{1,0:T(8,128)(2,1)S(1)} %bitcast.146, bf16[3,512,512]{2,1,0:T(8,128)(2,1)} %param.29), kind=kOutput, calls=%fused_computation.90 | convolution fusion | flops 167772160 | bytes 1507328 | tf_op jit(solution)/shard_map/dot_general | solution.py:25
  73.2 2.2 %fusion.151 = (f32[512]{0:T(512)S(1)}, f32[512,512]{0,1:T(8,128)S(1)}) fusion(f32[512]{0:T(512)S(1)} %bitcast.177, bf16[2,512,512]{2,1,0:T(8,128)(2,1)} %param.27, bf16[512,512]{1,0:T(8,128)(2,1)S(1)} %copy-done.5, f32[512]{0:T(512)S(1)} %bitcast.178), kind=kOutput, calls=%fused_computation.263 | convolution fusion | flops 538967552 | bytes 2627584 | tf_op jit(solution)/shard_map/dot_general | solution.py:25
  75.4 6.5 %collective-permute-done.15 = bf16[2,160,512]{2,1,0:T(8,128)(2,1)} collective-permute-done((bf16[2,160,512]{2,1,0:T(8,128)(2,1)S(1)}, bf16[2,160,512]{2,1,0:T(8,128)(2,1)}, u32[]{:S(2)}, u32[]{:S(2)}) %collective-permute-start.15) | collective-permute-done | bytes 327712 | tf_op jit(solution)/shard_map/ppermute | solution.py:39
  83.7 2.3 %fusion.154 = (f32[320]{0:T(512)S(1)}, f32[320,512]{1,0:T(8,128)S(1)}) fusion(f32[512]{0:T(512)S(1)} %bitcast.175, bf16[3,512,512]{2,1,0:T(8,128)(2,1)} %param.29, f32[320,512]{1,0:T(8,128)} %fusion.56, bf16[320,512]{1,0:T(8,128)(2,1)} %bitcast.153, f32[512]{0:T(512)S(1)} %bitcast.176), kind=kOutput, calls=%fused_computation.264 | convolution fusion | flops 337018560 | bytes 2692352 | tf_op jit(solution)/shard_map/dot_general | solution.py:25
  87.2 3.1 %fusion.44 = f32[1024,512]{1,0:T(8,128)} fusion(bf16[1024,512]{1,0:T(8,128)(2,1)S(1)} %copy-done.3, bf16[4,512,512]{2,1,0:T(8,128)(2,1)} %param.30), kind=kOutput, calls=%fused_computation.79 | convolution fusion | flops 536870912 | bytes 3670016 | tf_op jit(solution)/shard_map/dot_general | solution.py:25
  92.4 3.4 %collective-permute-done.17 = bf16[4,8,512]{2,1,0:T(8,128)(2,1)S(1)} collective-permute-done((bf16[4,8,512]{2,1,0:T(8,128)(2,1)S(1)}, bf16[4,8,512]{2,1,0:T(8,128)(2,1)S(1)}, u32[]{:S(2)}, u32[]{:S(2)}) %collective-permute-start.17) | collective-permute-done | bytes 32800 | tf_op jit(solution)/shard_map/ppermute | solution.py:39
  96.1 3.7 %collective-permute-done.18 = bf16[2,16,512]{2,1,0:T(8,128)(2,1)S(1)} collective-permute-done((bf16[2,16,512]{2,1,0:T(8,128)(2,1)S(1)}, bf16[2,16,512]{2,1,0:T(8,128)(2,1)S(1)}, u32[]{:S(2)}, u32[]{:S(2)}) %collective-permute-start.18) | collective-permute-done | bytes 32800 | tf_op jit(solution)/shard_map/ppermute | solution.py:39
  100.7 3.7 %fusion.1 = f32[1024,512]{1,0:T(8,128)} fusion(s32[1024]{0:T(1024)S(1)} %copy-done.17, bf16[4,512,512]{2,1,0:T(8,128)(2,1)} %param.30, bf16[320,512]{1,0:T(8,128)(2,1)S(1)} %collective-permute-done.16, bf16[320,512]{1,0:T(8,128)(2,1)S(1)} %add_convert_fusion.1), kind=kOutput, calls=%fused_computation.5 | convolution fusion | flops 1008926720 | bytes 3280896 | tf_op jit(solution)/shard_map/dot_general | solution.py:25
  104.8 5.1 %add_reduce_fusion = (f32[1024]{0:T(1024)S(1)}, f32[1024,512]{0,1:T(8,128)}) fusion(f32[512]{0:T(512)S(1)} %bitcast.164, bf16[4,512,512]{2,1,0:T(8,128)(2,1)} %param.30, f32[1024,512]{1,0:T(8,128)} %fusion.1, f32[1024,512]{1,0:T(8,128)} %fusion.44, bf16[64,512]{1,0:T(8,128)(2,1)S(1)} %bitcast.157, f32[512]{0:T(512)S(1)} %bitcast.174, s32[1024]{0:T(1024)S(1)} %copy-done.16), kind=kOutput, calls=%fused_computation.18 | convolution fusion | flops 609287168 | bytes 6893568 | tf_op jit(solution)/shard_map/dot_general | solution.py:25
  109.9 2.1 %multiply_reduce_fusion = f32[1024]{0:T(1024)S(1)} fusion(f32[1024,512]{0,1:T(8,128)} %get-tuple-element.52, f32[1024]{0:T(1024)S(1)} %broadcast_multiply_fusion, f32[512]{0:T(512)S(1)} %bitcast.165), kind=kLoop, calls=%fused_computation.7 | loop fusion | flops 2096128 | bytes 2107392 | tf_op jit(solution)/shard_map/reduce_sum | solution.py:14
  121.2 3.5 %collective-permute-done.21 = bf16[1,160,512]{2,1,0:T(8,128)(2,1)S(1)} collective-permute-done((bf16[1,160,512]{2,1,0:T(8,128)(2,1)S(1)}, bf16[1,160,512]{2,1,0:T(8,128)(2,1)S(1)}, u32[]{:S(2)}, u32[]{:S(2)}) %collective-permute-start.21) | collective-permute-done | bytes 163872 | tf_op jit(solution)/shard_map/ppermute | solution.py:39
  124.6 1.8 %fusion.157 = (f32[160]{0:T(256)S(1)}, f32[160,512]{1,0:T(8,128)S(1)}) fusion(f32[512]{0:T(512)S(1)} %bitcast.172, bf16[3,512,512]{2,1,0:T(8,128)(2,1)} %param.31, f32[160,512]{1,0:T(8,128)S(1)} %fusion.46, bf16[1,160,512]{2,1,0:T(8,128)(2,1)S(1)} %collective-permute-done.21, f32[2,160,512]{2,1,0:T(8,128)S(1)} %bitcast_add_fusion, s32[]{:T(128)S(6)} %select_n.215, ...), kind=kOutput, calls=%fused_computation.265 | convolution fusion | flops 168755040 | bytes 2200196 | tf_op jit(solution)/shard_map/dot_general | solution.py:25
  (172 shorter events, 51.0 us)
Async XLA Ops:
  6.8 22.9 %collective-permute-start = (bf16[64,512]{1,0:T(8,128)(2,1)}, bf16[64,512]{1,0:T(8,128)(2,1)}, u32[]{:S(2)}, u32[]{:S(2)}) collective-permute-start(bf16[64,512]{1,0:T(8,128)(2,1)} %get-tuple-element.20), channel_id=1, source_target_pairs={{0,4},{4,0},{8,12},{12,8},{16,20},{20,16},{24,28},{28,24},{1,5},{5... | collective-permute-start | bytes 196616 | tf_op jit(solution)/shard_map/ppermute | solution.py:39
  9.8 25.0 %collective-permute-start.1 = (bf16[64,512]{1,0:T(8,128)(2,1)S(1)}, bf16[64,512]{1,0:T(8,128)(2,1)}, u32[]{:S(2)}, u32[]{:S(2)}) collective-permute-start(bf16[64,512]{1,0:T(8,128)(2,1)S(1)} %get-tuple-element.19), channel_id=1, source_target_pairs={{0,8},{4,12},{8,0},{12,4},{16,24},{20,28},{24,16},{28,20},{1,9},{5... | collective-permute-start | bytes 196616 | tf_op jit(solution)/shard_map/ppermute | solution.py:39
  11.3 24.9 %collective-permute-start.2 = (bf16[64,512]{1,0:T(8,128)(2,1)S(1)}, bf16[64,512]{1,0:T(8,128)(2,1)}, u32[]{:S(2)}, u32[]{:S(2)}) collective-permute-start(bf16[64,512]{1,0:T(8,128)(2,1)S(1)} %get-tuple-element.18), channel_id=1, source_target_pairs={{0,12},{4,8},{8,4},{12,0},{16,28},{20,24},{24,20},{28,16},{1,13},{... | collective-permute-start | bytes 196616 | tf_op jit(solution)/shard_map/ppermute | solution.py:39
  11.4 26.4 %collective-permute-start.3 = (bf16[64,512]{1,0:T(8,128)(2,1)S(1)}, bf16[64,512]{1,0:T(8,128)(2,1)}, u32[]{:S(2)}, u32[]{:S(2)}) collective-permute-start(bf16[64,512]{1,0:T(8,128)(2,1)S(1)} %get-tuple-element.17), channel_id=1, source_target_pairs={{0,16},{4,20},{8,24},{12,28},{16,0},{20,4},{24,8},{28,12},{1,17},{... | collective-permute-start | bytes 196616 | tf_op jit(solution)/shard_map/ppermute | solution.py:39
  14.3 24.9 %collective-permute-start.4 = (bf16[64,512]{1,0:T(8,128)(2,1)S(1)}, bf16[64,512]{1,0:T(8,128)(2,1)}, u32[]{:S(2)}, u32[]{:S(2)}) collective-permute-start(bf16[64,512]{1,0:T(8,128)(2,1)S(1)} %get-tuple-element.16), channel_id=1, source_target_pairs={{0,20},{4,16},{8,28},{12,24},{16,4},{20,0},{24,12},{28,8},{1,21},{... | collective-permute-start | bytes 196616 | tf_op jit(solution)/shard_map/ppermute | solution.py:39
  29.7 11.0 %collective-permute-start.5 = (bf16[64,512]{1,0:T(8,128)(2,1)S(1)}, bf16[64,512]{1,0:T(8,128)(2,1)S(1)}, u32[]{:S(2)}, u32[]{:S(2)}) collective-permute-start(bf16[64,512]{1,0:T(8,128)(2,1)S(1)} %get-tuple-element.15), channel_id=1, source_target_pairs={{0,24},{4,28},{8,16},{12,20},{16,8},{20,12},{24,0},{28,4},{1,25},{... | collective-permute-start | bytes 196616 | tf_op jit(solution)/shard_map/ppermute | solution.py:39
  34.8 7.0 %collective-permute-start.6 = (bf16[64,512]{1,0:T(8,128)(2,1)S(1)}, bf16[64,512]{1,0:T(8,128)(2,1)S(1)}, u32[]{:S(2)}, u32[]{:S(2)}) collective-permute-start(bf16[64,512]{1,0:T(8,128)(2,1)S(1)} %get-tuple-element.14), channel_id=1, source_target_pairs={{0,28},{4,24},{8,20},{12,16},{16,12},{20,8},{24,4},{28,0},{1,29},{... | collective-permute-start | bytes 196616 | tf_op jit(solution)/shard_map/ppermute | solution.py:39
  49.4 19.2 %copy-start.24 = (s32[512]{0:T(512)S(1)}, s32[512]{0:T(512)}, u32[]{:S(2)}) copy-start(s32[512]{0:T(512)} %copy-done.23) | copy-start | bytes 6148
  50.3 18.9 %copy-start.7 = (bf16[640,512]{1,0:T(8,128)(2,1)S(1)}, bf16[640,512]{1,0:T(8,128)(2,1)}, u32[]{:S(2)}) copy-start(bf16[640,512]{1,0:T(8,128)(2,1)} %param.22) | copy-start | bytes 1966084
  50.4 7.6 %collective-permute-start.7 = (bf16[64,512]{1,0:T(8,128)(2,1)S(1)}, bf16[64,512]{1,0:T(8,128)(2,1)S(1)}, u32[]{:S(2)}, u32[]{:S(2)}) collective-permute-start(bf16[64,512]{1,0:T(8,128)(2,1)S(1)} %get-tuple-element.12), channel_id=1, source_target_pairs={{0,4},{4,0},{8,12},{12,8},{16,20},{20,16},{24,28},{28,24},{1,5},{5... | collective-permute-start | bytes 196616 | tf_op jit(solution)/shard_map/ppermute | solution.py:39
  52.1 9.5 %collective-permute-start.8 = (bf16[64,512]{1,0:T(8,128)(2,1)S(1)}, bf16[64,512]{1,0:T(8,128)(2,1)S(1)}, u32[]{:S(2)}, u32[]{:S(2)}) collective-permute-start(bf16[64,512]{1,0:T(8,128)(2,1)S(1)} %get-tuple-element.11), channel_id=1, source_target_pairs={{0,8},{4,12},{8,0},{12,4},{16,24},{20,28},{24,16},{28,20},{1,9},{5... | collective-permute-start | bytes 196616 | tf_op jit(solution)/shard_map/ppermute | solution.py:39
  52.1 9.9 %collective-permute-start.9 = (bf16[64,512]{1,0:T(8,128)(2,1)S(1)}, bf16[64,512]{1,0:T(8,128)(2,1)S(1)}, u32[]{:S(2)}, u32[]{:S(2)}) collective-permute-start(bf16[64,512]{1,0:T(8,128)(2,1)S(1)} %get-tuple-element.10), channel_id=1, source_target_pairs={{0,12},{4,8},{8,4},{12,0},{16,28},{20,24},{24,20},{28,16},{1,13},{... | collective-permute-start | bytes 196616 | tf_op jit(solution)/shard_map/ppermute | solution.py:39
  54.3 8.7 %collective-permute-start.10 = (bf16[64,512]{1,0:T(8,128)(2,1)S(1)}, bf16[64,512]{1,0:T(8,128)(2,1)S(1)}, u32[]{:S(2)}, u32[]{:S(2)}) collective-permute-start(bf16[64,512]{1,0:T(8,128)(2,1)S(1)} %get-tuple-element.9), channel_id=1, source_target_pairs={{0,16},{4,20},{8,24},{12,28},{16,0},{20,4},{24,8},{28,12},{1,17},{... | collective-permute-start | bytes 196616 | tf_op jit(solution)/shard_map/ppermute | solution.py:39
  56.3 9.6 %collective-permute-start.11 = (bf16[64,512]{1,0:T(8,128)(2,1)S(1)}, bf16[64,512]{1,0:T(8,128)(2,1)S(1)}, u32[]{:S(2)}, u32[]{:S(2)}) collective-permute-start(bf16[64,512]{1,0:T(8,128)(2,1)S(1)} %get-tuple-element.8), channel_id=1, source_target_pairs={{0,20},{4,16},{8,28},{12,24},{16,4},{20,0},{24,12},{28,8},{1,21},{... | collective-permute-start | bytes 196616 | tf_op jit(solution)/shard_map/ppermute | solution.py:39
  57.9 7.9 %collective-permute-start.12 = (bf16[64,512]{1,0:T(8,128)(2,1)S(1)}, bf16[64,512]{1,0:T(8,128)(2,1)S(1)}, u32[]{:S(2)}, u32[]{:S(2)}) collective-permute-start(bf16[64,512]{1,0:T(8,128)(2,1)S(1)} %get-tuple-element.7), channel_id=1, source_target_pairs={{0,24},{4,28},{8,16},{12,20},{16,8},{20,12},{24,0},{28,4},{1,25},{... | collective-permute-start | bytes 196616 | tf_op jit(solution)/shard_map/ppermute | solution.py:39
  61.6 7.0 %collective-permute-start.13 = (bf16[64,512]{1,0:T(8,128)(2,1)S(1)}, bf16[64,512]{1,0:T(8,128)(2,1)S(1)}, u32[]{:S(2)}, u32[]{:S(2)}) collective-permute-start(bf16[64,512]{1,0:T(8,128)(2,1)S(1)} %get-tuple-element.6), channel_id=1, source_target_pairs={{0,28},{4,24},{8,20},{12,16},{16,12},{20,8},{24,4},{28,0},{1,29},{... | collective-permute-start | bytes 196616 | tf_op jit(solution)/shard_map/ppermute | solution.py:39
  69.2 2.4 %collective-permute-start.14 = (bf16[2,160,512]{2,1,0:T(8,128)(2,1)S(1)}, bf16[2,160,512]{2,1,0:T(8,128)(2,1)S(1)}, u32[]{:S(2)}, u32[]{:S(2)}) collective-permute-start(bf16[2,160,512]{2,1,0:T(8,128)(2,1)S(1)} %fusion.82), channel_id=1, source_target_pairs={{0,1},{1,0},{2,3},{3,2},{4,5},{5,4},{6,7},{7,6},{8,9},{9,8},{10,11... | collective-permute-start | bytes 983048 | tf_op jit(solution)/shard_map/ppermute | solution.py:39
  71.7 10.3 %collective-permute-start.15 = (bf16[2,160,512]{2,1,0:T(8,128)(2,1)S(1)}, bf16[2,160,512]{2,1,0:T(8,128)(2,1)}, u32[]{:S(2)}, u32[]{:S(2)}) collective-permute-start(bf16[2,160,512]{2,1,0:T(8,128)(2,1)S(1)} %fusion.34), channel_id=1, source_target_pairs={{0,2},{1,3},{2,0},{3,1},{4,6},{5,7},{6,4},{7,5},{8,10},{9,11},{10,... | collective-permute-start | bytes 983048 | tf_op jit(solution)/shard_map/ppermute | solution.py:39
  86.4 3.9 %collective-permute-start.16 = (bf16[320,512]{1,0:T(8,128)(2,1)S(1)}, bf16[320,512]{1,0:T(8,128)(2,1)S(1)}, u32[]{:S(2)}, u32[]{:S(2)}) collective-permute-start(bf16[320,512]{1,0:T(8,128)(2,1)S(1)} %add_convert_fusion.1), channel_id=1, source_target_pairs={{0,1},{1,0},{2,3},{3,2},{4,5},{5,4},{6,7},{7,6},{8,9},{9,8},{10,11... | collective-permute-start | bytes 983048 | tf_op jit(solution)/shard_map/ppermute | solution.py:39
  91.8 4.0 %collective-permute-start.17 = (bf16[4,8,512]{2,1,0:T(8,128)(2,1)S(1)}, bf16[4,8,512]{2,1,0:T(8,128)(2,1)S(1)}, u32[]{:S(2)}, u32[]{:S(2)}) collective-permute-start(bf16[4,8,512]{2,1,0:T(8,128)(2,1)S(1)} %get-tuple-element.27), channel_id=1, source_target_pairs={{0,4},{4,0},{8,12},{12,8},{16,20},{20,16},{24,28},{28,24},{1,5},{5... | collective-permute-start | bytes 98312 | tf_op jit(solution)/shard_map/ppermute | solution.py:39
  95.8 4.0 %collective-permute-start.18 = (bf16[2,16,512]{2,1,0:T(8,128)(2,1)S(1)}, bf16[2,16,512]{2,1,0:T(8,128)(2,1)S(1)}, u32[]{:S(2)}, u32[]{:S(2)}) collective-permute-start(bf16[2,16,512]{2,1,0:T(8,128)(2,1)S(1)} %get-tuple-element.25), channel_id=1, source_target_pairs={{0,8},{4,12},{8,0},{12,4},{16,24},{20,28},{24,16},{28,20},{1,9},{5... | collective-permute-start | bytes 98312 | tf_op jit(solution)/shard_map/ppermute | solution.py:39
  99.8 4.9 %collective-permute-start.19 = (bf16[1,32,512]{2,1,0:T(8,128)(2,1)S(1)}, bf16[1,32,512]{2,1,0:T(8,128)(2,1)S(1)}, u32[]{:S(2)}, u32[]{:S(2)}) collective-permute-start(bf16[1,32,512]{2,1,0:T(8,128)(2,1)S(1)} %get-tuple-element.23), channel_id=1, source_target_pairs={{0,16},{4,20},{8,24},{12,28},{16,0},{20,4},{24,8},{28,12},{1,17},{... | collective-permute-start | bytes 98312 | tf_op jit(solution)/shard_map/ppermute | solution.py:39
  115.0 2.0 %collective-permute-start.20 = (bf16[2,160,512]{2,1,0:T(8,128)(2,1)}, bf16[2,160,512]{2,1,0:T(8,128)(2,1)}, u32[]{:S(2)}, u32[]{:S(2)}) collective-permute-start(bf16[2,160,512]{2,1,0:T(8,128)(2,1)} %fusion.83), channel_id=1, source_target_pairs={{0,1},{1,0},{2,3},{3,2},{4,5},{5,4},{6,7},{7,6},{8,9},{9,8},{10,11... | collective-permute-start | bytes 983048 | tf_op jit(solution)/shard_map/ppermute | solution.py:39
  118.3 6.3 %collective-permute-start.21 = (bf16[1,160,512]{2,1,0:T(8,128)(2,1)S(1)}, bf16[1,160,512]{2,1,0:T(8,128)(2,1)S(1)}, u32[]{:S(2)}, u32[]{:S(2)}) collective-permute-start(bf16[1,160,512]{2,1,0:T(8,128)(2,1)S(1)} %dynamic-slice_convert_fusion.2), channel_id=1, source_target_pairs={{0,2},{1,3},{2,0},{3,1},{4,6},{5,7},{6,4},{7,5},{8,10},{9,11},{10,... | collective-permute-start | bytes 491528 | tf_op jit(solution)/shard_map/ppermute | solution.py:39
  (29 other events, 167.1 us)

commit v2 on v1

v2 whole, which is shorter than its diff:
```python
import functools

import jax
import jax.numpy as jnp
from jax import lax
from jax.experimental import pallas as pl
from jax.experimental.pallas import tpu as pltpu
from jax.sharding import PartitionSpec as P


NEIGH = 8
BF16 = jnp.bfloat16
F32 = jnp.float32
TILE = 256


def project(node_rows, weight):
    return jnp.dot(node_rows, weight, preferred_element_type=F32)


def silu(values):
    half = values * 0.5
    return half + half * jnp.tanh(half)


def normed(second, gain_row):
    center = second - jnp.mean(second, axis=-1, keepdims=True)
    spread = jnp.mean(center * center, axis=-1, keepdims=True)
    return center * (lax.rsqrt(spread + 1e-05) * gain_row)


def tail(first, weight_ref, biases_ref, gains_ref, block):
    hidden = silu(first).astype(BF16)
    second = project(hidden, weight_ref[...]) + biases_ref[block, 1:2, :]
    return normed(second, gains_ref[block : block + 1, :])


def column(row):
    return jnp.broadcast_to(row, (128, row.shape[1])).T


def hot_columns(indices, names):
    wide = names.shape[1]
    if wide <= 128:
        return (indices[:, :wide] == names).astype(F32).astype(BF16)
    parts = [
        (indices == names[:, at : at + 128]).astype(F32).astype(BF16) for at in range(0, wide, 128)
    ]
    return jnp.concatenate(parts, axis=1)


def hot_rows(row, names):
    return (row == names).astype(F32).astype(BF16)


def lanes(count):
    return lax.broadcasted_iota(jnp.int32, (1, count), 1)


def sublanes(count):
    return lax.broadcasted_iota(jnp.int32, (count, 1), 0)


def share_names(iota, share_rows, band_count, core):
    half_count = band_count // 2
    names = iota
    for place in range(band_count):
        share = 2 * (place % half_count) + (core if place < half_count else 1 - core)
        offset = (share - place) * share_rows
        inside = (iota >= place * share_rows) & (iota < (place + 1) * share_rows)
        names = jnp.where(inside, iota + offset, names)
    return names


def call(kernel, outs, args, scratch=(), flops=0):
    single = not isinstance(outs, (list, tuple))
    return pl.pallas_call(
        kernel,
        out_shape=outs if single else tuple(outs),
        in_specs=[pl.BlockSpec(memory_space=pltpu.VMEM)] * len(args),
        out_specs=pl.BlockSpec(memory_space=pltpu.VMEM)
        if single
        else (pl.BlockSpec(memory_space=pltpu.VMEM),) * len(outs),
        scratch_shapes=list(scratch),
        cost_estimate=pl.CostEstimate(flops=flops, transcendentals=0, bytes_accessed=0),
    )(*args)


def shape(dims, kind):
    return jax.ShapeDtypeStruct(dims, kind)


def window_of(mask, exact, blk_count):
    if not exact:
        return mask
    blk = lax.axis_index("blk")
    return (blk - (blk ^ mask) + NEIGH // 2 + blk_count) % NEIGH


def keys_kernel(exact, blk_count, node_ref, mesh_ref, weight_ref, *refs):
    outs, held = refs[:NEIGH], refs[NEIGH]
    picks = hot_columns(column(node_ref[...]), lanes(mesh_ref.shape[0]))
    rows = project(picks, mesh_ref[...]).astype(BF16)
    keys = project(rows, weight_ref[...]).astype(BF16)
    held[...] = keys.reshape(held.shape)
    for mask in range(NEIGH):
        outs[mask][...] = held[window_of(mask, exact, blk_count)]


def local_kernel(
    sender_ref, grid_ref, edges_ref, w_edge, w_sender, w_grid, w_grid_last, biases_ref, gains_ref, part_ref, out_ref
):
    rows = grid_ref.shape[0]
    names = lanes(rows)
    senders = column(sender_ref[...])
    for at in range(0, edges_ref.shape[0], TILE):
        picks = hot_columns(senders[at : at + TILE], names)
        nodes = project(picks, grid_ref[...]).astype(BF16)
        part_ref[at : at + TILE, :] = (
            project(edges_ref[at : at + TILE, :], w_edge[...])
            + project(nodes, w_sender[...])
            + biases_ref[1, 0:1, :]
        )
    for at in range(0, rows, TILE):
        nodes = grid_ref[at : at + TILE, :]
        first = project(nodes, w_grid[...]) + biases_ref[0, 0:1, :]
        out_ref[at : at + TILE, :] = (
            nodes.astype(F32) + tail(first, w_grid_last, biases_ref, gains_ref, 0)
        ).astype(BF16)


def message_kernel(slot_ref, part_ref, weight_ref, biases_ref, gains_ref, *refs):
    keys, outs, table, sent = refs[:NEIGH], refs[NEIGH : 2 * NEIGH], refs[-2], refs[-1]
    cap = keys[0].shape[0]
    for window in range(NEIGH):
        table[window * cap : (window + 1) * cap, :] = keys[window][...]
    slots = column(slot_ref[...])
    names = lanes(table.shape[0])
    for at in range(0, part_ref.shape[0], TILE):
        picks = hot_columns(slots[at : at + TILE], names)
        first = part_ref[at : at + TILE, :] + project(picks, table[...])
        sent[at : at + TILE, :] = tail(first, weight_ref, biases_ref, gains_ref, 1).astype(BF16)
    sums = project(hot_rows(slot_ref[...], sublanes(table.shape[0])), sent[...]).astype(BF16)
    for window in range(NEIGH):
        outs[window][...] = sums[window * cap : (window + 1) * cap, :]


def land_kernel(exact, blk_count, band_count, node_ref, *refs):
    pieces, given_ref, kept_ref, held = refs[:NEIGH], refs[NEIGH], refs[NEIGH + 1], refs[NEIGH + 2]
    for mask in range(NEIGH):
        held[window_of(mask, exact, blk_count)] = pieces[mask][...]
    half = given_ref.shape[0]
    core = lax.axis_index("band") % 2
    names = share_names(sublanes(2 * half), 2 * half // band_count, band_count, 1 - core)
    landed = held[...].reshape(-1, held.shape[2])
    given_ref[...] = project(hot_rows(node_ref[...], names[:half]), landed).astype(BF16)
    kept_ref[...] = project(hot_rows(node_ref[...], names[half:]), landed)


def early_kernel(band_count, nodes_ref, edges_ref, w_node, w_edge, biases_ref, node_part_ref, edge_part_ref):
    core = lax.axis_index("band") % 2
    share = node_part_ref.shape[0] // (band_count // 2)
    for place in range(band_count // 2):
        rows = nodes_ref[2 * place + core]
        node_part_ref[place * share : (place + 1) * share, :] = (
            project(rows, w_node[...]) + biases_ref[2, 0:1, :]
        )
    for at in range(0, edges_ref.shape[0], TILE):
        edge_part_ref[at : at + TILE, :] = (
            project(edges_ref[at : at + TILE, :], w_edge[...]) + biases_ref[3, 0:1, :]
        )


def node_kernel(band_count, halves, *refs):
    sums, rest = refs[:halves], refs[halves:]
    nodes_ref, part_ref, w_sum, w_last, biases_ref, gains_ref, out_ref = rest
    core = lax.axis_index("band") % 2
    share = out_ref.shape[0] // (band_count // 2)
    total = sums[0][...].astype(F32)
    for other in sums[1:]:
        total = total + other[...].astype(F32)
    first = part_ref[...] + project(total.astype(BF16), w_sum[...])
    change = tail(first, w_last, biases_ref, gains_ref, 2)
    for place in range(band_count // 2):
        at = place * share
        out_ref[at : at + share, :] = (
            nodes_ref[2 * place + core].astype(F32) + change[at : at + share, :]
        ).astype(BF16)


def sender_kernel(band_count, send_ref, own_ref, other_ref, weight_ref, out_ref, table):
    half = own_ref.shape[0]
    table[:half, :] = own_ref[...]
    table[half:, :] = other_ref[...]
    core = lax.axis_index("band") % 2
    names = share_names(lanes(2 * half), 2 * half // band_count, band_count, core)
    rows = project(hot_columns(column(send_ref[...]), names), table[...]).astype(BF16)
    out_ref[...] = project(rows, weight_ref[...]).astype(BF16)


def target_kernel(band_count, receiver_ref, own_ref, other_ref, part_ref, weight_ref, out_ref, table):
    half = own_ref.shape[0]
    table[:half, :] = project(own_ref[...], weight_ref[...]).astype(BF16)
    table[half:, :] = project(other_ref[...], weight_ref[...]).astype(BF16)
    core = lax.axis_index("band") % 2
    names = share_names(lanes(2 * half), 2 * half // band_count, band_count, core)
    receivers = column(receiver_ref[...])
    for at in range(0, part_ref.shape[0], TILE):
        picks = hot_columns(receivers[at : at + TILE], names)
        out_ref[at : at + TILE, :] = part_ref[at : at + TILE, :] + project(picks, table[...])


def process_kernel(
    band_count, sender_ref, receiver_ref, part_ref, keys_ref, weight_ref, biases_ref, gains_ref, given_ref, kept_ref, sent
):
    senders = column(sender_ref[...])
    names = lanes(keys_ref.shape[0])
    for at in range(0, part_ref.shape[0], TILE):
        picks = hot_columns(senders[at : at + TILE], names)
        first = part_ref[at : at + TILE, :] + project(picks, keys_ref[...])
        sent[at : at + TILE, :] = tail(first, weight_ref, biases_ref, gains_ref, 3).astype(BF16)
    half = given_ref.shape[0]
    core = lax.axis_index("band") % 2
    places = share_names(sublanes(2 * half), 2 * half // band_count, band_count, 1 - core)
    given_ref[...] = project(hot_rows(receiver_ref[...], places[:half]), sent[...]).astype(BF16)
    kept_ref[...] = project(hot_rows(receiver_ref[...], places[half:]), sent[...])


def last_kernel(kept_ref, got_ref, own_ref, w_node, w_sum, w_last, biases_ref, gains_ref, out_ref):
    total = (kept_ref[...] + got_ref[...].astype(F32)).astype(BF16)
    first = (
        project(own_ref[...], w_node[...]) + project(total, w_sum[...]) + biases_ref[4, 0:1, :]
    )
    out_ref[...] = (
        own_ref[...].astype(F32) + tail(first, w_last, biases_ref, gains_ref, 4)
    ).astype(BF16)


def swap(rows, axis, mask):
    return lax.ppermute(rows, axis, [(i, i ^ mask) for i in range(lax.axis_size(axis))])


def window_exchange(blocks, back):
    blk_count = lax.axis_size("blk")
    pieces = []
    for window in range(NEIGH):
        if blk_count == NEIGH:
            pieces.append(swap(blocks[window], "blk", window) if window else blocks[0])
        else:
            distance = window - NEIGH // 2
            distance = distance if back else -distance
            route = [((i - distance) % blk_count, i) for i in range(blk_count)]
            pieces.append(lax.ppermute(blocks[window], "blk", route) if distance else blocks[window])
    return pieces


def body(
    grid_nodes,
    enc_edges,
    enc_sender,
    enc_slot,
    enc_slot_node,
    mesh_nodes,
    mesh_edges,
    mesh_sender,
    mesh_receiver,
    mesh_send_node,
    grid_weights,
    enc_edge_weights,
    enc_node_weights,
    proc_edge_weights,
    proc_node_weights,
    biases,
    gains,
):
    blk_count, band_count = lax.axis_size("blk"), lax.axis_size("band")
    blk_index, band_index = lax.axis_index("blk"), lax.axis_index("band")
    patch_rows, width = mesh_nodes.shape
    share_rows, half_rows = patch_rows // band_count, patch_rows // 2
    edge_rows, grid_rows, medge_rows = enc_edges.shape[0], grid_nodes.shape[0], mesh_edges.shape[0]
    slots = enc_slot_node.shape[1]
    cap = slots // NEIGH
    senders_all = mesh_send_node.shape[1]
    mcap = senders_all // blk_count
    exact = blk_count == NEIGH
    unit = 2 * width * width
    bf_piece = shape((cap, width), BF16)

    slot_place = enc_slot
    if exact:
        patch = (blk_index + lax.div(enc_slot, cap) + NEIGH // 2) % NEIGH
        slot_place = (patch ^ blk_index) * cap + lax.rem(enc_slot, cap)
    slot_place = slot_place.reshape(1, edge_rows)

    slot_keys = call(
        functools.partial(keys_kernel, exact, blk_count),
        [bf_piece] * NEIGH,
        (enc_slot_node, mesh_nodes, enc_edge_weights[2]),
        [pltpu.VMEM((NEIGH, cap, width), BF16)],
        unit * 2 * slots,
    )
    keys = window_exchange(slot_keys, False)

    edge_part, grid_out = call(
        local_kernel,
        [shape((edge_rows, width), F32), shape((grid_rows, width), BF16)],
        (
            enc_sender.reshape(1, edge_rows),
            grid_nodes,
            enc_edges,
            enc_edge_weights[0],
            enc_edge_weights[1],
            grid_weights[0],
            grid_weights[1],
            biases,
            gains,
        ),
        (),
        unit * (3 * edge_rows + 2 * grid_rows),
    )

    slot_sums = call(
        message_kernel,
        [bf_piece] * NEIGH,
        (slot_place, edge_part, enc_edge_weights[3], biases, gains, *keys),
        [pltpu.VMEM((slots, width), BF16), pltpu.VMEM((edge_rows, width), BF16)],
        unit * 3 * edge_rows,
    )
    landed = window_exchange(slot_sums, True)

    nodes_by_share = mesh_nodes.reshape(band_count, share_rows, width)
    node_part, mesh_part = call(
        functools.partial(early_kernel, band_count),
        [shape((half_rows, width), F32), shape((medge_rows, width), F32)],
        (nodes_by_share, mesh_edges, enc_node_weights[0], proc_edge_weights[0], biases),
        (),
        unit * (half_rows + medge_rows),
    )

    half_bf, half_f = shape((half_rows, width), BF16), shape((half_rows, width), F32)
    given, kept = call(
        functools.partial(land_kernel, exact, blk_count, band_count),
        [half_bf, half_f],
        (enc_slot_node, *landed),
        [pltpu.VMEM((NEIGH, cap, width), BF16)],
        unit * patch_rows,
    )
    half = (kept + swap(given, "band", 1).astype(F32)).astype(BF16)
    mask, halves = 2, (half,)
    while mask < band_count:
        if len(halves) == 2:
            half = (halves[0].astype(F32) + halves[1].astype(F32)).astype(BF16)
        halves = (half, swap(half, "band", mask))
        mask *= 2
    half_mid = call(
        functools.partial(node_kernel, band_count, len(halves)),
        half_bf,
        (*halves, nodes_by_share, node_part, enc_node_weights[1], enc_node_weights[2], biases, gains),
        (),
        unit * 2 * half_rows,
    )
    other_mid = swap(half_mid, "band", 1)

    send_nodes = jnp.take(
        mesh_send_node.reshape(blk_count, mcap), blk_index ^ jnp.arange(blk_count), axis=0, mode="clip"
    ).reshape(1, senders_all)
    senders = call(
        functools.partial(sender_kernel, band_count),
        shape((senders_all, width), BF16),
        (send_nodes, half_mid, other_mid, proc_edge_weights[1]),
        [pltpu.VMEM((patch_rows, width), BF16)],
        unit * 2 * senders_all,
    ).reshape(blk_count, mcap, width)
    mask = 1
    while mask < blk_count:
        view = senders.reshape(blk_count // (2 * mask), 2, mask * mcap, width)
        got = swap(view[:, 1], "blk", mask)
        senders = jnp.stack([view[:, 0], got], axis=1)
        mask *= 2
    arrived_senders = senders.reshape(senders_all, width)
    sender_place = (
        (lax.div(mesh_sender, mcap) ^ blk_index) * mcap + lax.rem(mesh_sender, mcap)
    ).reshape(1, medge_rows)
    receivers = mesh_receiver.reshape(1, medge_rows)

    mesh_part = call(
        functools.partial(target_kernel, band_count),
        shape((medge_rows, width), F32),
        (receivers, half_mid, other_mid, mesh_part, proc_edge_weights[2]),
        [pltpu.VMEM((patch_rows, width), BF16)],
        unit * (patch_rows + medge_rows),
    )
    given, kept = call(
        functools.partial(process_kernel, band_count),
        [half_bf, half_f],
        (sender_place, receivers, mesh_part, arrived_senders, proc_edge_weights[3], biases, gains),
        [pltpu.VMEM((medge_rows, width), BF16)],
        unit * 3 * medge_rows,
    )
    shares = kept + swap(given, "band", 1).astype(F32)
    shares = shares.reshape(band_count // 2, share_rows, width)
    got = jnp.zeros((1, share_rows, width), BF16)
    place, mask = band_index // 2, 2
    while mask < band_count:
        pairs = shares.reshape(-1, 2, share_rows, width)
        kept = lax.dynamic_index_in_dim(pairs, place % 2, 1, False)
        given = lax.dynamic_index_in_dim(pairs, 1 - place % 2, 1, False).astype(BF16)
        got = swap(given, "band", mask)
        place, mask = place // 2, mask * 2
        if mask < band_count:
            shares = kept + got.astype(F32)
    own_mid = lax.dynamic_index_in_dim(
        half_mid.reshape(band_count // 2, share_rows, width), band_index // 2, 0, False
    )
    mesh_out = call(
        last_kernel,
        shape((share_rows, width), BF16),
        (
            kept.reshape(share_rows, width),
            got.reshape(share_rows, width),
            own_mid,
            proc_node_weights[0],
            proc_node_weights[1],
            proc_node_weights[2],
            biases,
            gains,
        ),
        (),
        unit * 3 * share_rows,
    )
    return (grid_out, mesh_out)


def solution(mesh):
    rows = P(("blk", "band"), None)
    flat = P(("blk", "band"))
    in_specs = (rows, rows, flat, flat, rows, P("blk", None), rows, flat, flat, rows) + (P(),) * 7
    return jax.shard_map(
        body, mesh=mesh, in_specs=in_specs, out_specs=(rows, rows), check_vma=False
    )
```

time: 128 us -> 108 us (0.84)
  Pallas kernels: 0 us -> 38.8 us
  matrix products: 38.3 us -> 0 us
  other arithmetic: 16.4 us -> 2.72 us
  waiting for transfers between devices: 24.8 us -> 21 us
  local copies, waits for them, and re-layouts: 18.4 us -> 14.6 us
    pallas_call x0 -> x10, Pallas kernels: none -> 38.8 us  [call(): pl.pallas_call(kernel, out_shape=outs if single else tuple(outs), in_spec...]
    dot_general x16 -> x0, matrix products: 38.3 us -> none  [project(): return jnp.dot(node_rows, weight, preferred_element_type=F32)]
    unnamed x78 -> x56, local copies, waits for them, and re-layouts: 11.8 us -> 3.88 us
    squeeze x0 -> x5, local copies, waits for them, and re-layouts: none -> 7.94 us  [the longest x1 3.53 us: body(): enc_edge_weights[2]]
    reduce_sum x5 -> x0, other arithmetic: 4.78 us -> none  [layer_norm(): spread = jnp.mean(center * center, axis=-1, keepdims=True)]
    ppermute x22, waiting for transfers between devices: 24.8 us -> 21 us  [swap(): lax.ppermute(rows, axis, [(i, i ^ mask) for i in range(lax.axis_size(axis...]
    convert_element_type x4 -> x0, other arithmetic: 3.02 us -> none  [the longest x1 1.78 us: body(): (half.astype(F32) + swap(half, 'band', mask).astype(F32)).astype(BF16)]
    slice x4 -> x0, local copies, waits for them, and re-layouts: 2.87 us -> none  [the longest x1 1.51 us: body(): gains[4]]
  transfers between devices with their start and end apart: 22 -> 22, of which waited for: 10 -> 10; matrix products, arithmetic and copies ran while one was open for 29% -> 8% of each run, Pallas kernels for 0% -> 14%
where the time goes in v2:
time: 108 us
  Pallas kernels  38.8 us (36%)
  starting transfers between devices  29.5 us (27%)
  waiting for transfers between devices  21 us (19%)
  local copies, waits for them, and re-layouts  14.6 us (14%)
  other arithmetic  2.72 us (3%)
    pallas_call x10, Pallas kernels, call(): pl.pallas_call(kernel, out_shape=outs if single else tuple(outs), in_spec...  38.8 us
    ppermute x22, starting transfers between devices, swap(): lax.ppermute(rows, axis, [(i, i ^ mask) for i in range(lax.axis_size(axis...  29.5 us
    ppermute x22, waiting for transfers between devices, swap(): lax.ppermute(rows, axis, [(i, i ^ mask) for i in range(lax.axis_size(axis...  21 us
    unnamed x56, local copies, waits for them, and re-layouts  3.88 us
    squeeze x1, local copies, waits for them, and re-layouts, body(): enc_edge_weights[2]  3.53 us
  transfers between devices with their start and end apart: 22, of which 10 were waited for; matrix products, arithmetic and copies ran while one was open for 8% of the time, Pallas kernels for 14%

profile of v2, /device:TPU:0, one launch (start us, length us, event | category | flops | bytes accessed | tf_op | source)
XLA Modules:
  0.0 107.6 jit_solution(10975124054932442268)
XLA Ops:
  0.6 3.5 %slice_bitcast_fusion.10 = (bf16[512,512]{1,0:T(8,128)(2,1)}, bf16[512,512]{1,0:T(8,128)(2,1)}, bf16[512,512]{1,0:T(8,128)(2,1)}, bf16[512,512]{1,0:T(8,128)(2,1...) fusion(bf16[4,512,512]{2,1,0:T(8,128)(2,1)} %param.28, bf16[2,512,512]{2,1,0:T(8,128)(2,1)} %param.27), kind=kLoop, calls=%fused_computation.13 | loop fusion | bytes 6291456 | tf_op jit(solution)/shard_map/squeeze | solution.py:298
  4.2 2.9 %shard_map.182 = (bf16[64,512]{1,0:T(8,128)(2,1)}, bf16[64,512]{1,0:T(8,128)(2,1)}, bf16[64,512]{1,0:T(8,128)(2,1)}, bf16[64,512]{1,0:T(8,128)(2,1)}, bf16[64,51...) custom-call(s32[1,512]{1,0:T(1,128)} %node_ref.3, ...), custom_call_target="tpu_custom_call" | custom-call | flops 536870912 | tf_op jit(solution)/shard_map/pallas_call | solution.py:77
  7.1 3.0 %collective-permute-start = (bf16[64,512]{1,0:T(8,128)(2,1)}, bf16[64,512]{1,0:T(8,128)(2,1)S(1)}, u32[]{:S(2)}, u32[]{:S(2)}) collective-permute-start(bf16[64,512]{1,0:T(8,128)(2,1)} %get-tuple-element.29), channel_id=1, source_target_pairs={{0,4},{4,0},{8,12},{12,8},{16,20},{20,16},{24,28},{28,24},{1,5},{5... | collective-permute-start | bytes 196616 | tf_op jit(solution)/shard_map/ppermute | solution.py:240
  11.6 3.0 %collective-permute-start.3 = (bf16[64,512]{1,0:T(8,128)(2,1)}, bf16[64,512]{1,0:T(8,128)(2,1)S(1)}, u32[]{:S(2)}, u32[]{:S(2)}) collective-permute-start(bf16[64,512]{1,0:T(8,128)(2,1)} %get-tuple-element.32), channel_id=1, source_target_pairs={{0,16},{4,20},{8,24},{12,28},{16,0},{20,4},{24,8},{28,12},{1,17},{... | collective-permute-start | bytes 196616 | tf_op jit(solution)/shard_map/ppermute | solution.py:240
  16.5 3.6 %collective-permute-start.5 = (bf16[64,512]{1,0:T(8,128)(2,1)}, bf16[64,512]{1,0:T(8,128)(2,1)S(1)}, u32[]{:S(2)}, u32[]{:S(2)}) collective-permute-start(bf16[64,512]{1,0:T(8,128)(2,1)} %get-tuple-element.34), channel_id=1, source_target_pairs={{0,24},{4,28},{8,16},{12,20},{16,8},{20,12},{24,0},{28,4},{1,25},{... | collective-permute-start | bytes 196616 | tf_op jit(solution)/shard_map/ppermute | solution.py:240
  20.2 6.1 %shard_map.181 = (f32[1024,512]{1,0:T(8,128)}, bf16[512,512]{1,0:T(8,128)(2,1)}) custom-call(s32[1,1024]{1,0:T(1,128)} %bitcast.82, bf16[512,512]{1,0:T(8,128)(2,1)} %grid_ref.1, bf16[1024,512]{1,0:T(8,128)(2,1)} %edges_ref.2, bf16[512,512]{1,0:T(8,128)(2,1)} %get-tuple-element.56.w_edge, bf16[512,512]{1,0:T(8,128)(2,1)} %get-tuple-element.55.w_sender, ...), custom_call_target="tpu_custom_call" | custom-call | flops 2147483648 | tf_op jit(solution)/shard_map/pallas_call | solution.py:77
  28.0 5.0 %shard_map.183 = (bf16[64,512]{1,0:T(8,128)(2,1)}, bf16[64,512]{1,0:T(8,128)(2,1)}, bf16[64,512]{1,0:T(8,128)(2,1)}, bf16[64,512]{1,0:T(8,128)(2,1)}, bf16[64,51...) custom-call(s32[1,1024]{1,0:T(1,128)} %bitcast.80, ...), custom_call_target="tpu_custom_call" | custom-call | flops 1610612736 | tf_op jit(solution)/shard_map/pallas_call | solution.py:77
  33.1 2.2 %collective-permute-start.10 = (bf16[64,512]{1,0:T(8,128)(2,1)}, bf16[64,512]{1,0:T(8,128)(2,1)S(1)}, u32[]{:S(2)}, u32[]{:S(2)}) collective-permute-start(bf16[64,512]{1,0:T(8,128)(2,1)} %get-tuple-element.40), channel_id=1, source_target_pairs={{0,16},{4,20},{8,24},{12,28},{16,0},{20,4},{24,8},{28,12},{1,17},{... | collective-permute-start | bytes 196616 | tf_op jit(solution)/shard_map/ppermute | solution.py:240
  36.0 3.6 %collective-permute-start.12 = (bf16[64,512]{1,0:T(8,128)(2,1)}, bf16[64,512]{1,0:T(8,128)(2,1)S(1)}, u32[]{:S(2)}, u32[]{:S(2)}) collective-permute-start(bf16[64,512]{1,0:T(8,128)(2,1)} %get-tuple-element.42), channel_id=1, source_target_pairs={{0,24},{4,28},{8,16},{12,20},{16,8},{20,12},{24,0},{28,4},{1,25},{... | collective-permute-start | bytes 196616 | tf_op jit(solution)/shard_map/ppermute | solution.py:240
  42.4 2.3 %collective-permute-done.11.refs_5_ = bf16[64,512]{1,0:T(8,128)(2,1)S(1)} collective-permute-done((bf16[64,512]{1,0:T(8,128)(2,1)}, bf16[64,512]{1,0:T(8,128)(2,1)S(1)}, u32[]{:S(2)}, u32[]{:S(2)}) %collective-permute-start.11) | collective-permute-done | bytes 65568 | tf_op jit(solution)/shard_map/ppermute | solution.py:240
  46.9 3.1 %collective-permute-done.9.refs_3_ = bf16[64,512]{1,0:T(8,128)(2,1)S(1)} collective-permute-done((bf16[64,512]{1,0:T(8,128)(2,1)}, bf16[64,512]{1,0:T(8,128)(2,1)S(1)}, u32[]{:S(2)}, u32[]{:S(2)}) %collective-permute-start.9) | collective-permute-done | bytes 65568 | tf_op jit(solution)/shard_map/ppermute | solution.py:240
  50.7 2.5 %shard_map.184 = (bf16[320,512]{1,0:T(8,128)(2,1)}, f32[320,512]{1,0:T(8,128)}) custom-call(s32[1,512]{1,0:T(1,128)} %node_ref.3, bf16[64,512]{1,0:T(8,128)(2,1)} %get-tuple-element.36.refs_0_, bf16[64,512]{1,0:T(8,128)(2,1)} %copy-done.23, bf16[64,512]{1,0:T(8,128)(2,1)} %copy-done.24, bf16[64,512]{1,0:T(8,128)(2,1)} %copy-done.25, ...), custom_call_target="tpu_custom_call" | custom-call | flops 335544320 | tf_op jit(solution)/shard_map/pallas_call | solution.py:77
  55.1 1.7 %collective-permute-start.15 = (bf16[320,512]{1,0:T(8,128)(2,1)S(1)}, bf16[320,512]{1,0:T(8,128)(2,1)S(1)}, u32[]{:S(2)}, u32[]{:S(2)}) collective-permute-start(bf16[320,512]{1,0:T(8,128)(2,1)S(1)} %add_convert_fusion.refs_0_), channel_id=1, source_target_pairs={{0,2},{1,3},{2,0},{3,1},{4,6},{5,7},{6,4},{7,5},{8,10},{9,11},{10,... | collective-permute-start | bytes 983048 | tf_op jit(solution)/shard_map/ppermute | solution.py:240
  58.0 4.0 %shard_map.185 = (f32[320,512]{1,0:T(8,128)}, f32[1024,512]{1,0:T(8,128)}) custom-call(bf16[4,160,512]{2,1,0:T(8,128)(2,1)} %bitcast.66, bf16[1024,512]{1,0:T(8,128)(2,1)} %edges_ref.3, bf16[512,512]{1,0:T(8,128)(2,1)} %get-tuple-element.62.w_node, bf16[512,512]{1,0:T(8,128)(2,1)} %get-tuple-element.52.w_edge, f32[5,2,512]{2,1,0:T(2,128)} %biases_ref.9), custom_call_target="tpu_custom_call" | custom-call | flops 704643072 | tf_op jit(solution)/shard_map/pallas_call | solution.py:77
  62.0 3.0 %collective-permute-done.15.refs_1_ = bf16[320,512]{1,0:T(8,128)(2,1)S(1)} collective-permute-done((bf16[320,512]{1,0:T(8,128)(2,1)S(1)}, bf16[320,512]{1,0:T(8,128)(2,1)S(1)}, u32[]{:S(2)}, u32[]{:S(2)}) %collective-permute-start.15) | collective-permute-done | bytes 327712 | tf_op jit(solution)/shard_map/ppermute | solution.py:240
  65.7 3.4 %shard_map.186.own_ref = bf16[320,512]{1,0:T(8,128)(2,1)} custom-call(bf16[320,512]{1,0:T(8,128)(2,1)} %copy-done.5, bf16[320,512]{1,0:T(8,128)(2,1)} %copy-done.8, bf16[4,160,512]{2,1,0:T(8,128)(2,1)} %bitcast.67, f32[320,512]{1,0:T(8,128)} %get-tuple-element.46.refs_3_, bf16[512,512]{1,0:T(8,128)(2,1)} %get-tuple-element.63.refs_4_, ...), custom_call_target="tpu_custom_call" | custom-call | flops 335544320 | tf_op jit(solution)/shard_map/pallas_call | solution.py:77
  72.2 2.3 %shard_map.188 = bf16[64,512]{1,0:T(8,128)(2,1)} custom-call(s32[1,64]{1,0:T(1,128)} %reshape.70.send_ref, bf16[320,512]{1,0:T(8,128)(2,1)} %shard_map.186.own_ref, bf16[320,512]{1,0:T(8,128)(2,1)} %copy-done.4, bf16[512,512]{1,0:T(8,128)(2,1)} %get-tuple-element.53.weight_ref), custom_call_target="tpu_custom_call" | custom-call | flops 67108864 | tf_op jit(solution)/shard_map/pallas_call | solution.py:77
  76.5 2.8 %collective-permute-done.17 = bf16[4,8,512]{2,1,0:T(8,128)(2,1)S(1)} collective-permute-done((bf16[4,8,512]{2,1,0:T(8,128)(2,1)S(1)}, bf16[4,8,512]{2,1,0:T(8,128)(2,1)S(1)}, u32[]{:S(2)}, u32[]{:S(2)}) %collective-permute-start.17) | collective-permute-done | bytes 32800 | tf_op jit(solution)/shard_map/ppermute | solution.py:240
  80.4 2.8 %collective-permute-done.18 = bf16[2,16,512]{2,1,0:T(8,128)(2,1)S(1)} collective-permute-done((bf16[2,16,512]{2,1,0:T(8,128)(2,1)S(1)}, bf16[2,16,512]{2,1,0:T(8,128)(2,1)S(1)}, u32[]{:S(2)}, u32[]{:S(2)}) %collective-permute-start.18) | collective-permute-done | bytes 32800 | tf_op jit(solution)/shard_map/ppermute | solution.py:240
  83.3 2.0 %collective-permute-start.19 = (bf16[1,32,512]{2,1,0:T(8,128)(2,1)S(1)}, bf16[1,32,512]{2,1,0:T(8,128)(2,1)S(1)}, u32[]{:S(2)}, u32[]{:S(2)}) collective-permute-start(bf16[1,32,512]{2,1,0:T(8,128)(2,1)S(1)} %get-tuple-element.67), channel_id=1, source_target_pairs={{0,16},{4,20},{8,24},{12,28},{16,0},{20,4},{24,8},{28,12},{1,17},{... | collective-permute-start | bytes 98312 | tf_op jit(solution)/shard_map/ppermute | solution.py:240
  85.3 4.6 %shard_map.187.part_ref = f32[1024,512]{1,0:T(8,128)} custom-call(s32[1,1024]{1,0:T(1,128)} %bitcast.78, bf16[320,512]{1,0:T(8,128)(2,1)} %shard_map.186.own_ref, bf16[320,512]{1,0:T(8,128)(2,1)} %copy-done.4, f32[1024,512]{1,0:T(8,128)} %get-tuple-element.47.part_ref, bf16[512,512]{1,0:T(8,128)(2,1)} %get-tuple-element.51.weight_ref), custom_call_target="tpu_custom_call" | custom-call | flops 872415232 | tf_op jit(solution)/shard_map/pallas_call | solution.py:77
  90.5 5.1 %shard_map.189 = (bf16[320,512]{1,0:T(8,128)(2,1)}, f32[320,512]{1,0:T(8,128)}) custom-call(s32[1,1024]{1,0:T(1,128)} %bitcast.81, s32[1,1024]{1,0:T(1,128)} %bitcast.79, f32[1024,512]{1,0:T(8,128)} %shard_map.187.part_ref, bf16[64,512]{1,0:T(8,128)(2,1)} %bitcast.74, bf16[512,512]{1,0:T(8,128)(2,1)} %get-tuple-element.50.weight_ref, ...), custom_call_target="tpu_custom_call" | custom-call | flops 1610612736 | tf_op jit(solution)/shard_map/pallas_call | solution.py:77
  100.6 3.3 %collective-permute-done.21 = bf16[1,160,512]{2,1,0:T(8,128)(2,1)S(1)} collective-permute-done((bf16[1,160,512]{2,1,0:T(8,128)(2,1)S(1)}, bf16[1,160,512]{2,1,0:T(8,128)(2,1)S(1)}, u32[]{:S(2)}, u32[]{:S(2)}) %collective-permute-start.21) | collective-permute-done | bytes 163872 | tf_op jit(solution)/shard_map/ppermute | solution.py:240
  104.6 3.0 %shard_map.190 = bf16[160,512]{1,0:T(8,128)(2,1)} custom-call(f32[160,512]{1,0:T(8,128)} %dynamic-slice_bitcast_fusion.kept_ref, bf16[160,512]{1,0:T(8,128)(2,1)} %bitcast.73, bf16[160,512]{1,0:T(8,128)(2,1)} %dynamic-slice_bitcast_fusion.1.own_ref, bf16[512,512]{1,0:T(8,128)(2,1)} %get-tuple-element.59.w_node, bf16[512,512]{1,0:T(8,128)(2,1)} %get-tuple-element.60.w_sum, ...), custom_call_target="tpu_custom_call" | custom-call | flops 251658240 | tf_op jit(solution)/shard_map/pallas_call | solution.py:77
  (109 shorter events, 28.0 us)
Async XLA Ops:
  0.6 15.3 %copy-start.10 = (s32[1024]{0:T(1024)S(1)}, s32[1024]{0:T(1024)}, u32[]{:S(2)}) copy-start(s32[1024]{0:T(1024)} %param.20) | copy-start | bytes 12292
  7.1 9.5 %collective-permute-start = (bf16[64,512]{1,0:T(8,128)(2,1)}, bf16[64,512]{1,0:T(8,128)(2,1)S(1)}, u32[]{:S(2)}, u32[]{:S(2)}) collective-permute-start(bf16[64,512]{1,0:T(8,128)(2,1)} %get-tuple-element.29), channel_id=1, source_target_pairs={{0,4},{4,0},{8,12},{12,8},{16,20},{20,16},{24,28},{28,24},{1,5},{5... | collective-permute-start | bytes 196616 | tf_op jit(solution)/shard_map/ppermute | solution.py:240
  10.1 10.1 %collective-permute-start.1 = (bf16[64,512]{1,0:T(8,128)(2,1)}, bf16[64,512]{1,0:T(8,128)(2,1)S(1)}, u32[]{:S(2)}, u32[]{:S(2)}) collective-permute-start(bf16[64,512]{1,0:T(8,128)(2,1)} %get-tuple-element.30), channel_id=1, source_target_pairs={{0,8},{4,12},{8,0},{12,4},{16,24},{20,28},{24,16},{28,20},{1,9},{5... | collective-permute-start | bytes 196616 | tf_op jit(solution)/shard_map/ppermute | solution.py:240
  11.6 14.6 %collective-permute-start.2 = (bf16[64,512]{1,0:T(8,128)(2,1)}, bf16[64,512]{1,0:T(8,128)(2,1)S(1)}, u32[]{:S(2)}, u32[]{:S(2)}) collective-permute-start(bf16[64,512]{1,0:T(8,128)(2,1)} %get-tuple-element.31), channel_id=1, source_target_pairs={{0,12},{4,8},{8,4},{12,0},{16,28},{20,24},{24,20},{28,16},{1,13},{... | collective-permute-start | bytes 196616 | tf_op jit(solution)/shard_map/ppermute | solution.py:240
  11.6 14.6 %collective-permute-start.3 = (bf16[64,512]{1,0:T(8,128)(2,1)}, bf16[64,512]{1,0:T(8,128)(2,1)S(1)}, u32[]{:S(2)}, u32[]{:S(2)}) collective-permute-start(bf16[64,512]{1,0:T(8,128)(2,1)} %get-tuple-element.32), channel_id=1, source_target_pairs={{0,16},{4,20},{8,24},{12,28},{16,0},{20,4},{24,8},{28,12},{1,17},{... | collective-permute-start | bytes 196616 | tf_op jit(solution)/shard_map/ppermute | solution.py:240
  14.6 11.7 %collective-permute-start.4 = (bf16[64,512]{1,0:T(8,128)(2,1)}, bf16[64,512]{1,0:T(8,128)(2,1)S(1)}, u32[]{:S(2)}, u32[]{:S(2)}) collective-permute-start(bf16[64,512]{1,0:T(8,128)(2,1)} %get-tuple-element.33), channel_id=1, source_target_pairs={{0,20},{4,16},{8,28},{12,24},{16,4},{20,0},{24,12},{28,8},{1,21},{... | collective-permute-start | bytes 196616 | tf_op jit(solution)/shard_map/ppermute | solution.py:240
  16.5 9.8 %collective-permute-start.5 = (bf16[64,512]{1,0:T(8,128)(2,1)}, bf16[64,512]{1,0:T(8,128)(2,1)S(1)}, u32[]{:S(2)}, u32[]{:S(2)}) collective-permute-start(bf16[64,512]{1,0:T(8,128)(2,1)} %get-tuple-element.34), channel_id=1, source_target_pairs={{0,24},{4,28},{8,16},{12,20},{16,8},{20,12},{24,0},{28,4},{1,25},{... | collective-permute-start | bytes 196616 | tf_op jit(solution)/shard_map/ppermute | solution.py:240
  20.1 7.3 %collective-permute-start.6 = (bf16[64,512]{1,0:T(8,128)(2,1)}, bf16[64,512]{1,0:T(8,128)(2,1)S(1)}, u32[]{:S(2)}, u32[]{:S(2)}) collective-permute-start(bf16[64,512]{1,0:T(8,128)(2,1)} %get-tuple-element.35), channel_id=1, source_target_pairs={{0,28},{4,24},{8,20},{12,16},{16,12},{20,8},{24,4},{28,0},{1,29},{... | collective-permute-start | bytes 196616 | tf_op jit(solution)/shard_map/ppermute | solution.py:240
  28.0 25.1 %copy-start.1 = (bf16[4,512,512]{2,1,0:T(8,128)(2,1)S(1)}, bf16[4,512,512]{2,1,0:T(8,128)(2,1)}, u32[]{:S(2)}) copy-start(bf16[4,512,512]{2,1,0:T(8,128)(2,1)} %param.30) | copy-start | bytes 6291460
  33.1 8.3 %collective-permute-start.10 = (bf16[64,512]{1,0:T(8,128)(2,1)}, bf16[64,512]{1,0:T(8,128)(2,1)S(1)}, u32[]{:S(2)}, u32[]{:S(2)}) collective-permute-start(bf16[64,512]{1,0:T(8,128)(2,1)} %get-tuple-element.40), channel_id=1, source_target_pairs={{0,16},{4,20},{8,24},{12,28},{16,0},{20,4},{24,8},{28,12},{1,17},{... | collective-permute-start | bytes 196616 | tf_op jit(solution)/shard_map/ppermute | solution.py:240
  35.2 9.5 %collective-permute-start.11 = (bf16[64,512]{1,0:T(8,128)(2,1)}, bf16[64,512]{1,0:T(8,128)(2,1)S(1)}, u32[]{:S(2)}, u32[]{:S(2)}) collective-permute-start(bf16[64,512]{1,0:T(8,128)(2,1)} %get-tuple-element.41), channel_id=1, source_target_pairs={{0,20},{4,16},{8,28},{12,24},{16,4},{20,0},{24,12},{28,8},{1,21},{... | collective-permute-start | bytes 196616 | tf_op jit(solution)/shard_map/ppermute | solution.py:240
  36.0 9.4 %collective-permute-start.12 = (bf16[64,512]{1,0:T(8,128)(2,1)}, bf16[64,512]{1,0:T(8,128)(2,1)S(1)}, u32[]{:S(2)}, u32[]{:S(2)}) collective-permute-start(bf16[64,512]{1,0:T(8,128)(2,1)} %get-tuple-element.42), channel_id=1, source_target_pairs={{0,24},{4,28},{8,16},{12,20},{16,8},{20,12},{24,0},{28,4},{1,25},{... | collective-permute-start | bytes 196616 | tf_op jit(solution)/shard_map/ppermute | solution.py:240
  39.6 7.3 %collective-permute-start.13 = (bf16[64,512]{1,0:T(8,128)(2,1)}, bf16[64,512]{1,0:T(8,128)(2,1)S(1)}, u32[]{:S(2)}, u32[]{:S(2)}) collective-permute-start(bf16[64,512]{1,0:T(8,128)(2,1)} %get-tuple-element.43), channel_id=1, source_target_pairs={{0,28},{4,24},{8,20},{12,16},{16,12},{20,8},{24,4},{28,0},{1,29},{... | collective-permute-start | bytes 196616 | tf_op jit(solution)/shard_map/ppermute | solution.py:240
  40.7 6.2 %collective-permute-start.7 = (bf16[64,512]{1,0:T(8,128)(2,1)}, bf16[64,512]{1,0:T(8,128)(2,1)S(1)}, u32[]{:S(2)}, u32[]{:S(2)}) collective-permute-start(bf16[64,512]{1,0:T(8,128)(2,1)} %get-tuple-element.37), channel_id=1, source_target_pairs={{0,4},{4,0},{8,12},{12,8},{16,20},{20,16},{24,28},{28,24},{1,5},{5... | collective-permute-start | bytes 196616 | tf_op jit(solution)/shard_map/ppermute | solution.py:240
  41.3 5.6 %collective-permute-start.8 = (bf16[64,512]{1,0:T(8,128)(2,1)}, bf16[64,512]{1,0:T(8,128)(2,1)S(1)}, u32[]{:S(2)}, u32[]{:S(2)}) collective-permute-start(bf16[64,512]{1,0:T(8,128)(2,1)} %get-tuple-element.38), channel_id=1, source_target_pairs={{0,8},{4,12},{8,0},{12,4},{16,24},{20,28},{24,16},{28,20},{1,9},{5... | collective-permute-start | bytes 196616 | tf_op jit(solution)/shard_map/ppermute | solution.py:240
  44.7 5.4 %collective-permute-start.9 = (bf16[64,512]{1,0:T(8,128)(2,1)}, bf16[64,512]{1,0:T(8,128)(2,1)S(1)}, u32[]{:S(2)}, u32[]{:S(2)}) collective-permute-start(bf16[64,512]{1,0:T(8,128)(2,1)} %get-tuple-element.39), channel_id=1, source_target_pairs={{0,12},{4,8},{8,4},{12,0},{16,28},{20,24},{24,20},{28,16},{1,13},{... | collective-permute-start | bytes 196616 | tf_op jit(solution)/shard_map/ppermute | solution.py:240
  53.2 1.8 %collective-permute-start.14 = (bf16[320,512]{1,0:T(8,128)(2,1)}, bf16[320,512]{1,0:T(8,128)(2,1)S(1)}, u32[]{:S(2)}, u32[]{:S(2)}) collective-permute-start(bf16[320,512]{1,0:T(8,128)(2,1)} %get-tuple-element.45), channel_id=1, source_target_pairs={{0,1},{1,0},{2,3},{3,2},{4,5},{5,4},{6,7},{7,6},{8,9},{9,8},{10,11... | collective-permute-start | bytes 983048 | tf_op jit(solution)/shard_map/ppermute | solution.py:240
  55.1 9.8 %collective-permute-start.15 = (bf16[320,512]{1,0:T(8,128)(2,1)S(1)}, bf16[320,512]{1,0:T(8,128)(2,1)S(1)}, u32[]{:S(2)}, u32[]{:S(2)}) collective-permute-start(bf16[320,512]{1,0:T(8,128)(2,1)S(1)} %add_convert_fusion.refs_0_), channel_id=1, source_target_pairs={{0,2},{1,3},{2,0},{3,1},{4,6},{5,7},{6,4},{7,5},{8,10},{9,11},{10,... | collective-permute-start | bytes 983048 | tf_op jit(solution)/shard_map/ppermute | solution.py:240
  69.0 2.4 %collective-permute-start.16 = (bf16[320,512]{1,0:T(8,128)(2,1)}, bf16[320,512]{1,0:T(8,128)(2,1)S(1)}, u32[]{:S(2)}, u32[]{:S(2)}) collective-permute-start(bf16[320,512]{1,0:T(8,128)(2,1)} %shard_map.186.own_ref), channel_id=1, source_target_pairs={{0,1},{1,0},{2,3},{3,2},{4,5},{5,4},{6,7},{7,6},{8,9},{9,8},{10,11... | collective-permute-start | bytes 983048 | tf_op jit(solution)/shard_map/ppermute | solution.py:240
  75.3 3.9 %collective-permute-start.17 = (bf16[4,8,512]{2,1,0:T(8,128)(2,1)S(1)}, bf16[4,8,512]{2,1,0:T(8,128)(2,1)S(1)}, u32[]{:S(2)}, u32[]{:S(2)}) collective-permute-start(bf16[4,8,512]{2,1,0:T(8,128)(2,1)S(1)} %get-tuple-element.71), channel_id=1, source_target_pairs={{0,4},{4,0},{8,12},{12,8},{16,20},{20,16},{24,28},{28,24},{1,5},{5... | collective-permute-start | bytes 98312 | tf_op jit(solution)/shard_map/ppermute | solution.py:240
  79.2 4.0 %collective-permute-start.18 = (bf16[2,16,512]{2,1,0:T(8,128)(2,1)S(1)}, bf16[2,16,512]{2,1,0:T(8,128)(2,1)S(1)}, u32[]{:S(2)}, u32[]{:S(2)}) collective-permute-start(bf16[2,16,512]{2,1,0:T(8,128)(2,1)S(1)} %get-tuple-element.69), channel_id=1, source_target_pairs={{0,8},{4,12},{8,0},{12,4},{16,24},{20,28},{24,16},{28,20},{1,9},{5... | collective-permute-start | bytes 98312 | tf_op jit(solution)/shard_map/ppermute | solution.py:240
  83.3 6.6 %collective-permute-start.19 = (bf16[1,32,512]{2,1,0:T(8,128)(2,1)S(1)}, bf16[1,32,512]{2,1,0:T(8,128)(2,1)S(1)}, u32[]{:S(2)}, u32[]{:S(2)}) collective-permute-start(bf16[1,32,512]{2,1,0:T(8,128)(2,1)S(1)} %get-tuple-element.67), channel_id=1, source_target_pairs={{0,16},{4,20},{8,24},{12,28},{16,0},{20,4},{24,8},{28,12},{1,17},{... | collective-permute-start | bytes 98312 | tf_op jit(solution)/shard_map/ppermute | solution.py:240
  95.7 1.8 %collective-permute-start.20 = (bf16[320,512]{1,0:T(8,128)(2,1)}, bf16[320,512]{1,0:T(8,128)(2,1)S(1)}, u32[]{:S(2)}, u32[]{:S(2)}) collective-permute-start(bf16[320,512]{1,0:T(8,128)(2,1)} %get-tuple-element.49), channel_id=1, source_target_pairs={{0,1},{1,0},{2,3},{3,2},{4,5},{5,4},{6,7},{7,6},{8,9},{9,8},{10,11... | collective-permute-start | bytes 983048 | tf_op jit(solution)/shard_map/ppermute | solution.py:240
  97.6 6.3 %collective-permute-start.21 = (bf16[1,160,512]{2,1,0:T(8,128)(2,1)S(1)}, bf16[1,160,512]{2,1,0:T(8,128)(2,1)S(1)}, u32[]{:S(2)}, u32[]{:S(2)}) collective-permute-start(bf16[1,160,512]{2,1,0:T(8,128)(2,1)S(1)} %fusion), channel_id=1, source_target_pairs={{0,2},{1,3},{2,0},{3,1},{4,6},{5,7},{6,4},{7,5},{8,10},{9,11},{10,... | collective-permute-start | bytes 491528 | tf_op jit(solution)/shard_map/ppermute | solution.py:240
  (25 other events, 96.6 us)

commit v3 on v2

v3 whole, which is shorter than its diff:
```python
import functools

import jax
import jax.numpy as jnp
from jax import lax
from jax.experimental import pallas as pl
from jax.experimental.pallas import tpu as pltpu
from jax.sharding import PartitionSpec as P


NEIGH = 8
BF16 = jnp.bfloat16
F32 = jnp.float32
TILE = 256
GRANT = 16 << 20


def project(node_rows, weight):
    return jnp.dot(node_rows, weight, preferred_element_type=F32)


def silu(values):
    half = values * 0.5
    return half + half * jnp.tanh(half)


def normed(second, gain_row):
    center = second - jnp.mean(second, axis=-1, keepdims=True)
    spread = jnp.mean(center * center, axis=-1, keepdims=True)
    return center * (lax.rsqrt(spread + 1e-05) * gain_row)


def tail(first, weight, biases_ref, gains_ref, block):
    hidden = silu(first).astype(BF16)
    second = project(hidden, weight) + biases_ref[block, 1:2, :]
    return normed(second, gains_ref[block : block + 1, :])


def column(row):
    return jnp.broadcast_to(row, (128, row.shape[1])).T


def hot_columns(indices, names):
    wide = names.shape[1]
    if wide <= 128:
        return (indices[:, :wide] == names).astype(F32).astype(BF16)
    parts = [
        (indices == names[:, at : at + 128]).astype(F32).astype(BF16) for at in range(0, wide, 128)
    ]
    return jnp.concatenate(parts, axis=1)


def hot_rows(row, names):
    return (row == names).astype(F32).astype(BF16)


def lanes(count):
    return lax.broadcasted_iota(jnp.int32, (1, count), 1)


def sublanes(count):
    return lax.broadcasted_iota(jnp.int32, (count, 1), 0)


def share_names(iota, share_rows, band_count, core):
    half_count = band_count // 2
    x = lax.div(lax.axis_index("band"), 2)
    names = iota
    for place in range(band_count):
        share = 2 * ((place % half_count) ^ x) + (core if place < half_count else 1 - core)
        offset = (share - place) * share_rows
        inside = (iota >= place * share_rows) & (iota < (place + 1) * share_rows)
        names = jnp.where(inside, iota + offset, names)
    return names


def call(kernel, outs, args, scratch=(), flops=0, in_hbm=()):
    single = not isinstance(outs, (list, tuple))
    outs = [outs] if single else outs
    vmem = pl.BlockSpec(memory_space=pltpu.VMEM)
    args = [
        arg if at in in_hbm else pltpu.with_memory_space_constraint(arg, pltpu.VMEM)
        for at, arg in enumerate(args)
    ]
    results = pl.pallas_call(
        kernel,
        out_shape=tuple(pltpu.VMEM(out.shape, out.dtype) for out in outs),
        in_specs=[
            pl.BlockSpec(memory_space=pl.ANY) if at in in_hbm else vmem for at in range(len(args))
        ],
        out_specs=(vmem,) * len(outs),
        scratch_shapes=list(scratch),
        cost_estimate=pl.CostEstimate(flops=flops, transcendentals=0, bytes_accessed=0),
        compiler_params=pltpu.CompilerParams(vmem_limit_bytes=GRANT),
    )(*args)
    return results[0] if single else results


def shape(dims, kind):
    return jax.ShapeDtypeStruct(dims, kind)


def window_of(mask, exact):
    if not exact:
        return mask
    blk = lax.axis_index("blk")
    return lax.rem(blk - (blk ^ mask) + NEIGH // 2 + NEIGH, NEIGH)


def keys_kernel(exact, node_ref, mesh_hbm, weights_hbm, *refs):
    outs, (held, mesh, weight, sems) = refs[:NEIGH], refs[NEIGH:]
    get_mesh = pltpu.make_async_copy(mesh_hbm, mesh, sems.at[0])
    get_weight = pltpu.make_async_copy(weights_hbm.at[2], weight, sems.at[1])
    get_mesh.start()
    get_weight.start()
    picks = hot_columns(column(node_ref[...]), lanes(mesh.shape[0]))
    get_mesh.wait()
    rows = project(picks, mesh[...]).astype(BF16)
    get_weight.wait()
    keys = project(rows, weight[...]).astype(BF16)
    held[...] = keys.reshape(held.shape)
    for mask in range(NEIGH):
        outs[mask][...] = held[window_of(mask, exact)]


def edge_kernel(sender_ref, grid_ref, edges_ref, weights_ref, biases_ref, part_ref):
    names = lanes(grid_ref.shape[0])
    senders = column(sender_ref[...])
    for at in range(0, edges_ref.shape[0], TILE):
        picks = hot_columns(senders[at : at + TILE], names)
        nodes = project(picks, grid_ref[...]).astype(BF16)
        part_ref[at : at + TILE, :] = (
            project(edges_ref[at : at + TILE, :], weights_ref[0])
            + project(nodes, weights_ref[1])
            + biases_ref[1, 0:1, :]
        )


def grid_kernel(grid_ref, weights_ref, biases_ref, gains_ref, out_ref):
    for at in range(0, grid_ref.shape[0], TILE):
        nodes = grid_ref[at : at + TILE, :]
        first = project(nodes, weights_ref[0]) + biases_ref[0, 0:1, :]
        out_ref[at : at + TILE, :] = (
            nodes.astype(F32) + tail(first, weights_ref[1], biases_ref, gains_ref, 0)
        ).astype(BF16)


def message_kernel(exact, slot_ref, part_ref, weights_ref, biases_ref, gains_ref, *refs):
    keys, outs, table, sent = refs[:NEIGH], refs[NEIGH : 2 * NEIGH], refs[-2], refs[-1]
    cap = keys[0].shape[0]
    for window in range(NEIGH):
        table[window * cap : (window + 1) * cap, :] = keys[window][...]
    row = slot_ref[...]
    if exact:
        blk = lax.axis_index("blk")
        patch = (lax.div(row, cap) + (blk + NEIGH // 2)) & (NEIGH - 1)
        row = (patch ^ blk) * cap + lax.rem(row, cap)
    slots = column(row)
    names = lanes(table.shape[0])
    for at in range(0, part_ref.shape[0], TILE):
        picks = hot_columns(slots[at : at + TILE], names)
        first = part_ref[at : at + TILE, :] + project(picks, table[...])
        sent[at : at + TILE, :] = tail(first, weights_ref[3], biases_ref, gains_ref, 1).astype(BF16)
    sums = project(hot_rows(row, sublanes(table.shape[0])), sent[...]).astype(BF16)
    for window in range(NEIGH):
        outs[window][...] = sums[window * cap : (window + 1) * cap, :]


def land_kernel(exact, band_count, node_ref, *refs):
    pieces, given_ref, kept_ref, held = refs[:NEIGH], refs[NEIGH], refs[NEIGH + 1], refs[NEIGH + 2]
    for mask in range(NEIGH):
        held[window_of(mask, exact)] = pieces[mask][...]
    half = given_ref.shape[0]
    core = lax.rem(lax.axis_index("band"), 2)
    names = share_names(sublanes(2 * half), 2 * half // band_count, band_count, 1 - core)
    landed = held[...].reshape(-1, held.shape[2])
    given_ref[...] = project(hot_rows(node_ref[...], names[:half]), landed).astype(BF16)
    kept_ref[...] = project(hot_rows(node_ref[...], names[half:]), landed)


def own_share(place):
    band = lax.axis_index("band")
    return 2 * (place ^ lax.div(band, 2)) + lax.rem(band, 2)


def early_kernel(band_count, nodes_ref, edges_ref, w_nodes, w_edges, biases_ref, node_part_ref, edge_part_ref):
    share = node_part_ref.shape[0] // (band_count // 2)
    for place in range(band_count // 2):
        node_part_ref[place * share : (place + 1) * share, :] = (
            project(nodes_ref[own_share(place)], w_nodes[0]) + biases_ref[2, 0:1, :]
        )
    for at in range(0, edges_ref.shape[0], TILE):
        edge_part_ref[at : at + TILE, :] = (
            project(edges_ref[at : at + TILE, :], w_edges[0]) + biases_ref[3, 0:1, :]
        )


def node_kernel(band_count, bit, half_ref, got_ref, nodes_ref, part_ref, weights_ref, biases_ref, gains_ref, out_ref):
    share = out_ref.shape[0] // (band_count // 2)
    total = crossed(half_ref, got_ref, share, band_count, bit)
    first = part_ref[...] + project(total, weights_ref[1])
    change = tail(first, weights_ref[2], biases_ref, gains_ref, 2)
    for place in range(band_count // 2):
        at = place * share
        out_ref[at : at + share, :] = (
            nodes_ref[own_share(place)].astype(F32) + change[at : at + share, :]
        ).astype(BF16)


def crossed(half, got, share, band_count, bit):
    parts = []
    for place in range(band_count // 2):
        at, other = place * share, (place ^ bit) * share
        parts.append(half[at : at + share, :].astype(F32) + got[other : other + share, :].astype(F32))
    return jnp.concatenate(parts, axis=0).astype(BF16)


def sender_kernel(band_count, send_ref, own_ref, other_ref, weights_ref, kept_ref, given_ref, table, held):
    half = own_ref.shape[0]
    table[:half, :] = own_ref[...]
    table[half:, :] = other_ref[...]
    core = lax.rem(lax.axis_index("band"), 2)
    names = share_names(lanes(2 * half), 2 * half // band_count, band_count, core)
    rows = project(hot_columns(column(send_ref[...]), names), table[...]).astype(BF16)
    held[...] = project(rows, weights_ref[1]).astype(BF16).reshape(held.shape)
    blk = lax.axis_index("blk")
    for pair in range(kept_ref.shape[0]):
        kept_ref[pair] = held[blk ^ (2 * pair)]
        given_ref[pair] = held[blk ^ (2 * pair + 1)]


def target_kernel(band_count, receiver_ref, own_ref, other_ref, part_ref, weights_ref, out_ref, table):
    half = own_ref.shape[0]
    table[:half, :] = project(own_ref[...], weights_ref[2]).astype(BF16)
    table[half:, :] = project(other_ref[...], weights_ref[2]).astype(BF16)
    core = lax.rem(lax.axis_index("band"), 2)
    names = share_names(lanes(2 * half), 2 * half // band_count, band_count, core)
    receivers = column(receiver_ref[...])
    for at in range(0, part_ref.shape[0], TILE):
        picks = hot_columns(receivers[at : at + TILE], names)
        out_ref[at : at + TILE, :] = part_ref[at : at + TILE, :] + project(picks, table[...])


def process_kernel(
    band_count, mcap, sender_ref, receiver_ref, part_ref, keys_ref, weights_ref, biases_ref, gains_ref, given_ref, kept_ref, sent
):
    senders = column(sender_ref[...] ^ (lax.axis_index("blk") * mcap))
    names = lanes(keys_ref.shape[0])
    for at in range(0, part_ref.shape[0], TILE):
        picks = hot_columns(senders[at : at + TILE], names)
        first = part_ref[at : at + TILE, :] + project(picks, keys_ref[...])
        sent[at : at + TILE, :] = tail(first, weights_ref[3], biases_ref, gains_ref, 3).astype(BF16)
    half = given_ref.shape[0]
    core = lax.rem(lax.axis_index("band"), 2)
    places = share_names(sublanes(2 * half), 2 * half // band_count, band_count, 1 - core)
    given_ref[...] = project(hot_rows(receiver_ref[...], places[:half]), sent[...]).astype(BF16)
    kept_ref[...] = project(hot_rows(receiver_ref[...], places[half:]), sent[...])


def last_kernel(kept_ref, got_ref, half_ref, weights_ref, biases_ref, gains_ref, out_ref):
    own = half_ref[: out_ref.shape[0], :]
    total = (kept_ref[...] + got_ref[...].astype(F32)).astype(BF16)
    first = project(own, weights_ref[0]) + project(total, weights_ref[1]) + biases_ref[4, 0:1, :]
    out_ref[...] = (
        own.astype(F32) + tail(first, weights_ref[2], biases_ref, gains_ref, 4)
    ).astype(BF16)


def swap(rows, axis, mask):
    return lax.ppermute(rows, axis, [(i, i ^ mask) for i in range(lax.axis_size(axis))])


def window_exchange(blocks, back):
    blk_count = lax.axis_size("blk")
    pieces = []
    for window in range(NEIGH):
        if blk_count == NEIGH:
            pieces.append(swap(blocks[window], "blk", window) if window else blocks[0])
        else:
            distance = window - NEIGH // 2
            distance = distance if back else -distance
            route = [((i - distance) % blk_count, i) for i in range(blk_count)]
            pieces.append(lax.ppermute(blocks[window], "blk", route) if distance else blocks[window])
    return pieces


def body(
    grid_nodes,
    enc_edges,
    enc_sender,
    enc_slot,
    enc_slot_node,
    mesh_nodes,
    mesh_edges,
    mesh_sender,
    mesh_receiver,
    mesh_send_node,
    grid_weights,
    enc_edge_weights,
    enc_node_weights,
    proc_edge_weights,
    proc_node_weights,
    biases,
    gains,
):
    blk_count, band_count = lax.axis_size("blk"), lax.axis_size("band")
    patch_rows, width = mesh_nodes.shape
    share_rows, half_rows = patch_rows // band_count, patch_rows // 2
    edge_rows, grid_rows, medge_rows = enc_edges.shape[0], grid_nodes.shape[0], mesh_edges.shape[0]
    slots = enc_slot_node.shape[1]
    cap = slots // NEIGH
    senders_all = mesh_send_node.shape[1]
    mcap = senders_all // blk_count
    for count in (blk_count, band_count, cap, mcap):
        assert count & (count - 1) == 0
    exact = blk_count == NEIGH
    unit = 2 * width * width
    piece = shape((cap, width), BF16)
    half_bf, half_f = shape((half_rows, width), BF16), shape((half_rows, width), F32)

    slot_keys = call(
        functools.partial(keys_kernel, exact),
        [piece] * NEIGH,
        (enc_slot_node, mesh_nodes, enc_edge_weights),
        [
            pltpu.VMEM((NEIGH, cap, width), BF16),
            pltpu.VMEM((patch_rows, width), BF16),
            pltpu.VMEM((width, width), BF16),
            pltpu.SemaphoreType.DMA((2,)),
        ],
        unit * 2 * slots,
        (1, 2),
    )
    keys = window_exchange(slot_keys, False)

    edge_part = call(
        edge_kernel,
        shape((edge_rows, width), F32),
        (enc_sender.reshape(1, edge_rows), grid_nodes, enc_edges, enc_edge_weights, biases),
        (),
        unit * 3 * edge_rows,
    )
    slot_sums = call(
        functools.partial(message_kernel, exact),
        [piece] * NEIGH,
        (enc_slot.reshape(1, edge_rows), edge_part, enc_edge_weights, biases, gains, *keys),
        [pltpu.VMEM((slots, width), BF16), pltpu.VMEM((edge_rows, width), BF16)],
        unit * 3 * edge_rows,
    )
    landed = window_exchange(slot_sums, True)

    grid_out = call(
        grid_kernel,
        shape((grid_rows, width), BF16),
        (grid_nodes, grid_weights, biases, gains),
        (),
        unit * 2 * grid_rows,
    )
    nodes_by_share = mesh_nodes.reshape(band_count, share_rows, width)
    node_part, mesh_part = call(
        functools.partial(early_kernel, band_count),
        [half_f, shape((medge_rows, width), F32)],
        (nodes_by_share, mesh_edges, enc_node_weights, proc_edge_weights, biases),
        (),
        unit * (half_rows + medge_rows),
    )

    given, kept = call(
        functools.partial(land_kernel, exact, band_count),
        [half_bf, half_f],
        (enc_slot_node, *landed),
        [pltpu.VMEM((NEIGH, cap, width), BF16)],
        unit * patch_rows,
    )
    got = swap(given, "band", 1)
    half = (kept + got.astype(F32)).astype(BF16)
    mask = 2
    while True:
        got = swap(half, "band", mask)
        if 2 * mask >= band_count:
            break
        half = crossed(half, got, share_rows, band_count, mask // 2)
        mask *= 2
    half_mid = call(
        functools.partial(node_kernel, band_count, mask // 2),
        half_bf,
        (half, got, nodes_by_share, node_part, enc_node_weights, biases, gains),
        (),
        unit * 2 * half_rows,
    )
    other_mid = swap(half_mid, "band", 1)

    half_blocks = shape((blk_count // 2, mcap, width), BF16)
    kept, given = call(
        functools.partial(sender_kernel, band_count),
        [half_blocks, half_blocks],
        (mesh_send_node, half_mid, other_mid, proc_edge_weights),
        [pltpu.VMEM((patch_rows, width), BF16), pltpu.VMEM((blk_count, mcap, width), BF16)],
        unit * 2 * senders_all,
    )
    mask = 1
    while True:
        got = swap(given, "blk", mask)
        senders = jnp.stack([kept, got.reshape(kept.shape)], axis=1)
        mask *= 2
        if mask == blk_count:
            break
        view = senders.reshape(blk_count // (2 * mask), 2, mask * mcap, width)
        kept, given = view[:, 0], view[:, 1]
    arrived_senders = senders.reshape(senders_all, width)
    receivers = mesh_receiver.reshape(1, medge_rows)

    mesh_part = call(
        functools.partial(target_kernel, band_count),
        shape((medge_rows, width), F32),
        (receivers, half_mid, other_mid, mesh_part, proc_edge_weights),
        [pltpu.VMEM((patch_rows, width), BF16)],
        unit * (patch_rows + medge_rows),
    )
    given, kept = call(
        functools.partial(process_kernel, band_count, mcap),
        [half_bf, half_f],
        (
            mesh_sender.reshape(1, medge_rows),
            receivers,
            mesh_part,
            arrived_senders,
            proc_edge_weights,
            biases,
            gains,
        ),
        [pltpu.VMEM((medge_rows, width), BF16)],
        unit * 3 * medge_rows,
    )
    got = swap(given, "band", 1)
    count = band_count // 2
    while count > 1:
        shares = kept + got.astype(F32)
        count //= 2
        kept, given = shares[: count * share_rows], shares[count * share_rows :].astype(BF16)
        got = swap(given, "band", 2 * count)
    mesh_out = call(
        last_kernel,
        shape((share_rows, width), BF16),
        (kept, got, half_mid, proc_node_weights, biases, gains),
        (),
        unit * 3 * share_rows,
    )
    return (grid_out, mesh_out)


def solution(mesh):
    rows = P(("blk", "band"), None)
    flat = P(("blk", "band"))
    in_specs = (rows, rows, flat, flat, rows, P("blk", None), rows, flat, flat, rows) + (P(),) * 7
    return jax.shard_map(
        body, mesh=mesh, in_specs=in_specs, out_specs=(rows, rows), check_vma=False
    )
```

time: 108 us -> 85.9 us (0.80)
  Pallas kernels: 38.8 us -> 14.6 us
  waiting for transfers between devices: 21 us -> 38.6 us
  local copies, waits for them, and re-layouts: 14.6 us -> 6.18 us
  starting transfers between devices: 29.5 us -> 25.1 us
  other arithmetic: 2.72 us -> 0.2 us
    pallas_call x10 -> x11, Pallas kernels: 38.8 us -> 14.6 us  [call(): pl.pallas_call(kernel, out_shape=tuple((pltpu.VMEM(out.shape, out.dtype)...]
    ppermute x22, waiting for transfers between devices: 21 us -> 38.6 us  [swap(): lax.ppermute(rows, axis, [(i, i ^ mask) for i in range(lax.axis_size(axis...]
    squeeze x5 -> x0, local copies, waits for them, and re-layouts: 7.94 us -> none  [the longest x1 3.53 us: body(): enc_edge_weights[2]]
    ppermute x22, starting transfers between devices: 29.5 us -> 25.1 us  [swap(): lax.ppermute(rows, axis, [(i, i ^ mask) for i in range(lax.axis_size(axis...]
    unnamed x56 -> x41, local copies, waits for them, and re-layouts: 3.88 us -> 6.12 us
    reshape x3 -> x0, local copies, waits for them, and re-layouts: 1.44 us -> none  [the longest x1 0.76 us: body(): kept.reshape(share_rows, width)]
    add x3 -> x1, other arithmetic: 1.29 us -> 0.09 us  [body(): shares = kept + got.astype(F32)]
  transfers between devices with their start and end apart: 22 -> 22, of which waited for: 10 -> 15; matrix products, arithmetic and copies ran while one was open for 8% -> 1% of each run, Pallas kernels for 14% -> 7%
where the time goes in v3:
time: 85.9 us; the launch traced here: 85.7 us
  waiting for transfers between devices  38.6 us (45%)
  starting transfers between devices  25.1 us (29%)
  Pallas kernels  14.6 us (17%)
  local copies, waits for them, and re-layouts  6.18 us (7%)
  between operations  0.97 us (1%)
    ppermute x22, waiting for transfers between devices, swap(): lax.ppermute(rows, axis, [(i, i ^ mask) for i in range(lax.axis_size(axis...  38.6 us
    ppermute x22, starting transfers between devices, swap(): lax.ppermute(rows, axis, [(i, i ^ mask) for i in range(lax.axis_size(axis...  25.1 us
    pallas_call x11, Pallas kernels, call(): pl.pallas_call(kernel, out_shape=tuple((pltpu.VMEM(out.shape, out.dtype)...  14.6 us
    unnamed x41, local copies, waits for them, and re-layouts  6.12 us
  transfers between devices with their start and end apart: 22, of which 15 were waited for; matrix products, arithmetic and copies ran while one was open for 1% of the time, Pallas kernels for 7%

profile of v3, /device:TPU:0, one launch (start us, length us, event | category | flops | bytes accessed | tf_op | source)
XLA Modules:
  0.0 85.7 jit_solution(14980264646903111781)
XLA Ops:
  1.7 1.6 %copy-done.4 = bf16[4,512,512]{2,1,0:T(8,128)(2,1)S(1)} copy-done((bf16[4,512,512]{2,1,0:T(8,128)(2,1)S(1)}, bf16[4,512,512]{2,1,0:T(8,128)(2,1)}, u32[]{:S(2)}) %copy-start.4) | copy-done | bytes 2097176
  5.5 3.1 %collective-permute-start = (bf16[64,512]{1,0:T(8,128)(2,1)S(1)}, bf16[64,512]{1,0:T(8,128)(2,1)S(1)}, u32[]{:S(2)}, u32[]{:S(2)}) collective-permute-start(bf16[64,512]{1,0:T(8,128)(2,1)S(1)} %get-tuple-element.27), channel_id=1, source_target_pairs={{0,4},{4,0},{8,12},{12,8},{16,20},{20,16},{24,28},{28,24},{1,5},{5... | collective-permute-start | bytes 196616 | tf_op jit(solution)/shard_map/ppermute | solution.py:270
  8.6 1.6 %collective-permute-start.1 = (bf16[64,512]{1,0:T(8,128)(2,1)S(1)}, bf16[64,512]{1,0:T(8,128)(2,1)S(1)}, u32[]{:S(2)}, u32[]{:S(2)}) collective-permute-start(bf16[64,512]{1,0:T(8,128)(2,1)S(1)} %get-tuple-element.28), channel_id=1, source_target_pairs={{0,8},{4,12},{8,0},{12,4},{16,24},{20,28},{24,16},{28,20},{1,9},{5... | collective-permute-start | bytes 196616 | tf_op jit(solution)/shard_map/ppermute | solution.py:270
  10.1 3.0 %collective-permute-start.3 = (bf16[64,512]{1,0:T(8,128)(2,1)S(1)}, bf16[64,512]{1,0:T(8,128)(2,1)S(1)}, u32[]{:S(2)}, u32[]{:S(2)}) collective-permute-start(bf16[64,512]{1,0:T(8,128)(2,1)S(1)} %get-tuple-element.30), channel_id=1, source_target_pairs={{0,16},{4,20},{8,24},{12,28},{16,0},{20,4},{24,8},{28,12},{1,17},{... | collective-permute-start | bytes 196616 | tf_op jit(solution)/shard_map/ppermute | solution.py:270
  14.4 3.6 %collective-permute-start.5 = (bf16[64,512]{1,0:T(8,128)(2,1)S(1)}, bf16[64,512]{1,0:T(8,128)(2,1)S(1)}, u32[]{:S(2)}, u32[]{:S(2)}) collective-permute-start(bf16[64,512]{1,0:T(8,128)(2,1)S(1)} %get-tuple-element.32), channel_id=1, source_target_pairs={{0,24},{4,28},{8,16},{12,20},{16,8},{20,12},{24,0},{28,4},{1,25},{... | collective-permute-start | bytes 196616 | tf_op jit(solution)/shard_map/ppermute | solution.py:270
  19.3 2.2 %shard_map.177.part_ref = f32[1024,512]{1,0:T(8,128)S(1)} custom-call(s32[1,1024]{1,0:T(1,128)S(1)} %bitcast.24, bf16[512,512]{1,0:T(8,128)(2,1)S(1)} %copy-done.9, bf16[1024,512]{1,0:T(8,128)(2,1)S(1)} %copy-done.15, bf16[4,512,512]{2,1,0:T(8,128)(2,1)S(1)} %copy-done.5, f32[5,2,512]{2,1,0:T(2,128)S(1)} %copy-done.10), custom_call_target="tpu_custom_call" | custom-call | flops 1610612736 | tf_op jit(solution)/shard_map/pallas_call | solution.py:85
  21.5 1.8 %collective-permute-done.4.refs_5_ = bf16[64,512]{1,0:T(8,128)(2,1)S(1)} collective-permute-done((bf16[64,512]{1,0:T(8,128)(2,1)S(1)}, bf16[64,512]{1,0:T(8,128)(2,1)S(1)}, u32[]{:S(2)}, u32[]{:S(2)}) %collective-permute-start.4) | collective-permute-done | bytes 65568 | tf_op jit(solution)/shard_map/ppermute | solution.py:270
  23.3 1.8 %collective-permute-done.6.refs_7_ = bf16[64,512]{1,0:T(8,128)(2,1)S(1)} collective-permute-done((bf16[64,512]{1,0:T(8,128)(2,1)S(1)}, bf16[64,512]{1,0:T(8,128)(2,1)S(1)}, u32[]{:S(2)}, u32[]{:S(2)}) %collective-permute-start.6) | collective-permute-done | bytes 65568 | tf_op jit(solution)/shard_map/ppermute | solution.py:270
  25.1 2.4 %shard_map.179 = (bf16[64,512]{1,0:T(8,128)(2,1)S(1)}, bf16[64,512]{1,0:T(8,128)(2,1)S(1)}, bf16[64,512]{1,0:T(8,128)(2,1)S(1)}, bf16[64,512]{1,0:T(8,128)(2,1)S...) custom-call(s32[1,1024]{1,0:T(1,128)S(1)} %bitcast.25, ...), custom_call_target="tpu_custom_call" | custom-call | flops 1610612736 | tf_op jit(solution)/shard_map/pallas_call | solution.py:85
  27.6 2.8 %collective-permute-start.10 = (bf16[64,512]{1,0:T(8,128)(2,1)S(1)}, bf16[64,512]{1,0:T(8,128)(2,1)S(1)}, u32[]{:S(2)}, u32[]{:S(2)}) collective-permute-start(bf16[64,512]{1,0:T(8,128)(2,1)S(1)} %get-tuple-element.38), channel_id=1, source_target_pairs={{0,16},{4,20},{8,24},{12,28},{16,0},{20,4},{24,8},{28,12},{1,17},{... | collective-permute-start | bytes 196616 | tf_op jit(solution)/shard_map/ppermute | solution.py:270
  32.0 3.3 %collective-permute-start.13 = (bf16[64,512]{1,0:T(8,128)(2,1)S(1)}, bf16[64,512]{1,0:T(8,128)(2,1)S(1)}, u32[]{:S(2)}, u32[]{:S(2)}) collective-permute-start(bf16[64,512]{1,0:T(8,128)(2,1)S(1)} %get-tuple-element.41), channel_id=1, source_target_pairs={{0,28},{4,24},{8,20},{12,16},{16,12},{20,8},{24,4},{28,0},{1,29},{... | collective-permute-start | bytes 196616 | tf_op jit(solution)/shard_map/ppermute | solution.py:270
  35.8 2.2 %collective-permute-done.10.refs_4_ = bf16[64,512]{1,0:T(8,128)(2,1)S(1)} collective-permute-done((bf16[64,512]{1,0:T(8,128)(2,1)S(1)}, bf16[64,512]{1,0:T(8,128)(2,1)S(1)}, u32[]{:S(2)}, u32[]{:S(2)}) %collective-permute-start.10) | collective-permute-done | bytes 65568 | tf_op jit(solution)/shard_map/ppermute | solution.py:270
  38.0 2.4 %collective-permute-done.11.refs_5_ = bf16[64,512]{1,0:T(8,128)(2,1)S(1)} collective-permute-done((bf16[64,512]{1,0:T(8,128)(2,1)S(1)}, bf16[64,512]{1,0:T(8,128)(2,1)S(1)}, u32[]{:S(2)}, u32[]{:S(2)}) %collective-permute-start.11) | collective-permute-done | bytes 65568 | tf_op jit(solution)/shard_map/ppermute | solution.py:270
  40.6 2.2 %collective-permute-done.8.refs_2_ = bf16[64,512]{1,0:T(8,128)(2,1)S(1)} collective-permute-done((bf16[64,512]{1,0:T(8,128)(2,1)S(1)}, bf16[64,512]{1,0:T(8,128)(2,1)S(1)}, u32[]{:S(2)}, u32[]{:S(2)}) %collective-permute-start.8) | collective-permute-done | bytes 65568 | tf_op jit(solution)/shard_map/ppermute | solution.py:270
  42.8 2.7 %collective-permute-done.9.refs_3_ = bf16[64,512]{1,0:T(8,128)(2,1)S(1)} collective-permute-done((bf16[64,512]{1,0:T(8,128)(2,1)S(1)}, bf16[64,512]{1,0:T(8,128)(2,1)S(1)}, u32[]{:S(2)}, u32[]{:S(2)}) %collective-permute-start.9) | collective-permute-done | bytes 65568 | tf_op jit(solution)/shard_map/ppermute | solution.py:270
  46.2 1.6 %collective-permute-done.14 = bf16[320,512]{1,0:T(8,128)(2,1)S(1)} collective-permute-done((bf16[320,512]{1,0:T(8,128)(2,1)S(1)}, bf16[320,512]{1,0:T(8,128)(2,1)S(1)}, u32[]{:S(2)}, u32[]{:S(2)}) %collective-permute-start.14) | collective-permute-done | bytes 327712 | tf_op jit(solution)/shard_map/ppermute | solution.py:270
  50.2 7.5 %collective-permute-done.15.got_ref = bf16[320,512]{1,0:T(8,128)(2,1)S(1)} collective-permute-done((bf16[320,512]{1,0:T(8,128)(2,1)S(1)}, bf16[320,512]{1,0:T(8,128)(2,1)S(1)}, u32[]{:S(2)}, u32[]{:S(2)}) %collective-permute-start.15) | collective-permute-done | bytes 327712 | tf_op jit(solution)/shard_map/ppermute | solution.py:270
  58.6 1.6 %collective-permute-done.16.other_ref = bf16[320,512]{1,0:T(8,128)(2,1)S(1)} collective-permute-done((bf16[320,512]{1,0:T(8,128)(2,1)S(1)}, bf16[320,512]{1,0:T(8,128)(2,1)S(1)}, u32[]{:S(2)}, u32[]{:S(2)}) %collective-permute-start.16) | collective-permute-done | bytes 327712 | tf_op jit(solution)/shard_map/ppermute | solution.py:270
  61.9 2.8 %collective-permute-done.17 = bf16[4,8,512]{2,1,0:T(8,128)(2,1)S(1)} collective-permute-done((bf16[4,8,512]{2,1,0:T(8,128)(2,1)S(1)}, bf16[4,8,512]{2,1,0:T(8,128)(2,1)S(1)}, u32[]{:S(2)}, u32[]{:S(2)}) %collective-permute-start.17) | collective-permute-done | bytes 32800 | tf_op jit(solution)/shard_map/ppermute | solution.py:270
  64.8 3.9 %collective-permute-done.18 = bf16[2,16,512]{2,1,0:T(8,128)(2,1)S(1)} collective-permute-done((bf16[2,16,512]{2,1,0:T(8,128)(2,1)S(1)}, bf16[2,16,512]{2,1,0:T(8,128)(2,1)S(1)}, u32[]{:S(2)}, u32[]{:S(2)}) %collective-permute-start.18) | collective-permute-done | bytes 32800 | tf_op jit(solution)/shard_map/ppermute | solution.py:270
  70.2 3.4 %collective-permute-done.19 = bf16[1,32,512]{2,1,0:T(8,128)(2,1)S(1)} collective-permute-done((bf16[1,32,512]{2,1,0:T(8,128)(2,1)S(1)}, bf16[1,32,512]{2,1,0:T(8,128)(2,1)S(1)}, u32[]{:S(2)}, u32[]{:S(2)}) %collective-permute-start.19) | collective-permute-done | bytes 32800 | tf_op jit(solution)/shard_map/ppermute | solution.py:270
  73.6 2.5 %shard_map.185 = (bf16[320,512]{1,0:T(8,128)(2,1)S(1)}, f32[320,512]{1,0:T(8,128)S(1)}) custom-call(s32[1,1024]{1,0:T(1,128)S(1)} %bitcast.26, s32[1,1024]{1,0:T(1,128)S(1)} %bitcast.23, f32[1024,512]{1,0:T(8,128)S(1)} %shard_map.183.part_ref, bf16[64,512]{1,0:T(8,128)(2,1)S(1)} %bitcast.20, bf16[4,512,512]{2,1,0:T(8,128)(2,1)S(1)} %copy-done, ...), custom_call_target="tpu_custom_call" | custom-call | flops 1610612736 | tf_op jit(solution)/shard_map/pallas_call | solution.py:85
  76.2 1.6 %collective-permute-done.20 = bf16[320,512]{1,0:T(8,128)(2,1)S(1)} collective-permute-done((bf16[320,512]{1,0:T(8,128)(2,1)S(1)}, bf16[320,512]{1,0:T(8,128)(2,1)S(1)}, u32[]{:S(2)}, u32[]{:S(2)}) %collective-permute-start.20) | collective-permute-done | bytes 327712 | tf_op jit(solution)/shard_map/ppermute | solution.py:270
  81.5 2.8 %collective-permute-done.21.got_ref = bf16[160,512]{1,0:T(8,128)(2,1)S(1)} collective-permute-done((bf16[160,512]{1,0:T(8,128)(2,1)S(1)}, bf16[160,512]{1,0:T(8,128)(2,1)S(1)}, u32[]{:S(2)}, u32[]{:S(2)}) %collective-permute-start.21) | collective-permute-done | bytes 163872 | tf_op jit(solution)/shard_map/ppermute | solution.py:270
  (82 shorter events, 20.3 us)
Async XLA Ops:
  5.5 8.9 %collective-permute-start = (bf16[64,512]{1,0:T(8,128)(2,1)S(1)}, bf16[64,512]{1,0:T(8,128)(2,1)S(1)}, u32[]{:S(2)}, u32[]{:S(2)}) collective-permute-start(bf16[64,512]{1,0:T(8,128)(2,1)S(1)} %get-tuple-element.27), channel_id=1, source_target_pairs={{0,4},{4,0},{8,12},{12,8},{16,20},{20,16},{24,28},{28,24},{1,5},{5... | collective-permute-start | bytes 196616 | tf_op jit(solution)/shard_map/ppermute | solution.py:270
  8.6 9.5 %collective-permute-start.1 = (bf16[64,512]{1,0:T(8,128)(2,1)S(1)}, bf16[64,512]{1,0:T(8,128)(2,1)S(1)}, u32[]{:S(2)}, u32[]{:S(2)}) collective-permute-start(bf16[64,512]{1,0:T(8,128)(2,1)S(1)} %get-tuple-element.28), channel_id=1, source_target_pairs={{0,8},{4,12},{8,0},{12,4},{16,24},{20,28},{24,16},{28,20},{1,9},{5... | collective-permute-start | bytes 196616 | tf_op jit(solution)/shard_map/ppermute | solution.py:270
  10.1 11.3 %collective-permute-start.2 = (bf16[64,512]{1,0:T(8,128)(2,1)S(1)}, bf16[64,512]{1,0:T(8,128)(2,1)S(1)}, u32[]{:S(2)}, u32[]{:S(2)}) collective-permute-start(bf16[64,512]{1,0:T(8,128)(2,1)S(1)} %get-tuple-element.29), channel_id=1, source_target_pairs={{0,12},{4,8},{8,4},{12,0},{16,28},{20,24},{24,20},{28,16},{1,13},{... | collective-permute-start | bytes 196616 | tf_op jit(solution)/shard_map/ppermute | solution.py:270
  10.1 11.3 %collective-permute-start.3 = (bf16[64,512]{1,0:T(8,128)(2,1)S(1)}, bf16[64,512]{1,0:T(8,128)(2,1)S(1)}, u32[]{:S(2)}, u32[]{:S(2)}) collective-permute-start(bf16[64,512]{1,0:T(8,128)(2,1)S(1)} %get-tuple-element.30), channel_id=1, source_target_pairs={{0,16},{4,20},{8,24},{12,28},{16,0},{20,4},{24,8},{28,12},{1,17},{... | collective-permute-start | bytes 196616 | tf_op jit(solution)/shard_map/ppermute | solution.py:270
  13.1 10.2 %collective-permute-start.4 = (bf16[64,512]{1,0:T(8,128)(2,1)S(1)}, bf16[64,512]{1,0:T(8,128)(2,1)S(1)}, u32[]{:S(2)}, u32[]{:S(2)}) collective-permute-start(bf16[64,512]{1,0:T(8,128)(2,1)S(1)} %get-tuple-element.31), channel_id=1, source_target_pairs={{0,20},{4,16},{8,28},{12,24},{16,4},{20,0},{24,12},{28,8},{1,21},{... | collective-permute-start | bytes 196616 | tf_op jit(solution)/shard_map/ppermute | solution.py:270
  14.4 8.9 %collective-permute-start.5 = (bf16[64,512]{1,0:T(8,128)(2,1)S(1)}, bf16[64,512]{1,0:T(8,128)(2,1)S(1)}, u32[]{:S(2)}, u32[]{:S(2)}) collective-permute-start(bf16[64,512]{1,0:T(8,128)(2,1)S(1)} %get-tuple-element.32), channel_id=1, source_target_pairs={{0,24},{4,28},{8,16},{12,20},{16,8},{20,12},{24,0},{28,4},{1,25},{... | collective-permute-start | bytes 196616 | tf_op jit(solution)/shard_map/ppermute | solution.py:270
  18.0 7.1 %collective-permute-start.6 = (bf16[64,512]{1,0:T(8,128)(2,1)S(1)}, bf16[64,512]{1,0:T(8,128)(2,1)S(1)}, u32[]{:S(2)}, u32[]{:S(2)}) collective-permute-start(bf16[64,512]{1,0:T(8,128)(2,1)S(1)} %get-tuple-element.33), channel_id=1, source_target_pairs={{0,28},{4,24},{8,20},{12,16},{16,12},{20,8},{24,4},{28,0},{1,29},{... | collective-permute-start | bytes 196616 | tf_op jit(solution)/shard_map/ppermute | solution.py:270
  25.1 24.2 %copy-start.1 = (bf16[3,512,512]{2,1,0:T(8,128)(2,1)S(1)}, bf16[3,512,512]{2,1,0:T(8,128)(2,1)}, u32[]{:S(2)}) copy-start(bf16[3,512,512]{2,1,0:T(8,128)(2,1)} %weights_ref.11) | copy-start | bytes 4718596
  25.1 24.2 %copy-start.3 = (bf16[640,512]{1,0:T(8,128)(2,1)S(1)}, bf16[640,512]{1,0:T(8,128)(2,1)}, u32[]{:S(2)}) copy-start(bf16[640,512]{1,0:T(8,128)(2,1)} %mesh_hbm.1) | copy-start | bytes 1966084
  27.6 10.4 %collective-permute-start.10 = (bf16[64,512]{1,0:T(8,128)(2,1)S(1)}, bf16[64,512]{1,0:T(8,128)(2,1)S(1)}, u32[]{:S(2)}, u32[]{:S(2)}) collective-permute-start(bf16[64,512]{1,0:T(8,128)(2,1)S(1)} %get-tuple-element.38), channel_id=1, source_target_pairs={{0,16},{4,20},{8,24},{12,28},{16,0},{20,4},{24,8},{28,12},{1,17},{... | collective-permute-start | bytes 196616 | tf_op jit(solution)/shard_map/ppermute | solution.py:270
  30.4 9.9 %collective-permute-start.11 = (bf16[64,512]{1,0:T(8,128)(2,1)S(1)}, bf16[64,512]{1,0:T(8,128)(2,1)S(1)}, u32[]{:S(2)}, u32[]{:S(2)}) collective-permute-start(bf16[64,512]{1,0:T(8,128)(2,1)S(1)} %get-tuple-element.39), channel_id=1, source_target_pairs={{0,20},{4,16},{8,28},{12,24},{16,4},{20,0},{24,12},{28,8},{1,21},{... | collective-permute-start | bytes 196616 | tf_op jit(solution)/shard_map/ppermute | solution.py:270
  30.5 9.8 %collective-permute-start.12 = (bf16[64,512]{1,0:T(8,128)(2,1)S(1)}, bf16[64,512]{1,0:T(8,128)(2,1)S(1)}, u32[]{:S(2)}, u32[]{:S(2)}) collective-permute-start(bf16[64,512]{1,0:T(8,128)(2,1)S(1)} %get-tuple-element.40), channel_id=1, source_target_pairs={{0,24},{4,28},{8,16},{12,20},{16,8},{20,12},{24,0},{28,4},{1,25},{... | collective-permute-start | bytes 196616 | tf_op jit(solution)/shard_map/ppermute | solution.py:270
  32.0 8.4 %collective-permute-start.13 = (bf16[64,512]{1,0:T(8,128)(2,1)S(1)}, bf16[64,512]{1,0:T(8,128)(2,1)S(1)}, u32[]{:S(2)}, u32[]{:S(2)}) collective-permute-start(bf16[64,512]{1,0:T(8,128)(2,1)S(1)} %get-tuple-element.41), channel_id=1, source_target_pairs={{0,28},{4,24},{8,20},{12,16},{16,12},{20,8},{24,4},{28,0},{1,29},{... | collective-permute-start | bytes 196616 | tf_op jit(solution)/shard_map/ppermute | solution.py:270
  35.3 5.3 %collective-permute-start.7 = (bf16[64,512]{1,0:T(8,128)(2,1)S(1)}, bf16[64,512]{1,0:T(8,128)(2,1)S(1)}, u32[]{:S(2)}, u32[]{:S(2)}) collective-permute-start(bf16[64,512]{1,0:T(8,128)(2,1)S(1)} %get-tuple-element.35), channel_id=1, source_target_pairs={{0,4},{4,0},{8,12},{12,8},{16,20},{20,16},{24,28},{28,24},{1,5},{5... | collective-permute-start | bytes 196616 | tf_op jit(solution)/shard_map/ppermute | solution.py:270
  38.0 4.8 %collective-permute-start.8 = (bf16[64,512]{1,0:T(8,128)(2,1)S(1)}, bf16[64,512]{1,0:T(8,128)(2,1)S(1)}, u32[]{:S(2)}, u32[]{:S(2)}) collective-permute-start(bf16[64,512]{1,0:T(8,128)(2,1)S(1)} %get-tuple-element.36), channel_id=1, source_target_pairs={{0,8},{4,12},{8,0},{12,4},{16,24},{20,28},{24,16},{28,20},{1,9},{5... | collective-permute-start | bytes 196616 | tf_op jit(solution)/shard_map/ppermute | solution.py:270
  40.4 5.2 %collective-permute-start.9 = (bf16[64,512]{1,0:T(8,128)(2,1)S(1)}, bf16[64,512]{1,0:T(8,128)(2,1)S(1)}, u32[]{:S(2)}, u32[]{:S(2)}) collective-permute-start(bf16[64,512]{1,0:T(8,128)(2,1)S(1)} %get-tuple-element.37), channel_id=1, source_target_pairs={{0,12},{4,8},{8,4},{12,0},{16,28},{20,24},{24,20},{28,16},{1,13},{... | collective-permute-start | bytes 196616 | tf_op jit(solution)/shard_map/ppermute | solution.py:270
  46.1 1.7 %collective-permute-start.14 = (bf16[320,512]{1,0:T(8,128)(2,1)S(1)}, bf16[320,512]{1,0:T(8,128)(2,1)S(1)}, u32[]{:S(2)}, u32[]{:S(2)}) collective-permute-start(bf16[320,512]{1,0:T(8,128)(2,1)S(1)} %get-tuple-element.43), channel_id=1, source_target_pairs={{0,1},{1,0},{2,3},{3,2},{4,5},{5,4},{6,7},{7,6},{8,9},{9,8},{10,11... | collective-permute-start | bytes 983048 | tf_op jit(solution)/shard_map/ppermute | solution.py:270
  47.9 9.8 %collective-permute-start.15 = (bf16[320,512]{1,0:T(8,128)(2,1)S(1)}, bf16[320,512]{1,0:T(8,128)(2,1)S(1)}, u32[]{:S(2)}, u32[]{:S(2)}) collective-permute-start(bf16[320,512]{1,0:T(8,128)(2,1)S(1)} %add_convert_fusion.half_ref), channel_id=1, source_target_pairs={{0,2},{1,3},{2,0},{3,1},{4,6},{5,7},{6,4},{7,5},{8,10},{9,11},{10,... | collective-permute-start | bytes 983048 | tf_op jit(solution)/shard_map/ppermute | solution.py:270
  58.5 1.7 %collective-permute-start.16 = (bf16[320,512]{1,0:T(8,128)(2,1)S(1)}, bf16[320,512]{1,0:T(8,128)(2,1)S(1)}, u32[]{:S(2)}, u32[]{:S(2)}) collective-permute-start(bf16[320,512]{1,0:T(8,128)(2,1)S(1)} %shard_map.182.own_ref.half_ref), channel_id=1, source_target_pairs={{0,1},{1,0},{2,3},{3,2},{4,5},{5,4},{6,7},{7,6},{8,9},{9,8},{10,11... | collective-permute-start | bytes 983048 | tf_op jit(solution)/shard_map/ppermute | solution.py:270
  60.7 4.0 %collective-permute-start.17 = (bf16[4,8,512]{2,1,0:T(8,128)(2,1)S(1)}, bf16[4,8,512]{2,1,0:T(8,128)(2,1)S(1)}, u32[]{:S(2)}, u32[]{:S(2)}) collective-permute-start(bf16[4,8,512]{2,1,0:T(8,128)(2,1)S(1)} %get-tuple-element.47), channel_id=1, source_target_pairs={{0,4},{4,0},{8,12},{12,8},{16,20},{20,16},{24,28},{28,24},{1,5},{5... | collective-permute-start | bytes 98312 | tf_op jit(solution)/shard_map/ppermute | solution.py:270
  64.7 4.0 %collective-permute-start.18 = (bf16[2,16,512]{2,1,0:T(8,128)(2,1)S(1)}, bf16[2,16,512]{2,1,0:T(8,128)(2,1)S(1)}, u32[]{:S(2)}, u32[]{:S(2)}) collective-permute-start(bf16[2,16,512]{2,1,0:T(8,128)(2,1)S(1)} %get-tuple-element.53), channel_id=1, source_target_pairs={{0,8},{4,12},{8,0},{12,4},{16,24},{20,28},{24,16},{28,20},{1,9},{5... | collective-permute-start | bytes 98312 | tf_op jit(solution)/shard_map/ppermute | solution.py:270
  68.7 4.9 %collective-permute-start.19 = (bf16[1,32,512]{2,1,0:T(8,128)(2,1)S(1)}, bf16[1,32,512]{2,1,0:T(8,128)(2,1)S(1)}, u32[]{:S(2)}, u32[]{:S(2)}) collective-permute-start(bf16[1,32,512]{2,1,0:T(8,128)(2,1)S(1)} %get-tuple-element.51), channel_id=1, source_target_pairs={{0,16},{4,20},{8,24},{12,28},{16,0},{20,4},{24,8},{28,12},{1,17},{... | collective-permute-start | bytes 98312 | tf_op jit(solution)/shard_map/ppermute | solution.py:270
  76.1 1.7 %collective-permute-start.20 = (bf16[320,512]{1,0:T(8,128)(2,1)S(1)}, bf16[320,512]{1,0:T(8,128)(2,1)S(1)}, u32[]{:S(2)}, u32[]{:S(2)}) collective-permute-start(bf16[320,512]{1,0:T(8,128)(2,1)S(1)} %get-tuple-element.49), channel_id=1, source_target_pairs={{0,1},{1,0},{2,3},{3,2},{4,5},{5,4},{6,7},{7,6},{8,9},{9,8},{10,11... | collective-permute-start | bytes 983048 | tf_op jit(solution)/shard_map/ppermute | solution.py:270
  77.9 6.3 %collective-permute-start.21 = (bf16[160,512]{1,0:T(8,128)(2,1)S(1)}, bf16[160,512]{1,0:T(8,128)(2,1)S(1)}, u32[]{:S(2)}, u32[]{:S(2)}) collective-permute-start(bf16[160,512]{1,0:T(8,128)(2,1)S(1)} %slice.35), channel_id=1, source_target_pairs={{0,2},{1,3},{2,0},{3,1},{4,6},{5,7},{6,4},{7,5},{8,10},{9,11},{10,... | collective-permute-start | bytes 491528 | tf_op jit(solution)/shard_map/ppermute | solution.py:270
  (17 other events, 153.1 us)

commit v4 on v3

--- a/solution.py
+++ b/solution.py
@@ -79,14 +79,14 @@
     outs = [outs] if single else outs
     vmem = pl.BlockSpec(memory_space=pltpu.VMEM)
     args = [
-        arg if at in in_hbm else pltpu.with_memory_space_constraint(arg, pltpu.VMEM)
+        pltpu.with_memory_space_constraint(arg, pltpu.HBM if at in in_hbm else pltpu.VMEM)
         for at, arg in enumerate(args)
     ]
     results = pl.pallas_call(
         kernel,
         out_shape=tuple(pltpu.VMEM(out.shape, out.dtype) for out in outs),
         in_specs=[
-            pl.BlockSpec(memory_space=pl.ANY) if at in in_hbm else vmem for at in range(len(args))
+            pl.BlockSpec(memory_space=pltpu.HBM) if at in in_hbm else vmem for at in range(len(args))
         ],
         out_specs=(vmem,) * len(outs),
         scratch_shapes=list(scratch),
@@ -107,16 +107,21 @@
     return lax.rem(blk - (blk ^ mask) + NEIGH // 2 + NEIGH, NEIGH)
 
 
-def keys_kernel(exact, node_ref, mesh_hbm, weights_hbm, *refs):
-    outs, (held, mesh, weight, sems) = refs[:NEIGH], refs[NEIGH:]
-    get_mesh = pltpu.make_async_copy(mesh_hbm, mesh, sems.at[0])
-    get_weight = pltpu.make_async_copy(weights_hbm.at[2], weight, sems.at[1])
-    get_mesh.start()
-    get_weight.start()
-    picks = hot_columns(column(node_ref[...]), lanes(mesh.shape[0]))
-    get_mesh.wait()
+def keys_kernel(exact, node_hbm, mesh_hbm, weights_hbm, *refs):
+    outs, (held, nodes, mesh, weight, sems) = refs[:NEIGH], refs[NEIGH:]
+    copies = [
+        pltpu.make_async_copy(source, target, sems.at[at])
+        for at, (source, target) in enumerate(
+            ((node_hbm, nodes), (mesh_hbm, mesh), (weights_hbm.at[2], weight))
+        )
+    ]
+    for copy in copies:
+        copy.start()
+    copies[0].wait()
+    picks = hot_columns(column(nodes[...]), lanes(mesh.shape[0]))
+    copies[1].wait()
     rows = project(picks, mesh[...]).astype(BF16)
-    get_weight.wait()
+    copies[2].wait()
     keys = project(rows, weight[...]).astype(BF16)
     held[...] = keys.reshape(held.shape)
     for mask in range(NEIGH):
@@ -145,8 +150,10 @@
         ).astype(BF16)
 
 
-def message_kernel(exact, slot_ref, part_ref, weights_ref, biases_ref, gains_ref, *refs):
-    keys, outs, table, sent = refs[:NEIGH], refs[NEIGH : 2 * NEIGH], refs[-2], refs[-1]
+def message_kernel(exact, slot_ref, part_ref, weights_ref, biases_ref, gains_ref, near_ref, far_ref, *refs):
+    keys, outs, (lists_ref, table, sent) = refs[:NEIGH], refs[NEIGH : 2 * NEIGH], refs[2 * NEIGH :]
+    lists_ref[: near_ref.shape[0], :] = near_ref[...]
+    lists_ref[near_ref.shape[0] :, :] = far_ref[...]
     cap = keys[0].shape[0]
     for window in range(NEIGH):
         table[window * cap : (window + 1) * cap, :] = keys[window][...]
@@ -166,16 +173,29 @@
         outs[window][...] = sums[window * cap : (window + 1) * cap, :]
 
 
-def land_kernel(exact, band_count, node_ref, *refs):
-    pieces, given_ref, kept_ref, held = refs[:NEIGH], refs[NEIGH], refs[NEIGH + 1], refs[NEIGH + 2]
+def hot_lists(lists_ref, row):
+    return jnp.concatenate(
+        [
+            hot_columns(column(lists_ref[at : at + 1, :]), row)
+            for at in range(lists_ref.shape[0])
+        ],
+        axis=0,
+    )
+
+
+def land_kernel(exact, band_count, node_ref, own_ref, other_ref, *refs):
+    pieces, (given_ref, kept_ref, listed_ref, held) = refs[:NEIGH], refs[NEIGH:]
     for mask in range(NEIGH):
         held[window_of(mask, exact)] = pieces[mask][...]
-    half = given_ref.shape[0]
+    half = kept_ref.shape[0]
     core = lax.rem(lax.axis_index("band"), 2)
     names = share_names(sublanes(2 * half), 2 * half // band_count, band_count, 1 - core)
+    row = node_ref[...]
     landed = held[...].reshape(-1, held.shape[2])
-    given_ref[...] = project(hot_rows(node_ref[...], names[:half]), landed).astype(BF16)
-    kept_ref[...] = project(hot_rows(node_ref[...], names[half:]), landed)
+    given_ref[:half, :] = project(hot_rows(row, names[:half]), landed).astype(BF16)
+    given_ref[half:, :] = project(hot_lists(other_ref, row), landed).astype(BF16)
+    kept_ref[...] = project(hot_rows(row, names[half:]), landed)
+    listed_ref[...] = project(hot_lists(own_ref, row), landed)
 
 
 def own_share(place):
@@ -183,8 +203,14 @@
     return 2 * (place ^ lax.div(band, 2)) + lax.rem(band, 2)
 
 
-def early_kernel(band_count, nodes_ref, edges_ref, w_nodes, w_edges, biases_ref, node_part_ref, edge_part_ref):
+def early_kernel(
+    band_count, send_ref, nodes_ref, edges_ref, w_nodes, w_edges, biases_ref, node_part_ref, edge_part_ref, listed_ref, listed_part_ref
+):
     share = node_part_ref.shape[0] // (band_count // 2)
+    nodes = nodes_ref[...].reshape(-1, nodes_ref.shape[2])
+    rows = project(hot_columns(column(send_ref[...]), lanes(nodes.shape[0])), nodes).astype(BF16)
+    listed_ref[...] = rows
+    listed_part_ref[...] = project(rows, w_nodes[0]) + biases_ref[2, 0:1, :]
     for place in range(band_count // 2):
         node_part_ref[place * share : (place + 1) * share, :] = (
             project(nodes_ref[own_share(place)], w_nodes[0]) + biases_ref[2, 0:1, :]
@@ -215,14 +241,14 @@
     return jnp.concatenate(parts, axis=0).astype(BF16)
 
 
-def sender_kernel(band_count, send_ref, own_ref, other_ref, weights_ref, kept_ref, given_ref, table, held):
-    half = own_ref.shape[0]
-    table[:half, :] = own_ref[...]
-    table[half:, :] = other_ref[...]
-    core = lax.rem(lax.axis_index("band"), 2)
-    names = share_names(lanes(2 * half), 2 * half // band_count, band_count, core)
-    rows = project(hot_columns(column(send_ref[...]), names), table[...]).astype(BF16)
-    held[...] = project(rows, weights_ref[1]).astype(BF16).reshape(held.shape)
+def sender_kernel(
+    sums_ref, got_ref, nodes_ref, part_ref, w_nodes, w_edges, biases_ref, gains_ref, kept_ref, given_ref, held
+):
+    total = (sums_ref[...].astype(F32) + got_ref[...].astype(F32)).astype(BF16)
+    first = part_ref[...] + project(total, w_nodes[1])
+    change = tail(first, w_nodes[2], biases_ref, gains_ref, 2)
+    rows = (nodes_ref[...].astype(F32) + change).astype(BF16)
+    held[...] = project(rows, w_edges[1]).astype(BF16).reshape(held.shape)
     blk = lax.axis_index("blk")
     for pair in range(kept_ref.shape[0]):
         kept_ref[pair] = held[blk ^ (2 * pair)]
@@ -324,12 +350,13 @@
         (enc_slot_node, mesh_nodes, enc_edge_weights),
         [
             pltpu.VMEM((NEIGH, cap, width), BF16),
+            pltpu.VMEM((1, slots), jnp.int32),
             pltpu.VMEM((patch_rows, width), BF16),
             pltpu.VMEM((width, width), BF16),
-            pltpu.SemaphoreType.DMA((2,)),
+            pltpu.SemaphoreType.DMA((3,)),
         ],
         unit * 2 * slots,
-        (1, 2),
+        (0, 1, 2),
     )
     keys = window_exchange(slot_keys, False)
 
@@ -340,10 +367,17 @@
         (),
         unit * 3 * edge_rows,
     )
-    slot_sums = call(
+    near, mask = mesh_send_node, 2
+    while True:
+        far = swap(near, "band", mask)
+        mask *= 2
+        if mask >= band_count:
+            break
+        near = jnp.concatenate([near, far], axis=0)
+    *slot_sums, lists = call(
         functools.partial(message_kernel, exact),
-        [piece] * NEIGH,
-        (enc_slot.reshape(1, edge_rows), edge_part, enc_edge_weights, biases, gains, *keys),
+        [piece] * NEIGH + [shape((band_count // 2, senders_all), jnp.int32)],
+        (enc_slot.reshape(1, edge_rows), edge_part, enc_edge_weights, biases, gains, near, far, *keys),
         [pltpu.VMEM((slots, width), BF16), pltpu.VMEM((edge_rows, width), BF16)],
         unit * 3 * edge_rows,
     )
@@ -356,24 +390,36 @@
         (),
         unit * 2 * grid_rows,
     )
+    other_lists = swap(lists, "band", 1)
+    listed = band_count // 2 * senders_all
+
     nodes_by_share = mesh_nodes.reshape(band_count, share_rows, width)
-    node_part, mesh_part = call(
+    node_part, mesh_part, listed_nodes, listed_part = call(
         functools.partial(early_kernel, band_count),
-        [half_f, shape((medge_rows, width), F32)],
-        (nodes_by_share, mesh_edges, enc_node_weights, proc_edge_weights, biases),
+        [half_f, shape((medge_rows, width), F32), shape((senders_all, width), BF16), shape((senders_all, width), F32)],
+        (mesh_send_node, nodes_by_share, mesh_edges, enc_node_weights, proc_edge_weights, biases),
         (),
-        unit * (half_rows + medge_rows),
-    )
-
-    given, kept = call(
+        unit * (half_rows + medge_rows + 2 * senders_all),
+    )
+
+    given, kept, kept_listed = call(
         functools.partial(land_kernel, exact, band_count),
-        [half_bf, half_f],
-        (enc_slot_node, *landed),
+        [shape((half_rows + listed, width), BF16), half_f, shape((listed, width), F32)],
+        (enc_slot_node, lists, other_lists, *landed),
         [pltpu.VMEM((NEIGH, cap, width), BF16)],
-        unit * patch_rows,
+        unit * (patch_rows + 2 * listed),
     )
     got = swap(given, "band", 1)
-    half = (kept + got.astype(F32)).astype(BF16)
+    half = (kept + got[:half_rows].astype(F32)).astype(BF16)
+    sums = (kept_listed + got[half_rows:].astype(F32)).astype(BF16)
+    count = band_count // 2
+    while True:
+        count //= 2
+        kept, given = sums[: count * senders_all], sums[count * senders_all :]
+        got_listed = swap(given, "band", 2 * count)
+        if count == 1:
+            break
+        sums = (kept.astype(F32) + got_listed.astype(F32)).astype(BF16)
     mask = 2
     while True:
         got = swap(half, "band", mask)
@@ -381,6 +427,36 @@
             break
         half = crossed(half, got, share_rows, band_count, mask // 2)
         mask *= 2
+
+    half_blocks = shape((blk_count // 2, mcap, width), BF16)
+    kept, given = call(
+        sender_kernel,
+        [half_blocks, half_blocks],
+        (
+            kept,
+            got_listed,
+            listed_nodes,
+            listed_part,
+            enc_node_weights,
+            proc_edge_weights,
+            biases,
+            gains,
+        ),
+        [pltpu.VMEM((blk_count, mcap, width), BF16)],
+        unit * 3 * senders_all,
+    )
+    bit = 1
+    while True:
+        got_rows = swap(given, "blk", bit)
+        senders = jnp.stack([kept, got_rows.reshape(kept.shape)], axis=1)
+        bit *= 2
+        if bit == blk_count:
+            break
+        view = senders.reshape(blk_count // (2 * bit), 2, bit * mcap, width)
+        kept, given = view[:, 0], view[:, 1]
+    arrived_senders = senders.reshape(senders_all, width)
+    receivers = mesh_receiver.reshape(1, medge_rows)
+
     half_mid = call(
         functools.partial(node_kernel, band_count, mask // 2),
         half_bf,
@@ -389,26 +465,6 @@
         unit * 2 * half_rows,
     )
     other_mid = swap(half_mid, "band", 1)
-
-    half_blocks = shape((blk_count // 2, mcap, width), BF16)
-    kept, given = call(
-        functools.partial(sender_kernel, band_count),
-        [half_blocks, half_blocks],
-        (mesh_send_node, half_mid, other_mid, proc_edge_weights),
-        [pltpu.VMEM((patch_rows, width), BF16), pltpu.VMEM((blk_count, mcap, width), BF16)],
-        unit * 2 * senders_all,
-    )
-    mask = 1
-    while True:
-        got = swap(given, "blk", mask)
-        senders = jnp.stack([kept, got.reshape(kept.shape)], axis=1)
-        mask *= 2
-        if mask == blk_count:
-            break
-        view = senders.reshape(blk_count // (2 * mask), 2, mask * mcap, width)
-        kept, given = view[:, 0], view[:, 1]
-    arrived_senders = senders.reshape(senders_all, width)
-    receivers = mesh_receiver.reshape(1, medge_rows)
 
     mesh_part = call(
         functools.partial(target_kernel, band_count),
@@ -453,6 +509,4 @@
     rows = P(("blk", "band"), None)
     flat = P(("blk", "band"))
     in_specs = (rows, rows, flat, flat, rows, P("blk", None), rows, flat, flat, rows) + (P(),) * 7
-    return jax.shard_map(
-        body, mesh=mesh, in_specs=in_specs, out_specs=(rows, rows), check_vma=False
-    )
+    return jax.shard_map(body, mesh=mesh, in_specs=in_specs, out_specs=(rows, rows), check_vma=False)

time: 85.9 us -> 79.4 us (0.924)
  waiting for transfers between devices: 38.6 us -> 23 us
  starting transfers between devices: 25.1 us -> 35.9 us
  local copies, waits for them, and re-layouts: 6.18 us -> 2.85 us
  Pallas kernels: 14.6 us -> 16.2 us
    ppermute x22 -> x25, waiting for transfers between devices: 38.6 us -> 23 us  [swap(): lax.ppermute(rows, axis, [(i, i ^ mask) for i in range(lax.axis_size(axis...]
    ppermute x22 -> x25, starting transfers between devices: 25.1 us -> 35.9 us  [swap(): lax.ppermute(rows, axis, [(i, i ^ mask) for i in range(lax.axis_size(axis...]
    unnamed x41 -> x37, local copies, waits for them, and re-layouts: 6.12 us -> 2.77 us
    pallas_call x11, Pallas kernels: 14.6 us -> 16.2 us  [call(): pl.pallas_call(kernel, out_shape=tuple((pltpu.VMEM(out.shape, out.dtype)...]
  transfers between devices with their start and end apart: 22 -> 25, of which waited for: 15 -> 12; matrix products, arithmetic and copies ran while one was open for 1% -> 1% of each run, Pallas kernels for 7% -> 6%
where the time goes in v4:
time: 79.4 us; the launch traced here: 79.2 us
  starting transfers between devices  35.9 us (45%)
  waiting for transfers between devices  23 us (29%)
  Pallas kernels  16.2 us (20%)
  local copies, waits for them, and re-layouts  2.85 us (4%)
  between operations  0.99 us (1%)
    ppermute x25, starting transfers between devices, swap(): lax.ppermute(rows, axis, [(i, i ^ mask) for i in range(lax.axis_size(axis...  35.9 us
    ppermute x25, waiting for transfers between devices, swap(): lax.ppermute(rows, axis, [(i, i ^ mask) for i in range(lax.axis_size(axis...  23 us
    pallas_call x11, Pallas kernels, call(): pl.pallas_call(kernel, out_shape=tuple((pltpu.VMEM(out.shape, out.dtype)...  16.2 us
    unnamed x37, local copies, waits for them, and re-layouts  2.77 us
  transfers between devices with their start and end apart: 25, of which 12 were waited for; matrix products, arithmetic and copies ran while one was open for 1% of the time, Pallas kernels for 6%

profile of v4, /device:TPU:0, one launch (start us, length us, event | category | flops | bytes accessed | tf_op | source)
XLA Modules:
  0.0 79.2 jit_solution(10044015675065760355)
XLA Ops:
  0.7 2.3 %shard_map.178 = (bf16[64,512]{1,0:T(8,128)(2,1)S(1)}, bf16[64,512]{1,0:T(8,128)(2,1)S(1)}, bf16[64,512]{1,0:T(8,128)(2,1)S(1)}, bf16[64,512]{1,0:T(8,128)(2,1)S...) custom-call(s32[1,512]{1,0:T(1,128)} %node_ref.1, ...), custom_call_target="tpu_custom_call" | custom-call | flops 536870912 | tf_op jit(solution)/shard_map/pallas_call | solution.py:85
  3.0 3.1 %collective-permute-start.1 = (bf16[64,512]{1,0:T(8,128)(2,1)S(1)}, bf16[64,512]{1,0:T(8,128)(2,1)S(1)}, u32[]{:S(2)}, u32[]{:S(2)}) collective-permute-start(bf16[64,512]{1,0:T(8,128)(2,1)S(1)} %get-tuple-element.31), channel_id=1, source_target_pairs={{0,4},{4,0},{8,12},{12,8},{16,20},{20,16},{24,28},{28,24},{1,5},{5... | collective-permute-start | bytes 196616 | tf_op jit(solution)/shard_map/ppermute | solution.py:296
  6.1 1.6 %collective-permute-start.2 = (bf16[64,512]{1,0:T(8,128)(2,1)S(1)}, bf16[64,512]{1,0:T(8,128)(2,1)S(1)}, u32[]{:S(2)}, u32[]{:S(2)}) collective-permute-start(bf16[64,512]{1,0:T(8,128)(2,1)S(1)} %get-tuple-element.32), channel_id=1, source_target_pairs={{0,8},{4,12},{8,0},{12,4},{16,24},{20,28},{24,16},{28,20},{1,9},{5... | collective-permute-start | bytes 196616 | tf_op jit(solution)/shard_map/ppermute | solution.py:296
  9.5 2.6 %collective-permute-start.4 = (bf16[64,512]{1,0:T(8,128)(2,1)S(1)}, bf16[64,512]{1,0:T(8,128)(2,1)S(1)}, u32[]{:S(2)}, u32[]{:S(2)}) collective-permute-start(bf16[64,512]{1,0:T(8,128)(2,1)S(1)} %get-tuple-element.34), channel_id=1, source_target_pairs={{0,16},{4,20},{8,24},{12,28},{16,0},{20,4},{24,8},{28,12},{1,17},{... | collective-permute-start | bytes 196616 | tf_op jit(solution)/shard_map/ppermute | solution.py:296
  12.1 1.6 %collective-permute-start.5 = (bf16[64,512]{1,0:T(8,128)(2,1)S(1)}, bf16[64,512]{1,0:T(8,128)(2,1)S(1)}, u32[]{:S(2)}, u32[]{:S(2)}) collective-permute-start(bf16[64,512]{1,0:T(8,128)(2,1)S(1)} %get-tuple-element.35), channel_id=1, source_target_pairs={{0,20},{4,16},{8,28},{12,24},{16,4},{20,0},{24,12},{28,8},{1,21},{... | collective-permute-start | bytes 196616 | tf_op jit(solution)/shard_map/ppermute | solution.py:296
  13.8 3.3 %collective-permute-start.6 = (bf16[64,512]{1,0:T(8,128)(2,1)S(1)}, bf16[64,512]{1,0:T(8,128)(2,1)S(1)}, u32[]{:S(2)}, u32[]{:S(2)}) collective-permute-start(bf16[64,512]{1,0:T(8,128)(2,1)S(1)} %get-tuple-element.36), channel_id=1, source_target_pairs={{0,24},{4,28},{8,16},{12,20},{16,8},{20,12},{24,0},{28,4},{1,25},{... | collective-permute-start | bytes 196616 | tf_op jit(solution)/shard_map/ppermute | solution.py:296
  19.8 2.2 %shard_map.177.part_ref = f32[1024,512]{1,0:T(8,128)S(1)} custom-call(s32[1,1024]{1,0:T(1,128)S(1)} %bitcast.24, bf16[512,512]{1,0:T(8,128)(2,1)S(1)} %copy-done.7, bf16[1024,512]{1,0:T(8,128)(2,1)S(1)} %copy-done.13, bf16[4,512,512]{2,1,0:T(8,128)(2,1)S(1)} %copy-done.3, f32[5,2,512]{2,1,0:T(2,128)S(1)} %copy-done.8), custom_call_target="tpu_custom_call" | custom-call | flops 1610612736 | tf_op jit(solution)/shard_map/pallas_call | solution.py:85
  22.1 2.0 %collective-permute-done.7.refs_7_ = bf16[64,512]{1,0:T(8,128)(2,1)S(1)} collective-permute-done((bf16[64,512]{1,0:T(8,128)(2,1)S(1)}, bf16[64,512]{1,0:T(8,128)(2,1)S(1)}, u32[]{:S(2)}, u32[]{:S(2)}) %collective-permute-start.7) | collective-permute-done | bytes 65568 | tf_op jit(solution)/shard_map/ppermute | solution.py:296
  24.1 2.4 %shard_map.179 = (bf16[64,512]{1,0:T(8,128)(2,1)S(1)}, bf16[64,512]{1,0:T(8,128)(2,1)S(1)}, bf16[64,512]{1,0:T(8,128)(2,1)S(1)}, bf16[64,512]{1,0:T(8,128)(2,1)S...) custom-call(s32[1,1024]{1,0:T(1,128)S(1)} %bitcast.25, ...), custom_call_target="tpu_custom_call" | custom-call | flops 1610612736 | tf_op jit(solution)/shard_map/pallas_call | solution.py:85
  28.6 2.5 %collective-permute-start.12 = (bf16[64,512]{1,0:T(8,128)(2,1)S(1)}, bf16[64,512]{1,0:T(8,128)(2,1)S(1)}, u32[]{:S(2)}, u32[]{:S(2)}) collective-permute-start(bf16[64,512]{1,0:T(8,128)(2,1)S(1)} %get-tuple-element.43), channel_id=1, source_target_pairs={{0,16},{4,20},{8,24},{12,28},{16,0},{20,4},{24,8},{28,12},{1,17},{... | collective-permute-start | bytes 196616 | tf_op jit(solution)/shard_map/ppermute | solution.py:296
  32.5 2.0 %collective-permute-start.14 = (bf16[64,512]{1,0:T(8,128)(2,1)S(1)}, bf16[64,512]{1,0:T(8,128)(2,1)S(1)}, u32[]{:S(2)}, u32[]{:S(2)}) collective-permute-start(bf16[64,512]{1,0:T(8,128)(2,1)S(1)} %get-tuple-element.45), channel_id=1, source_target_pairs={{0,24},{4,28},{8,16},{12,20},{16,8},{20,12},{24,0},{28,4},{1,25},{... | collective-permute-start | bytes 196616 | tf_op jit(solution)/shard_map/ppermute | solution.py:296
  34.5 1.8 %collective-permute-start.15 = (bf16[64,512]{1,0:T(8,128)(2,1)S(1)}, bf16[64,512]{1,0:T(8,128)(2,1)S(1)}, u32[]{:S(2)}, u32[]{:S(2)}) collective-permute-start(bf16[64,512]{1,0:T(8,128)(2,1)S(1)} %get-tuple-element.46), channel_id=1, source_target_pairs={{0,28},{4,24},{8,20},{12,16},{16,12},{20,8},{24,4},{28,0},{1,29},{... | collective-permute-start | bytes 196616 | tf_op jit(solution)/shard_map/ppermute | solution.py:296
  36.3 1.5 %collective-permute-start.9 = (bf16[64,512]{1,0:T(8,128)(2,1)S(1)}, bf16[64,512]{1,0:T(8,128)(2,1)S(1)}, u32[]{:S(2)}, u32[]{:S(2)}) collective-permute-start(bf16[64,512]{1,0:T(8,128)(2,1)S(1)} %get-tuple-element.40), channel_id=1, source_target_pairs={{0,4},{4,0},{8,12},{12,8},{16,20},{20,16},{24,28},{28,24},{1,5},{5... | collective-permute-start | bytes 196616 | tf_op jit(solution)/shard_map/ppermute | solution.py:296
  37.8 4.7 %collective-permute-done.13.refs_5_ = bf16[64,512]{1,0:T(8,128)(2,1)S(1)} collective-permute-done((bf16[64,512]{1,0:T(8,128)(2,1)S(1)}, bf16[64,512]{1,0:T(8,128)(2,1)S(1)}, u32[]{:S(2)}, u32[]{:S(2)}) %collective-permute-start.13) | collective-permute-done | bytes 65568 | tf_op jit(solution)/shard_map/ppermute | solution.py:296
  43.5 1.8 %collective-permute-done.16 = bf16[448,512]{1,0:T(8,128)(2,1)S(1)} collective-permute-done((bf16[448,512]{1,0:T(8,128)(2,1)S(1)}, bf16[448,512]{1,0:T(8,128)(2,1)S(1)}, u32[]{:S(2)}, u32[]{:S(2)}) %collective-permute-start.16) | collective-permute-done | bytes 458784 | tf_op jit(solution)/shard_map/ppermute | solution.py:296
  47.2 2.5 %collective-permute-done.19.got_ref = bf16[64,512]{1,0:T(8,128)(2,1)S(1)} collective-permute-done((bf16[64,512]{1,0:T(8,128)(2,1)S(1)}, bf16[64,512]{1,0:T(8,128)(2,1)S(1)}, u32[]{:S(2)}, u32[]{:S(2)}) %collective-permute-start.19) | collective-permute-done | bytes 65568 | tf_op jit(solution)/shard_map/ppermute | solution.py:296
  52.2 2.2 %collective-permute-done.20 = bf16[4,8,512]{2,1,0:T(8,128)(2,1)S(1)} collective-permute-done((bf16[4,8,512]{2,1,0:T(8,128)(2,1)S(1)}, bf16[4,8,512]{2,1,0:T(8,128)(2,1)S(1)}, u32[]{:S(2)}, u32[]{:S(2)}) %collective-permute-start.20) | collective-permute-done | bytes 32800 | tf_op jit(solution)/shard_map/ppermute | solution.py:296
  54.4 2.8 %collective-permute-start.21 = (bf16[2,16,512]{2,1,0:T(8,128)(2,1)S(1)}, bf16[2,16,512]{2,1,0:T(8,128)(2,1)S(1)}, u32[]{:S(2)}, u32[]{:S(2)}) collective-permute-start(bf16[2,16,512]{2,1,0:T(8,128)(2,1)S(1)} %get-tuple-element.63), channel_id=1, source_target_pairs={{0,8},{4,12},{8,0},{12,4},{16,24},{20,28},{24,16},{28,20},{1,9},{5... | collective-permute-start | bytes 98312 | tf_op jit(solution)/shard_map/ppermute | solution.py:296
  57.2 1.9 %collective-permute-done.21 = bf16[2,16,512]{2,1,0:T(8,128)(2,1)S(1)} collective-permute-done((bf16[2,16,512]{2,1,0:T(8,128)(2,1)S(1)}, bf16[2,16,512]{2,1,0:T(8,128)(2,1)S(1)}, u32[]{:S(2)}, u32[]{:S(2)}) %collective-permute-start.21) | collective-permute-done | bytes 32800 | tf_op jit(solution)/shard_map/ppermute | solution.py:296
  60.9 2.9 %collective-permute-start.22 = (bf16[1,32,512]{2,1,0:T(8,128)(2,1)S(1)}, bf16[1,32,512]{2,1,0:T(8,128)(2,1)S(1)}, u32[]{:S(2)}, u32[]{:S(2)}) collective-permute-start(bf16[1,32,512]{2,1,0:T(8,128)(2,1)S(1)} %get-tuple-element.61), channel_id=1, source_target_pairs={{0,16},{4,20},{8,24},{12,28},{16,0},{20,4},{24,8},{28,12},{1,17},{... | collective-permute-start | bytes 98312 | tf_op jit(solution)/shard_map/ppermute | solution.py:296
  63.8 2.0 %collective-permute-done.22 = bf16[1,32,512]{2,1,0:T(8,128)(2,1)S(1)} collective-permute-done((bf16[1,32,512]{2,1,0:T(8,128)(2,1)S(1)}, bf16[1,32,512]{2,1,0:T(8,128)(2,1)S(1)}, u32[]{:S(2)}, u32[]{:S(2)}) %collective-permute-start.22) | collective-permute-done | bytes 32800 | tf_op jit(solution)/shard_map/ppermute | solution.py:296
  67.2 2.5 %shard_map.185 = (bf16[320,512]{1,0:T(8,128)(2,1)S(1)}, f32[320,512]{1,0:T(8,128)S(1)}) custom-call(s32[1,1024]{1,0:T(1,128)S(1)} %bitcast.26, s32[1,1024]{1,0:T(1,128)S(1)} %bitcast.23, f32[1024,512]{1,0:T(8,128)S(1)} %shard_map.183.part_ref, bf16[64,512]{1,0:T(8,128)(2,1)S(1)} %bitcast.20, bf16[4,512,512]{2,1,0:T(8,128)(2,1)S(1)} %copy-done, ...), custom_call_target="tpu_custom_call" | custom-call | flops 1610612736 | tf_op jit(solution)/shard_map/pallas_call | solution.py:85
  69.7 1.6 %collective-permute-done.23 = bf16[320,512]{1,0:T(8,128)(2,1)S(1)} collective-permute-done((bf16[320,512]{1,0:T(8,128)(2,1)S(1)}, bf16[320,512]{1,0:T(8,128)(2,1)S(1)}, u32[]{:S(2)}, u32[]{:S(2)}) %collective-permute-start.23) | collective-permute-done | bytes 327712 | tf_op jit(solution)/shard_map/ppermute | solution.py:296
  74.6 3.2 %collective-permute-done.24.got_ref = bf16[160,512]{1,0:T(8,128)(2,1)S(1)} collective-permute-done((bf16[160,512]{1,0:T(8,128)(2,1)S(1)}, bf16[160,512]{1,0:T(8,128)(2,1)S(1)}, u32[]{:S(2)}, u32[]{:S(2)}) %collective-permute-start.24) | collective-permute-done | bytes 163872 | tf_op jit(solution)/shard_map/ppermute | solution.py:296
  (86 shorter events, 21.4 us)
Async XLA Ops:
  3.0 10.7 %collective-permute-start.1 = (bf16[64,512]{1,0:T(8,128)(2,1)S(1)}, bf16[64,512]{1,0:T(8,128)(2,1)S(1)}, u32[]{:S(2)}, u32[]{:S(2)}) collective-permute-start(bf16[64,512]{1,0:T(8,128)(2,1)S(1)} %get-tuple-element.31), channel_id=1, source_target_pairs={{0,4},{4,0},{8,12},{12,8},{16,20},{20,16},{24,28},{28,24},{1,5},{5... | collective-permute-start | bytes 196616 | tf_op jit(solution)/shard_map/ppermute | solution.py:296
  6.1 11.0 %collective-permute-start.2 = (bf16[64,512]{1,0:T(8,128)(2,1)S(1)}, bf16[64,512]{1,0:T(8,128)(2,1)S(1)}, u32[]{:S(2)}, u32[]{:S(2)}) collective-permute-start(bf16[64,512]{1,0:T(8,128)(2,1)S(1)} %get-tuple-element.32), channel_id=1, source_target_pairs={{0,8},{4,12},{8,0},{12,4},{16,24},{20,28},{24,16},{28,20},{1,9},{5... | collective-permute-start | bytes 196616 | tf_op jit(solution)/shard_map/ppermute | solution.py:296
  7.7 4.5 %collective-permute-start = (s32[1,64]{1,0:T(1,128)S(1)}, s32[1,64]{1,0:T(1,128)S(1)}, u32[]{:S(2)}, u32[]{:S(2)}) collective-permute-start(s32[1,64]{1,0:T(1,128)S(1)} %copy-done.12), channel_id=1, source_target_pairs={{0,2},{1,3},{2,0},{3,1},{4,6},{5,7},{6,4},{7,5},{8,10},{9,11},{10,... | collective-permute-start | bytes 776 | tf_op jit(solution)/shard_map/ppermute | solution.py:296
  9.1 12.8 %collective-permute-start.3 = (bf16[64,512]{1,0:T(8,128)(2,1)S(1)}, bf16[64,512]{1,0:T(8,128)(2,1)S(1)}, u32[]{:S(2)}, u32[]{:S(2)}) collective-permute-start(bf16[64,512]{1,0:T(8,128)(2,1)S(1)} %get-tuple-element.33), channel_id=1, source_target_pairs={{0,12},{4,8},{8,4},{12,0},{16,28},{20,24},{24,20},{28,16},{1,13},{... | collective-permute-start | bytes 196616 | tf_op jit(solution)/shard_map/ppermute | solution.py:296
  9.5 12.4 %collective-permute-start.4 = (bf16[64,512]{1,0:T(8,128)(2,1)S(1)}, bf16[64,512]{1,0:T(8,128)(2,1)S(1)}, u32[]{:S(2)}, u32[]{:S(2)}) collective-permute-start(bf16[64,512]{1,0:T(8,128)(2,1)S(1)} %get-tuple-element.34), channel_id=1, source_target_pairs={{0,16},{4,20},{8,24},{12,28},{16,0},{20,4},{24,8},{28,12},{1,17},{... | collective-permute-start | bytes 196616 | tf_op jit(solution)/shard_map/ppermute | solution.py:296
  12.1 10.0 %collective-permute-start.5 = (bf16[64,512]{1,0:T(8,128)(2,1)S(1)}, bf16[64,512]{1,0:T(8,128)(2,1)S(1)}, u32[]{:S(2)}, u32[]{:S(2)}) collective-permute-start(bf16[64,512]{1,0:T(8,128)(2,1)S(1)} %get-tuple-element.35), channel_id=1, source_target_pairs={{0,20},{4,16},{8,28},{12,24},{16,4},{20,0},{24,12},{28,8},{1,21},{... | collective-permute-start | bytes 196616 | tf_op jit(solution)/shard_map/ppermute | solution.py:296
  13.8 8.3 %collective-permute-start.6 = (bf16[64,512]{1,0:T(8,128)(2,1)S(1)}, bf16[64,512]{1,0:T(8,128)(2,1)S(1)}, u32[]{:S(2)}, u32[]{:S(2)}) collective-permute-start(bf16[64,512]{1,0:T(8,128)(2,1)S(1)} %get-tuple-element.36), channel_id=1, source_target_pairs={{0,24},{4,28},{8,16},{12,20},{16,8},{20,12},{24,0},{28,4},{1,25},{... | collective-permute-start | bytes 196616 | tf_op jit(solution)/shard_map/ppermute | solution.py:296
  17.0 7.1 %collective-permute-start.7 = (bf16[64,512]{1,0:T(8,128)(2,1)S(1)}, bf16[64,512]{1,0:T(8,128)(2,1)S(1)}, u32[]{:S(2)}, u32[]{:S(2)}) collective-permute-start(bf16[64,512]{1,0:T(8,128)(2,1)S(1)} %get-tuple-element.37), channel_id=1, source_target_pairs={{0,28},{4,24},{8,20},{12,16},{16,12},{20,8},{24,4},{28,0},{1,29},{... | collective-permute-start | bytes 196616 | tf_op jit(solution)/shard_map/ppermute | solution.py:296
  26.6 7.9 %collective-permute-start.10 = (bf16[64,512]{1,0:T(8,128)(2,1)S(1)}, bf16[64,512]{1,0:T(8,128)(2,1)S(1)}, u32[]{:S(2)}, u32[]{:S(2)}) collective-permute-start(bf16[64,512]{1,0:T(8,128)(2,1)S(1)} %get-tuple-element.41), channel_id=1, source_target_pairs={{0,8},{4,12},{8,0},{12,4},{16,24},{20,28},{24,16},{28,20},{1,9},{5... | collective-permute-start | bytes 196616 | tf_op jit(solution)/shard_map/ppermute | solution.py:296
  28.0 8.3 %collective-permute-start.11 = (bf16[64,512]{1,0:T(8,128)(2,1)S(1)}, bf16[64,512]{1,0:T(8,128)(2,1)S(1)}, u32[]{:S(2)}, u32[]{:S(2)}) collective-permute-start(bf16[64,512]{1,0:T(8,128)(2,1)S(1)} %get-tuple-element.42), channel_id=1, source_target_pairs={{0,12},{4,8},{8,4},{12,0},{16,28},{20,24},{24,20},{28,16},{1,13},{... | collective-permute-start | bytes 196616 | tf_op jit(solution)/shard_map/ppermute | solution.py:296
  28.6 3.9 %collective-permute-start.8 = (s32[2,64]{1,0:T(2,128)S(1)}, s32[2,64]{1,0:T(2,128)S(1)}, u32[]{:S(2)}, u32[]{:S(2)}) collective-permute-start(s32[2,64]{1,0:T(2,128)S(1)} %get-tuple-element.38.own_ref), channel_id=1, source_target_pairs={{0,1},{1,0},{2,3},{3,2},{4,5},{5,4},{6,7},{7,6},{8,9},{9,8},{10,11... | collective-permute-start | bytes 1544 | tf_op jit(solution)/shard_map/ppermute | solution.py:296
  28.6 9.2 %collective-permute-start.12 = (bf16[64,512]{1,0:T(8,128)(2,1)S(1)}, bf16[64,512]{1,0:T(8,128)(2,1)S(1)}, u32[]{:S(2)}, u32[]{:S(2)}) collective-permute-start(bf16[64,512]{1,0:T(8,128)(2,1)S(1)} %get-tuple-element.43), channel_id=1, source_target_pairs={{0,16},{4,20},{8,24},{12,28},{16,0},{20,4},{24,8},{28,12},{1,17},{... | collective-permute-start | bytes 196616 | tf_op jit(solution)/shard_map/ppermute | solution.py:296
  31.1 11.4 %collective-permute-start.13 = (bf16[64,512]{1,0:T(8,128)(2,1)S(1)}, bf16[64,512]{1,0:T(8,128)(2,1)S(1)}, u32[]{:S(2)}, u32[]{:S(2)}) collective-permute-start(bf16[64,512]{1,0:T(8,128)(2,1)S(1)} %get-tuple-element.44), channel_id=1, source_target_pairs={{0,20},{4,16},{8,28},{12,24},{16,4},{20,0},{24,12},{28,8},{1,21},{... | collective-permute-start | bytes 196616 | tf_op jit(solution)/shard_map/ppermute | solution.py:296
  32.5 10.0 %collective-permute-start.14 = (bf16[64,512]{1,0:T(8,128)(2,1)S(1)}, bf16[64,512]{1,0:T(8,128)(2,1)S(1)}, u32[]{:S(2)}, u32[]{:S(2)}) collective-permute-start(bf16[64,512]{1,0:T(8,128)(2,1)S(1)} %get-tuple-element.45), channel_id=1, source_target_pairs={{0,24},{4,28},{8,16},{12,20},{16,8},{20,12},{24,0},{28,4},{1,25},{... | collective-permute-start | bytes 196616 | tf_op jit(solution)/shard_map/ppermute | solution.py:296
  34.5 8.0 %collective-permute-start.15 = (bf16[64,512]{1,0:T(8,128)(2,1)S(1)}, bf16[64,512]{1,0:T(8,128)(2,1)S(1)}, u32[]{:S(2)}, u32[]{:S(2)}) collective-permute-start(bf16[64,512]{1,0:T(8,128)(2,1)S(1)} %get-tuple-element.46), channel_id=1, source_target_pairs={{0,28},{4,24},{8,20},{12,16},{16,12},{20,8},{24,4},{28,0},{1,29},{... | collective-permute-start | bytes 196616 | tf_op jit(solution)/shard_map/ppermute | solution.py:296
  36.3 6.4 %collective-permute-start.9 = (bf16[64,512]{1,0:T(8,128)(2,1)S(1)}, bf16[64,512]{1,0:T(8,128)(2,1)S(1)}, u32[]{:S(2)}, u32[]{:S(2)}) collective-permute-start(bf16[64,512]{1,0:T(8,128)(2,1)S(1)} %get-tuple-element.40), channel_id=1, source_target_pairs={{0,4},{4,0},{8,12},{12,8},{16,20},{20,16},{24,28},{28,24},{1,5},{5... | collective-permute-start | bytes 196616 | tf_op jit(solution)/shard_map/ppermute | solution.py:296
  43.4 1.9 %collective-permute-start.16 = (bf16[448,512]{1,0:T(8,128)(2,1)S(1)}, bf16[448,512]{1,0:T(8,128)(2,1)S(1)}, u32[]{:S(2)}, u32[]{:S(2)}) collective-permute-start(bf16[448,512]{1,0:T(8,128)(2,1)S(1)} %get-tuple-element.48), channel_id=1, source_target_pairs={{0,1},{1,0},{2,3},{3,2},{4,5},{5,4},{6,7},{7,6},{8,9},{9,8},{10,11... | collective-permute-start | bytes 1376264 | tf_op jit(solution)/shard_map/ppermute | solution.py:296
  45.3 4.3 %collective-permute-start.19 = (bf16[64,512]{1,0:T(8,128)(2,1)S(1)}, bf16[64,512]{1,0:T(8,128)(2,1)S(1)}, u32[]{:S(2)}, u32[]{:S(2)}) collective-permute-start(bf16[64,512]{1,0:T(8,128)(2,1)S(1)} %get-tuple-element.58), channel_id=1, source_target_pairs={{0,2},{1,3},{2,0},{3,1},{4,6},{5,7},{6,4},{7,5},{8,10},{9,11},{10,... | collective-permute-start | bytes 196616 | tf_op jit(solution)/shard_map/ppermute | solution.py:296
  50.4 4.0 %collective-permute-start.20 = (bf16[4,8,512]{2,1,0:T(8,128)(2,1)S(1)}, bf16[4,8,512]{2,1,0:T(8,128)(2,1)S(1)}, u32[]{:S(2)}, u32[]{:S(2)}) collective-permute-start(bf16[4,8,512]{2,1,0:T(8,128)(2,1)S(1)} %get-tuple-element.55), channel_id=1, source_target_pairs={{0,4},{4,0},{8,12},{12,8},{16,20},{20,16},{24,28},{28,24},{1,5},{5... | collective-permute-start | bytes 98312 | tf_op jit(solution)/shard_map/ppermute | solution.py:296
  51.6 8.4 %collective-permute-start.17 = (bf16[320,512]{1,0:T(8,128)(2,1)S(1)}, bf16[320,512]{1,0:T(8,128)(2,1)S(1)}, u32[]{:S(2)}, u32[]{:S(2)}) collective-permute-start(bf16[320,512]{1,0:T(8,128)(2,1)S(1)} %add_convert_fusion.half_ref), channel_id=1, source_target_pairs={{0,2},{1,3},{2,0},{3,1},{4,6},{5,7},{6,4},{7,5},{8,10},{9,11},{10,... | collective-permute-start | bytes 983048 | tf_op jit(solution)/shard_map/ppermute | solution.py:296
  54.4 4.7 %collective-permute-start.21 = (bf16[2,16,512]{2,1,0:T(8,128)(2,1)S(1)}, bf16[2,16,512]{2,1,0:T(8,128)(2,1)S(1)}, u32[]{:S(2)}, u32[]{:S(2)}) collective-permute-start(bf16[2,16,512]{2,1,0:T(8,128)(2,1)S(1)} %get-tuple-element.63), channel_id=1, source_target_pairs={{0,8},{4,12},{8,0},{12,4},{16,24},{20,28},{24,16},{28,20},{1,9},{5... | collective-permute-start | bytes 98312 | tf_op jit(solution)/shard_map/ppermute | solution.py:296
  60.8 5.0 %collective-permute-start.18 = (bf16[320,512]{1,0:T(8,128)(2,1)S(1)}, bf16[320,512]{1,0:T(8,128)(2,1)S(1)}, u32[]{:S(2)}, u32[]{:S(2)}) collective-permute-start(bf16[320,512]{1,0:T(8,128)(2,1)S(1)} %shard_map.182.own_ref.half_ref), channel_id=1, source_target_pairs={{0,1},{1,0},{2,3},{3,2},{4,5},{5,4},{6,7},{7,6},{8,9},{9,8},{10,11... | collective-permute-start | bytes 983048 | tf_op jit(solution)/shard_map/ppermute | solution.py:296
  60.9 4.9 %collective-permute-start.22 = (bf16[1,32,512]{2,1,0:T(8,128)(2,1)S(1)}, bf16[1,32,512]{2,1,0:T(8,128)(2,1)S(1)}, u32[]{:S(2)}, u32[]{:S(2)}) collective-permute-start(bf16[1,32,512]{2,1,0:T(8,128)(2,1)S(1)} %get-tuple-element.61), channel_id=1, source_target_pairs={{0,16},{4,20},{8,24},{12,28},{16,0},{20,4},{24,8},{28,12},{1,17},{... | collective-permute-start | bytes 98312 | tf_op jit(solution)/shard_map/ppermute | solution.py:296
  71.5 6.3 %collective-permute-start.24 = (bf16[160,512]{1,0:T(8,128)(2,1)S(1)}, bf16[160,512]{1,0:T(8,128)(2,1)S(1)}, u32[]{:S(2)}, u32[]{:S(2)}) collective-permute-start(bf16[160,512]{1,0:T(8,128)(2,1)S(1)} %slice.57), channel_id=1, source_target_pairs={{0,2},{1,3},{2,0},{3,1},{4,6},{5,7},{6,4},{7,5},{8,10},{9,11},{10,... | collective-permute-start | bytes 491528 | tf_op jit(solution)/shard_map/ppermute | solution.py:296
  (18 other events, 210.8 us)

commit v5 on v4

--- a/solution.py
+++ b/solution.py
@@ -128,17 +128,24 @@
         outs[mask][...] = held[window_of(mask, exact)]
 
 
-def edge_kernel(sender_ref, grid_ref, edges_ref, weights_ref, biases_ref, part_ref):
+def edge_kernel(sender_ref, grid_ref, weights_ref, biases_ref, edges_hbm, part_ref, edges, sems):
+    tiles = range(0, edges.shape[0], TILE)
+    copies = [
+        pltpu.make_async_copy(
+            edges_hbm.at[pl.ds(at, TILE), :], edges.at[pl.ds(at, TILE), :], sems.at[at // TILE]
+        )
+        for at in tiles
+    ]
+    for copy in copies:
+        copy.start()
     names = lanes(grid_ref.shape[0])
     senders = column(sender_ref[...])
-    for at in range(0, edges_ref.shape[0], TILE):
+    for at, copy in zip(tiles, copies):
         picks = hot_columns(senders[at : at + TILE], names)
         nodes = project(picks, grid_ref[...]).astype(BF16)
-        part_ref[at : at + TILE, :] = (
-            project(edges_ref[at : at + TILE, :], weights_ref[0])
-            + project(nodes, weights_ref[1])
-            + biases_ref[1, 0:1, :]
-        )
+        part = project(nodes, weights_ref[1]) + biases_ref[1, 0:1, :]
+        copy.wait()
+        part_ref[at : at + TILE, :] = part + project(edges[at : at + TILE, :], weights_ref[0])
 
 
 def grid_kernel(grid_ref, weights_ref, biases_ref, gains_ref, out_ref):
@@ -183,19 +190,26 @@
     )
 
 
-def land_kernel(exact, band_count, node_ref, own_ref, other_ref, *refs):
-    pieces, (given_ref, kept_ref, listed_ref, held) = refs[:NEIGH], refs[NEIGH:]
+def land_kernel(exact, band_count, half, node_ref, lists_ref, *refs):
+    pieces, (given_ref, held) = refs[:NEIGH], refs[NEIGH:]
     for mask in range(NEIGH):
         held[window_of(mask, exact)] = pieces[mask][...]
-    half = kept_ref.shape[0]
     core = lax.rem(lax.axis_index("band"), 2)
     names = share_names(sublanes(2 * half), 2 * half // band_count, band_count, 1 - core)
     row = node_ref[...]
     landed = held[...].reshape(-1, held.shape[2])
     given_ref[:half, :] = project(hot_rows(row, names[:half]), landed).astype(BF16)
-    given_ref[half:, :] = project(hot_lists(other_ref, row), landed).astype(BF16)
-    kept_ref[...] = project(hot_rows(row, names[half:]), landed)
-    listed_ref[...] = project(hot_lists(own_ref, row), landed)
+    given_ref[half:, :] = project(hot_lists(lists_ref, row), landed).astype(BF16)
+
+
+def keep_kernel(band_count, node_ref, lists_ref, held, kept_ref, listed_ref):
+    half = kept_ref.shape[0]
+    core = lax.rem(lax.axis_index("band"), 2)
+    names = share_names(sublanes(2 * half), 2 * half // band_count, band_count, core)
+    row = node_ref[...]
+    landed = held[...].reshape(-1, held.shape[2])
+    kept_ref[...] = project(hot_rows(row, names[:half]), landed)
+    listed_ref[...] = project(hot_lists(lists_ref, row), landed)
 
 
 def own_share(place):
@@ -268,7 +282,7 @@
 
 
 def process_kernel(
-    band_count, mcap, sender_ref, receiver_ref, part_ref, keys_ref, weights_ref, biases_ref, gains_ref, given_ref, kept_ref, sent
+    band_count, mcap, sender_ref, receiver_ref, part_ref, keys_ref, weights_ref, biases_ref, gains_ref, given_ref, sent
 ):
     senders = column(sender_ref[...] ^ (lax.axis_index("blk") * mcap))
     names = lanes(keys_ref.shape[0])
@@ -280,13 +294,20 @@
     core = lax.rem(lax.axis_index("band"), 2)
     places = share_names(sublanes(2 * half), 2 * half // band_count, band_count, 1 - core)
     given_ref[...] = project(hot_rows(receiver_ref[...], places[:half]), sent[...]).astype(BF16)
-    kept_ref[...] = project(hot_rows(receiver_ref[...], places[half:]), sent[...])
-
-
-def last_kernel(kept_ref, got_ref, half_ref, weights_ref, biases_ref, gains_ref, out_ref):
+
+
+def own_kernel(band_count, receiver_ref, sent_ref, half_ref, weights_ref, biases_ref, kept_ref, part_ref):
+    half = kept_ref.shape[0]
+    core = lax.rem(lax.axis_index("band"), 2)
+    places = share_names(sublanes(2 * half), 2 * half // band_count, band_count, core)
+    kept_ref[...] = project(hot_rows(receiver_ref[...], places[:half]), sent_ref[...])
+    part_ref[...] = project(half_ref[: part_ref.shape[0], :], weights_ref[0]) + biases_ref[4, 0:1, :]
+
+
+def last_kernel(kept_ref, got_ref, half_ref, part_ref, weights_ref, biases_ref, gains_ref, out_ref):
     own = half_ref[: out_ref.shape[0], :]
     total = (kept_ref[...] + got_ref[...].astype(F32)).astype(BF16)
-    first = project(own, weights_ref[0]) + project(total, weights_ref[1]) + biases_ref[4, 0:1, :]
+    first = part_ref[...] + project(total, weights_ref[1])
     out_ref[...] = (
         own.astype(F32) + tail(first, weights_ref[2], biases_ref, gains_ref, 4)
     ).astype(BF16)
@@ -363,9 +384,10 @@
     edge_part = call(
         edge_kernel,
         shape((edge_rows, width), F32),
-        (enc_sender.reshape(1, edge_rows), grid_nodes, enc_edges, enc_edge_weights, biases),
-        (),
+        (enc_sender.reshape(1, edge_rows), grid_nodes, enc_edge_weights, biases, enc_edges),
+        [pltpu.VMEM((edge_rows, width), BF16), pltpu.SemaphoreType.DMA((edge_rows // TILE,))],
         unit * 3 * edge_rows,
+        (4,),
     )
     near, mask = mesh_send_node, 2
     while True:
@@ -402,12 +424,19 @@
         unit * (half_rows + medge_rows + 2 * senders_all),
     )
 
-    given, kept, kept_listed = call(
-        functools.partial(land_kernel, exact, band_count),
-        [shape((half_rows + listed, width), BF16), half_f, shape((listed, width), F32)],
-        (enc_slot_node, lists, other_lists, *landed),
-        [pltpu.VMEM((NEIGH, cap, width), BF16)],
-        unit * (patch_rows + 2 * listed),
+    given, held = call(
+        functools.partial(land_kernel, exact, band_count, half_rows),
+        [shape((half_rows + listed, width), BF16), shape((NEIGH, cap, width), BF16)],
+        (enc_slot_node, other_lists, *landed),
+        (),
+        unit * (half_rows + listed),
+    )
+    kept, kept_listed = call(
+        functools.partial(keep_kernel, band_count),
+        [half_f, shape((listed, width), F32)],
+        (enc_slot_node, lists, held),
+        (),
+        unit * (half_rows + listed),
     )
     got = swap(given, "band", 1)
     half = (kept + got[:half_rows].astype(F32)).astype(BF16)
@@ -473,9 +502,9 @@
         [pltpu.VMEM((patch_rows, width), BF16)],
         unit * (patch_rows + medge_rows),
     )
-    given, kept = call(
+    given, sent = call(
         functools.partial(process_kernel, band_count, mcap),
-        [half_bf, half_f],
+        [half_bf, shape((medge_rows, width), BF16)],
         (
             mesh_sender.reshape(1, medge_rows),
             receivers,
@@ -485,8 +514,15 @@
             biases,
             gains,
         ),
-        [pltpu.VMEM((medge_rows, width), BF16)],
-        unit * 3 * medge_rows,
+        (),
+        unit * 2 * medge_rows,
+    )
+    kept, own_part = call(
+        functools.partial(own_kernel, band_count),
+        [half_f, shape((share_rows, width), F32)],
+        (receivers, sent, half_mid, proc_node_weights, biases),
+        (),
+        unit * medge_rows,
     )
     got = swap(given, "band", 1)
     count = band_count // 2
@@ -498,7 +534,7 @@
     mesh_out = call(
         last_kernel,
         shape((share_rows, width), BF16),
-        (kept, got, half_mid, proc_node_weights, biases, gains),
+        (kept, got, half_mid, own_part, proc_node_weights, biases, gains),
         (),
         unit * 3 * share_rows,
     )

time: 79.4 us -> 78.7 us (level)
  local copies, waits for them, and re-layouts: 2.85 us -> 1.63 us
  Pallas kernels: 16.2 us -> 17.3 us
    unnamed x37 -> x35, local copies, waits for them, and re-layouts: 2.77 us -> 1.56 us
    pallas_call x11 -> x13, Pallas kernels: 16.2 us -> 17.3 us  [call(): pl.pallas_call(kernel, out_shape=tuple((pltpu.VMEM(out.shape, out.dtype)...]
  transfers between devices with their start and end apart: 25 -> 25, of which waited for: 12 -> 12; matrix products, arithmetic and copies ran while one was open for 1% -> 1% of each run, Pallas kernels for 6% -> 8%
where the time goes in v5:
time: 78.7 us; the launch traced here: 78.6 us
  starting transfers between devices  35.9 us (46%)
  waiting for transfers between devices  22.5 us (29%)
  Pallas kernels  17.3 us (22%)
  local copies, waits for them, and re-layouts  1.63 us (2%)
  between operations  1.03 us (1%)
    ppermute x25, starting transfers between devices, swap(): lax.ppermute(rows, axis, [(i, i ^ mask) for i in range(lax.axis_size(axis...  35.9 us
    ppermute x25, waiting for transfers between devices, swap(): lax.ppermute(rows, axis, [(i, i ^ mask) for i in range(lax.axis_size(axis...  22.5 us
    pallas_call x13, Pallas kernels, call(): pl.pallas_call(kernel, out_shape=tuple((pltpu.VMEM(out.shape, out.dtype)...  17.3 us
  transfers between devices with their start and end apart: 25, of which 12 were waited for; matrix products, arithmetic and copies ran while one was open for 1% of the time, Pallas kernels for 8%

profile of v5, /device:TPU:0, one launch (start us, length us, event | category | flops | bytes accessed | tf_op | source)
XLA Modules:
  0.0 78.6 jit_solution(2671315828001113446)
XLA Ops:
  0.7 2.3 %shard_map.178 = (bf16[64,512]{1,0:T(8,128)(2,1)S(1)}, bf16[64,512]{1,0:T(8,128)(2,1)S(1)}, bf16[64,512]{1,0:T(8,128)(2,1)S(1)}, bf16[64,512]{1,0:T(8,128)(2,1)S...) custom-call(s32[1,512]{1,0:T(1,128)} %node_ref.3, ...), custom_call_target="tpu_custom_call" | custom-call | flops 536870912 | tf_op jit(solution)/shard_map/pallas_call | solution.py:85
  3.0 3.1 %collective-permute-start.1 = (bf16[64,512]{1,0:T(8,128)(2,1)S(1)}, bf16[64,512]{1,0:T(8,128)(2,1)S(1)}, u32[]{:S(2)}, u32[]{:S(2)}) collective-permute-start(bf16[64,512]{1,0:T(8,128)(2,1)S(1)} %get-tuple-element.34), channel_id=1, source_target_pairs={{0,4},{4,0},{8,12},{12,8},{16,20},{20,16},{24,28},{28,24},{1,5},{5... | collective-permute-start | bytes 196616 | tf_op jit(solution)/shard_map/ppermute | solution.py:317
  6.1 1.6 %collective-permute-start.2 = (bf16[64,512]{1,0:T(8,128)(2,1)S(1)}, bf16[64,512]{1,0:T(8,128)(2,1)S(1)}, u32[]{:S(2)}, u32[]{:S(2)}) collective-permute-start(bf16[64,512]{1,0:T(8,128)(2,1)S(1)} %get-tuple-element.35), channel_id=1, source_target_pairs={{0,8},{4,12},{8,0},{12,4},{16,24},{20,28},{24,16},{28,20},{1,9},{5... | collective-permute-start | bytes 196616 | tf_op jit(solution)/shard_map/ppermute | solution.py:317
  7.7 1.5 %collective-permute-start = (s32[1,64]{1,0:T(1,128)S(1)}, s32[1,64]{1,0:T(1,128)S(1)}, u32[]{:S(2)}, u32[]{:S(2)}) collective-permute-start(s32[1,64]{1,0:T(1,128)S(1)} %copy-done.13), channel_id=1, source_target_pairs={{0,2},{1,3},{2,0},{3,1},{4,6},{5,7},{6,4},{7,5},{8,10},{9,11},{10,... | collective-permute-start | bytes 776 | tf_op jit(solution)/shard_map/ppermute | solution.py:317
  9.5 2.6 %collective-permute-start.4 = (bf16[64,512]{1,0:T(8,128)(2,1)S(1)}, bf16[64,512]{1,0:T(8,128)(2,1)S(1)}, u32[]{:S(2)}, u32[]{:S(2)}) collective-permute-start(bf16[64,512]{1,0:T(8,128)(2,1)S(1)} %get-tuple-element.37), channel_id=1, source_target_pairs={{0,16},{4,20},{8,24},{12,28},{16,0},{20,4},{24,8},{28,12},{1,17},{... | collective-permute-start | bytes 196616 | tf_op jit(solution)/shard_map/ppermute | solution.py:317
  12.1 1.6 %collective-permute-start.5 = (bf16[64,512]{1,0:T(8,128)(2,1)S(1)}, bf16[64,512]{1,0:T(8,128)(2,1)S(1)}, u32[]{:S(2)}, u32[]{:S(2)}) collective-permute-start(bf16[64,512]{1,0:T(8,128)(2,1)S(1)} %get-tuple-element.38), channel_id=1, source_target_pairs={{0,20},{4,16},{8,28},{12,24},{16,4},{20,0},{24,12},{28,8},{1,21},{... | collective-permute-start | bytes 196616 | tf_op jit(solution)/shard_map/ppermute | solution.py:317
  13.8 3.3 %collective-permute-start.6 = (bf16[64,512]{1,0:T(8,128)(2,1)S(1)}, bf16[64,512]{1,0:T(8,128)(2,1)S(1)}, u32[]{:S(2)}, u32[]{:S(2)}) collective-permute-start(bf16[64,512]{1,0:T(8,128)(2,1)S(1)} %get-tuple-element.39), channel_id=1, source_target_pairs={{0,24},{4,28},{8,16},{12,20},{16,8},{20,12},{24,0},{28,4},{1,25},{... | collective-permute-start | bytes 196616 | tf_op jit(solution)/shard_map/ppermute | solution.py:317
  17.0 1.5 %collective-permute-start.7 = (bf16[64,512]{1,0:T(8,128)(2,1)S(1)}, bf16[64,512]{1,0:T(8,128)(2,1)S(1)}, u32[]{:S(2)}, u32[]{:S(2)}) collective-permute-start(bf16[64,512]{1,0:T(8,128)(2,1)S(1)} %get-tuple-element.40), channel_id=1, source_target_pairs={{0,28},{4,24},{8,20},{12,16},{16,12},{20,8},{24,4},{28,0},{1,29},{... | collective-permute-start | bytes 196616 | tf_op jit(solution)/shard_map/ppermute | solution.py:317
  18.6 2.9 %shard_map.177.part_ref = f32[1024,512]{1,0:T(8,128)S(1)} custom-call(s32[1,1024]{1,0:T(1,128)S(1)} %bitcast.26, bf16[512,512]{1,0:T(8,128)(2,1)S(1)} %copy-done.8, bf16[4,512,512]{2,1,0:T(8,128)(2,1)S(1)} %copy-done.4, f32[5,2,512]{2,1,0:T(2,128)S(1)} %copy-done.7, bf16[1024,512]{1,0:T(8,128)(2,1)} %edges_hbm.1), custom_call_target="tpu_custom_call" | custom-call | flops 1610612736 | tf_op jit(solution)/shard_map/pallas_call | solution.py:85
  22.1 2.0 %collective-permute-done.7.refs_7_ = bf16[64,512]{1,0:T(8,128)(2,1)S(1)} collective-permute-done((bf16[64,512]{1,0:T(8,128)(2,1)S(1)}, bf16[64,512]{1,0:T(8,128)(2,1)S(1)}, u32[]{:S(2)}, u32[]{:S(2)}) %collective-permute-start.7) | collective-permute-done | bytes 65568 | tf_op jit(solution)/shard_map/ppermute | solution.py:317
  24.1 2.5 %shard_map.179 = (bf16[64,512]{1,0:T(8,128)(2,1)S(1)}, bf16[64,512]{1,0:T(8,128)(2,1)S(1)}, bf16[64,512]{1,0:T(8,128)(2,1)S(1)}, bf16[64,512]{1,0:T(8,128)(2,1)S...) custom-call(s32[1,1024]{1,0:T(1,128)S(1)} %bitcast.27, ...), custom_call_target="tpu_custom_call" | custom-call | flops 1610612736 | tf_op jit(solution)/shard_map/pallas_call | solution.py:85
  28.7 2.5 %collective-permute-start.12 = (bf16[64,512]{1,0:T(8,128)(2,1)S(1)}, bf16[64,512]{1,0:T(8,128)(2,1)S(1)}, u32[]{:S(2)}, u32[]{:S(2)}) collective-permute-start(bf16[64,512]{1,0:T(8,128)(2,1)S(1)} %get-tuple-element.46), channel_id=1, source_target_pairs={{0,16},{4,20},{8,24},{12,28},{16,0},{20,4},{24,8},{28,12},{1,17},{... | collective-permute-start | bytes 196616 | tf_op jit(solution)/shard_map/ppermute | solution.py:317
  32.5 2.0 %collective-permute-start.14 = (bf16[64,512]{1,0:T(8,128)(2,1)S(1)}, bf16[64,512]{1,0:T(8,128)(2,1)S(1)}, u32[]{:S(2)}, u32[]{:S(2)}) collective-permute-start(bf16[64,512]{1,0:T(8,128)(2,1)S(1)} %get-tuple-element.48), channel_id=1, source_target_pairs={{0,24},{4,28},{8,16},{12,20},{16,8},{20,12},{24,0},{28,4},{1,25},{... | collective-permute-start | bytes 196616 | tf_op jit(solution)/shard_map/ppermute | solution.py:317
  34.5 1.8 %collective-permute-start.15 = (bf16[64,512]{1,0:T(8,128)(2,1)S(1)}, bf16[64,512]{1,0:T(8,128)(2,1)S(1)}, u32[]{:S(2)}, u32[]{:S(2)}) collective-permute-start(bf16[64,512]{1,0:T(8,128)(2,1)S(1)} %get-tuple-element.49), channel_id=1, source_target_pairs={{0,28},{4,24},{8,20},{12,16},{16,12},{20,8},{24,4},{28,0},{1,29},{... | collective-permute-start | bytes 196616 | tf_op jit(solution)/shard_map/ppermute | solution.py:317
  36.3 1.5 %collective-permute-start.9 = (bf16[64,512]{1,0:T(8,128)(2,1)S(1)}, bf16[64,512]{1,0:T(8,128)(2,1)S(1)}, u32[]{:S(2)}, u32[]{:S(2)}) collective-permute-start(bf16[64,512]{1,0:T(8,128)(2,1)S(1)} %get-tuple-element.43), channel_id=1, source_target_pairs={{0,4},{4,0},{8,12},{12,8},{16,20},{20,16},{24,28},{28,24},{1,5},{5... | collective-permute-start | bytes 196616 | tf_op jit(solution)/shard_map/ppermute | solution.py:317
  37.8 4.7 %collective-permute-done.13.refs_5_ = bf16[64,512]{1,0:T(8,128)(2,1)S(1)} collective-permute-done((bf16[64,512]{1,0:T(8,128)(2,1)S(1)}, bf16[64,512]{1,0:T(8,128)(2,1)S(1)}, u32[]{:S(2)}, u32[]{:S(2)}) %collective-permute-start.13) | collective-permute-done | bytes 65568 | tf_op jit(solution)/shard_map/ppermute | solution.py:317
  46.9 2.5 %collective-permute-done.19.got_ref = bf16[64,512]{1,0:T(8,128)(2,1)S(1)} collective-permute-done((bf16[64,512]{1,0:T(8,128)(2,1)S(1)}, bf16[64,512]{1,0:T(8,128)(2,1)S(1)}, u32[]{:S(2)}, u32[]{:S(2)}) %collective-permute-start.19) | collective-permute-done | bytes 65568 | tf_op jit(solution)/shard_map/ppermute | solution.py:317
  51.9 2.2 %collective-permute-done.20 = bf16[4,8,512]{2,1,0:T(8,128)(2,1)S(1)} collective-permute-done((bf16[4,8,512]{2,1,0:T(8,128)(2,1)S(1)}, bf16[4,8,512]{2,1,0:T(8,128)(2,1)S(1)}, u32[]{:S(2)}, u32[]{:S(2)}) %collective-permute-start.20) | collective-permute-done | bytes 32800 | tf_op jit(solution)/shard_map/ppermute | solution.py:317
  54.2 2.8 %collective-permute-start.21 = (bf16[2,16,512]{2,1,0:T(8,128)(2,1)S(1)}, bf16[2,16,512]{2,1,0:T(8,128)(2,1)S(1)}, u32[]{:S(2)}, u32[]{:S(2)}) collective-permute-start(bf16[2,16,512]{2,1,0:T(8,128)(2,1)S(1)} %get-tuple-element.69), channel_id=1, source_target_pairs={{0,8},{4,12},{8,0},{12,4},{16,24},{20,28},{24,16},{28,20},{1,9},{5... | collective-permute-start | bytes 98312 | tf_op jit(solution)/shard_map/ppermute | solution.py:317
  57.0 1.9 %collective-permute-done.21 = bf16[2,16,512]{2,1,0:T(8,128)(2,1)S(1)} collective-permute-done((bf16[2,16,512]{2,1,0:T(8,128)(2,1)S(1)}, bf16[2,16,512]{2,1,0:T(8,128)(2,1)S(1)}, u32[]{:S(2)}, u32[]{:S(2)}) %collective-permute-start.21) | collective-permute-done | bytes 32800 | tf_op jit(solution)/shard_map/ppermute | solution.py:317
  60.7 2.9 %collective-permute-start.22 = (bf16[1,32,512]{2,1,0:T(8,128)(2,1)S(1)}, bf16[1,32,512]{2,1,0:T(8,128)(2,1)S(1)}, u32[]{:S(2)}, u32[]{:S(2)}) collective-permute-start(bf16[1,32,512]{2,1,0:T(8,128)(2,1)S(1)} %get-tuple-element.67), channel_id=1, source_target_pairs={{0,16},{4,20},{8,24},{12,28},{16,0},{20,4},{24,8},{28,12},{1,17},{... | collective-permute-start | bytes 98312 | tf_op jit(solution)/shard_map/ppermute | solution.py:317
  63.5 2.0 %collective-permute-done.22 = bf16[1,32,512]{2,1,0:T(8,128)(2,1)S(1)} collective-permute-done((bf16[1,32,512]{2,1,0:T(8,128)(2,1)S(1)}, bf16[1,32,512]{2,1,0:T(8,128)(2,1)S(1)}, u32[]{:S(2)}, u32[]{:S(2)}) %collective-permute-start.22) | collective-permute-done | bytes 32800 | tf_op jit(solution)/shard_map/ppermute | solution.py:317
  67.0 2.2 %shard_map.186 = (bf16[320,512]{1,0:T(8,128)(2,1)S(1)}, bf16[1024,512]{1,0:T(8,128)(2,1)S(1)}) custom-call(s32[1,1024]{1,0:T(1,128)S(1)} %bitcast.25, s32[1,1024]{1,0:T(1,128)S(1)} %bitcast.22, f32[1024,512]{1,0:T(8,128)S(1)} %shard_map.184.part_ref, bf16[64,512]{1,0:T(8,128)(2,1)S(1)} %bitcast.20, bf16[4,512,512]{2,1,0:T(8,128)(2,1)S(1)} %copy-done, ...), custom_call_target="tpu_custom_call" | custom-call | flops 1073741824 | tf_op jit(solution)/shard_map/pallas_call | solution.py:85
  74.1 3.2 %collective-permute-done.24.got_ref = bf16[160,512]{1,0:T(8,128)(2,1)S(1)} collective-permute-done((bf16[160,512]{1,0:T(8,128)(2,1)S(1)}, bf16[160,512]{1,0:T(8,128)(2,1)S(1)}, u32[]{:S(2)}, u32[]{:S(2)}) %collective-permute-start.24) | collective-permute-done | bytes 163872 | tf_op jit(solution)/shard_map/ppermute | solution.py:317
  (86 shorter events, 20.7 us)
Async XLA Ops:
  3.0 10.7 %collective-permute-start.1 = (bf16[64,512]{1,0:T(8,128)(2,1)S(1)}, bf16[64,512]{1,0:T(8,128)(2,1)S(1)}, u32[]{:S(2)}, u32[]{:S(2)}) collective-permute-start(bf16[64,512]{1,0:T(8,128)(2,1)S(1)} %get-tuple-element.34), channel_id=1, source_target_pairs={{0,4},{4,0},{8,12},{12,8},{16,20},{20,16},{24,28},{28,24},{1,5},{5... | collective-permute-start | bytes 196616 | tf_op jit(solution)/shard_map/ppermute | solution.py:317
  6.1 11.0 %collective-permute-start.2 = (bf16[64,512]{1,0:T(8,128)(2,1)S(1)}, bf16[64,512]{1,0:T(8,128)(2,1)S(1)}, u32[]{:S(2)}, u32[]{:S(2)}) collective-permute-start(bf16[64,512]{1,0:T(8,128)(2,1)S(1)} %get-tuple-element.35), channel_id=1, source_target_pairs={{0,8},{4,12},{8,0},{12,4},{16,24},{20,28},{24,16},{28,20},{1,9},{5... | collective-permute-start | bytes 196616 | tf_op jit(solution)/shard_map/ppermute | solution.py:317
  7.7 4.5 %collective-permute-start = (s32[1,64]{1,0:T(1,128)S(1)}, s32[1,64]{1,0:T(1,128)S(1)}, u32[]{:S(2)}, u32[]{:S(2)}) collective-permute-start(s32[1,64]{1,0:T(1,128)S(1)} %copy-done.13), channel_id=1, source_target_pairs={{0,2},{1,3},{2,0},{3,1},{4,6},{5,7},{6,4},{7,5},{8,10},{9,11},{10,... | collective-permute-start | bytes 776 | tf_op jit(solution)/shard_map/ppermute | solution.py:317
  9.1 12.4 %collective-permute-start.3 = (bf16[64,512]{1,0:T(8,128)(2,1)S(1)}, bf16[64,512]{1,0:T(8,128)(2,1)S(1)}, u32[]{:S(2)}, u32[]{:S(2)}) collective-permute-start(bf16[64,512]{1,0:T(8,128)(2,1)S(1)} %get-tuple-element.36), channel_id=1, source_target_pairs={{0,12},{4,8},{8,4},{12,0},{16,28},{20,24},{24,20},{28,16},{1,13},{... | collective-permute-start | bytes 196616 | tf_op jit(solution)/shard_map/ppermute | solution.py:317
  9.5 12.0 %collective-permute-start.4 = (bf16[64,512]{1,0:T(8,128)(2,1)S(1)}, bf16[64,512]{1,0:T(8,128)(2,1)S(1)}, u32[]{:S(2)}, u32[]{:S(2)}) collective-permute-start(bf16[64,512]{1,0:T(8,128)(2,1)S(1)} %get-tuple-element.37), channel_id=1, source_target_pairs={{0,16},{4,20},{8,24},{12,28},{16,0},{20,4},{24,8},{28,12},{1,17},{... | collective-permute-start | bytes 196616 | tf_op jit(solution)/shard_map/ppermute | solution.py:317
  12.1 10.0 %collective-permute-start.5 = (bf16[64,512]{1,0:T(8,128)(2,1)S(1)}, bf16[64,512]{1,0:T(8,128)(2,1)S(1)}, u32[]{:S(2)}, u32[]{:S(2)}) collective-permute-start(bf16[64,512]{1,0:T(8,128)(2,1)S(1)} %get-tuple-element.38), channel_id=1, source_target_pairs={{0,20},{4,16},{8,28},{12,24},{16,4},{20,0},{24,12},{28,8},{1,21},{... | collective-permute-start | bytes 196616 | tf_op jit(solution)/shard_map/ppermute | solution.py:317
  13.8 8.3 %collective-permute-start.6 = (bf16[64,512]{1,0:T(8,128)(2,1)S(1)}, bf16[64,512]{1,0:T(8,128)(2,1)S(1)}, u32[]{:S(2)}, u32[]{:S(2)}) collective-permute-start(bf16[64,512]{1,0:T(8,128)(2,1)S(1)} %get-tuple-element.39), channel_id=1, source_target_pairs={{0,24},{4,28},{8,16},{12,20},{16,8},{20,12},{24,0},{28,4},{1,25},{... | collective-permute-start | bytes 196616 | tf_op jit(solution)/shard_map/ppermute | solution.py:317
  17.0 7.1 %collective-permute-start.7 = (bf16[64,512]{1,0:T(8,128)(2,1)S(1)}, bf16[64,512]{1,0:T(8,128)(2,1)S(1)}, u32[]{:S(2)}, u32[]{:S(2)}) collective-permute-start(bf16[64,512]{1,0:T(8,128)(2,1)S(1)} %get-tuple-element.40), channel_id=1, source_target_pairs={{0,28},{4,24},{8,20},{12,16},{16,12},{20,8},{24,4},{28,0},{1,29},{... | collective-permute-start | bytes 196616 | tf_op jit(solution)/shard_map/ppermute | solution.py:317
  26.6 7.9 %collective-permute-start.10 = (bf16[64,512]{1,0:T(8,128)(2,1)S(1)}, bf16[64,512]{1,0:T(8,128)(2,1)S(1)}, u32[]{:S(2)}, u32[]{:S(2)}) collective-permute-start(bf16[64,512]{1,0:T(8,128)(2,1)S(1)} %get-tuple-element.44), channel_id=1, source_target_pairs={{0,8},{4,12},{8,0},{12,4},{16,24},{20,28},{24,16},{28,20},{1,9},{5... | collective-permute-start | bytes 196616 | tf_op jit(solution)/shard_map/ppermute | solution.py:317
  28.0 8.3 %collective-permute-start.11 = (bf16[64,512]{1,0:T(8,128)(2,1)S(1)}, bf16[64,512]{1,0:T(8,128)(2,1)S(1)}, u32[]{:S(2)}, u32[]{:S(2)}) collective-permute-start(bf16[64,512]{1,0:T(8,128)(2,1)S(1)} %get-tuple-element.45), channel_id=1, source_target_pairs={{0,12},{4,8},{8,4},{12,0},{16,28},{20,24},{24,20},{28,16},{1,13},{... | collective-permute-start | bytes 196616 | tf_op jit(solution)/shard_map/ppermute | solution.py:317
  28.7 3.9 %collective-permute-start.8 = (s32[2,64]{1,0:T(2,128)S(1)}, s32[2,64]{1,0:T(2,128)S(1)}, u32[]{:S(2)}, u32[]{:S(2)}) collective-permute-start(s32[2,64]{1,0:T(2,128)S(1)} %get-tuple-element.41.lists_ref), channel_id=1, source_target_pairs={{0,1},{1,0},{2,3},{3,2},{4,5},{5,4},{6,7},{7,6},{8,9},{9,8},{10,11... | collective-permute-start | bytes 1544 | tf_op jit(solution)/shard_map/ppermute | solution.py:317
  28.7 9.2 %collective-permute-start.12 = (bf16[64,512]{1,0:T(8,128)(2,1)S(1)}, bf16[64,512]{1,0:T(8,128)(2,1)S(1)}, u32[]{:S(2)}, u32[]{:S(2)}) collective-permute-start(bf16[64,512]{1,0:T(8,128)(2,1)S(1)} %get-tuple-element.46), channel_id=1, source_target_pairs={{0,16},{4,20},{8,24},{12,28},{16,0},{20,4},{24,8},{28,12},{1,17},{... | collective-permute-start | bytes 196616 | tf_op jit(solution)/shard_map/ppermute | solution.py:317
  31.1 11.4 %collective-permute-start.13 = (bf16[64,512]{1,0:T(8,128)(2,1)S(1)}, bf16[64,512]{1,0:T(8,128)(2,1)S(1)}, u32[]{:S(2)}, u32[]{:S(2)}) collective-permute-start(bf16[64,512]{1,0:T(8,128)(2,1)S(1)} %get-tuple-element.47), channel_id=1, source_target_pairs={{0,20},{4,16},{8,28},{12,24},{16,4},{20,0},{24,12},{28,8},{1,21},{... | collective-permute-start | bytes 196616 | tf_op jit(solution)/shard_map/ppermute | solution.py:317
  32.5 10.0 %collective-permute-start.14 = (bf16[64,512]{1,0:T(8,128)(2,1)S(1)}, bf16[64,512]{1,0:T(8,128)(2,1)S(1)}, u32[]{:S(2)}, u32[]{:S(2)}) collective-permute-start(bf16[64,512]{1,0:T(8,128)(2,1)S(1)} %get-tuple-element.48), channel_id=1, source_target_pairs={{0,24},{4,28},{8,16},{12,20},{16,8},{20,12},{24,0},{28,4},{1,25},{... | collective-permute-start | bytes 196616 | tf_op jit(solution)/shard_map/ppermute | solution.py:317
  34.5 8.0 %collective-permute-start.15 = (bf16[64,512]{1,0:T(8,128)(2,1)S(1)}, bf16[64,512]{1,0:T(8,128)(2,1)S(1)}, u32[]{:S(2)}, u32[]{:S(2)}) collective-permute-start(bf16[64,512]{1,0:T(8,128)(2,1)S(1)} %get-tuple-element.49), channel_id=1, source_target_pairs={{0,28},{4,24},{8,20},{12,16},{16,12},{20,8},{24,4},{28,0},{1,29},{... | collective-permute-start | bytes 196616 | tf_op jit(solution)/shard_map/ppermute | solution.py:317
  36.3 6.4 %collective-permute-start.9 = (bf16[64,512]{1,0:T(8,128)(2,1)S(1)}, bf16[64,512]{1,0:T(8,128)(2,1)S(1)}, u32[]{:S(2)}, u32[]{:S(2)}) collective-permute-start(bf16[64,512]{1,0:T(8,128)(2,1)S(1)} %get-tuple-element.43), channel_id=1, source_target_pairs={{0,4},{4,0},{8,12},{12,8},{16,20},{20,16},{24,28},{28,24},{1,5},{5... | collective-permute-start | bytes 196616 | tf_op jit(solution)/shard_map/ppermute | solution.py:317
  43.2 1.9 %collective-permute-start.16 = (bf16[448,512]{1,0:T(8,128)(2,1)S(1)}, bf16[448,512]{1,0:T(8,128)(2,1)S(1)}, u32[]{:S(2)}, u32[]{:S(2)}) collective-permute-start(bf16[448,512]{1,0:T(8,128)(2,1)S(1)} %get-tuple-element.52), channel_id=1, source_target_pairs={{0,1},{1,0},{2,3},{3,2},{4,5},{5,4},{6,7},{7,6},{8,9},{9,8},{10,11... | collective-permute-start | bytes 1376264 | tf_op jit(solution)/shard_map/ppermute | solution.py:317
  45.1 4.3 %collective-permute-start.19 = (bf16[64,512]{1,0:T(8,128)(2,1)S(1)}, bf16[64,512]{1,0:T(8,128)(2,1)S(1)}, u32[]{:S(2)}, u32[]{:S(2)}) collective-permute-start(bf16[64,512]{1,0:T(8,128)(2,1)S(1)} %get-tuple-element.64), channel_id=1, source_target_pairs={{0,2},{1,3},{2,0},{3,1},{4,6},{5,7},{6,4},{7,5},{8,10},{9,11},{10,... | collective-permute-start | bytes 196616 | tf_op jit(solution)/shard_map/ppermute | solution.py:317
  50.2 4.0 %collective-permute-start.20 = (bf16[4,8,512]{2,1,0:T(8,128)(2,1)S(1)}, bf16[4,8,512]{2,1,0:T(8,128)(2,1)S(1)}, u32[]{:S(2)}, u32[]{:S(2)}) collective-permute-start(bf16[4,8,512]{2,1,0:T(8,128)(2,1)S(1)} %get-tuple-element.59), channel_id=1, source_target_pairs={{0,4},{4,0},{8,12},{12,8},{16,20},{20,16},{24,28},{28,24},{1,5},{5... | collective-permute-start | bytes 98312 | tf_op jit(solution)/shard_map/ppermute | solution.py:317
  51.3 8.4 %collective-permute-start.17 = (bf16[320,512]{1,0:T(8,128)(2,1)S(1)}, bf16[320,512]{1,0:T(8,128)(2,1)S(1)}, u32[]{:S(2)}, u32[]{:S(2)}) collective-permute-start(bf16[320,512]{1,0:T(8,128)(2,1)S(1)} %add_convert_fusion.half_ref), channel_id=1, source_target_pairs={{0,2},{1,3},{2,0},{3,1},{4,6},{5,7},{6,4},{7,5},{8,10},{9,11},{10,... | collective-permute-start | bytes 983048 | tf_op jit(solution)/shard_map/ppermute | solution.py:317
  54.2 4.7 %collective-permute-start.21 = (bf16[2,16,512]{2,1,0:T(8,128)(2,1)S(1)}, bf16[2,16,512]{2,1,0:T(8,128)(2,1)S(1)}, u32[]{:S(2)}, u32[]{:S(2)}) collective-permute-start(bf16[2,16,512]{2,1,0:T(8,128)(2,1)S(1)} %get-tuple-element.69), channel_id=1, source_target_pairs={{0,8},{4,12},{8,0},{12,4},{16,24},{20,28},{24,16},{28,20},{1,9},{5... | collective-permute-start | bytes 98312 | tf_op jit(solution)/shard_map/ppermute | solution.py:317
  60.6 5.0 %collective-permute-start.18 = (bf16[320,512]{1,0:T(8,128)(2,1)S(1)}, bf16[320,512]{1,0:T(8,128)(2,1)S(1)}, u32[]{:S(2)}, u32[]{:S(2)}) collective-permute-start(bf16[320,512]{1,0:T(8,128)(2,1)S(1)} %shard_map.183.own_ref.half_ref), channel_id=1, source_target_pairs={{0,1},{1,0},{2,3},{3,2},{4,5},{5,4},{6,7},{7,6},{8,9},{9,8},{10,11... | collective-permute-start | bytes 983048 | tf_op jit(solution)/shard_map/ppermute | solution.py:317
  60.7 4.9 %collective-permute-start.22 = (bf16[1,32,512]{2,1,0:T(8,128)(2,1)S(1)}, bf16[1,32,512]{2,1,0:T(8,128)(2,1)S(1)}, u32[]{:S(2)}, u32[]{:S(2)}) collective-permute-start(bf16[1,32,512]{2,1,0:T(8,128)(2,1)S(1)} %get-tuple-element.67), channel_id=1, source_target_pairs={{0,16},{4,20},{8,24},{12,28},{16,0},{20,4},{24,8},{28,12},{1,17},{... | collective-permute-start | bytes 98312 | tf_op jit(solution)/shard_map/ppermute | solution.py:317
  70.9 6.3 %collective-permute-start.24 = (bf16[160,512]{1,0:T(8,128)(2,1)S(1)}, bf16[160,512]{1,0:T(8,128)(2,1)S(1)}, u32[]{:S(2)}, u32[]{:S(2)}) collective-permute-start(bf16[160,512]{1,0:T(8,128)(2,1)S(1)} %slice.57), channel_id=1, source_target_pairs={{0,2},{1,3},{2,0},{3,1},{4,6},{5,7},{6,4},{7,5},{8,10},{9,11},{10,... | collective-permute-start | bytes 491528 | tf_op jit(solution)/shard_map/ppermute | solution.py:317
  (17 other events, 207.0 us)

commit v6 on v5

--- a/solution.py
+++ b/solution.py
@@ -11,7 +11,7 @@
 NEIGH = 8
 BF16 = jnp.bfloat16
 F32 = jnp.float32
-TILE = 256
+TILE = 512
 GRANT = 16 << 20
 
 
@@ -190,26 +190,24 @@
     )
 
 
-def land_kernel(exact, band_count, half, node_ref, lists_ref, *refs):
-    pieces, (given_ref, held) = refs[:NEIGH], refs[NEIGH:]
+def listed_kernel(exact, node_ref, own_ref, other_ref, *refs):
+    pieces, (given_ref, kept_ref, held) = refs[:NEIGH], refs[NEIGH:]
     for mask in range(NEIGH):
         held[window_of(mask, exact)] = pieces[mask][...]
-    core = lax.rem(lax.axis_index("band"), 2)
-    names = share_names(sublanes(2 * half), 2 * half // band_count, band_count, 1 - core)
     row = node_ref[...]
     landed = held[...].reshape(-1, held.shape[2])
-    given_ref[:half, :] = project(hot_rows(row, names[:half]), landed).astype(BF16)
-    given_ref[half:, :] = project(hot_lists(lists_ref, row), landed).astype(BF16)
-
-
-def keep_kernel(band_count, node_ref, lists_ref, held, kept_ref, listed_ref):
-    half = kept_ref.shape[0]
+    given_ref[...] = project(hot_lists(other_ref, row), landed).astype(BF16)
+    kept_ref[...] = project(hot_lists(own_ref, row), landed)
+
+
+def land_kernel(band_count, own, node_ref, held, sums_ref):
+    half = sums_ref.shape[0]
     core = lax.rem(lax.axis_index("band"), 2)
+    core = core if own else 1 - core
     names = share_names(sublanes(2 * half), 2 * half // band_count, band_count, core)
-    row = node_ref[...]
     landed = held[...].reshape(-1, held.shape[2])
-    kept_ref[...] = project(hot_rows(row, names[:half]), landed)
-    listed_ref[...] = project(hot_lists(lists_ref, row), landed)
+    sums = project(hot_rows(node_ref[...], names[:half]), landed)
+    sums_ref[...] = sums.astype(sums_ref.dtype)
 
 
 def own_share(place):
@@ -290,23 +288,30 @@
         picks = hot_columns(senders[at : at + TILE], names)
         first = part_ref[at : at + TILE, :] + project(picks, keys_ref[...])
         sent[at : at + TILE, :] = tail(first, weights_ref[3], biases_ref, gains_ref, 3).astype(BF16)
-    half = given_ref.shape[0]
+    given_ref[...] = half_sums(band_count, 0, 1, receiver_ref, sent, given_ref.shape[0]).astype(BF16)
+
+
+def half_sums(band_count, own, far, receiver_ref, sent, count):
     core = lax.rem(lax.axis_index("band"), 2)
-    places = share_names(sublanes(2 * half), 2 * half // band_count, band_count, 1 - core)
-    given_ref[...] = project(hot_rows(receiver_ref[...], places[:half]), sent[...]).astype(BF16)
-
-
-def own_kernel(band_count, receiver_ref, sent_ref, half_ref, weights_ref, biases_ref, kept_ref, part_ref):
-    half = kept_ref.shape[0]
-    core = lax.rem(lax.axis_index("band"), 2)
-    places = share_names(sublanes(2 * half), 2 * half // band_count, band_count, core)
-    kept_ref[...] = project(hot_rows(receiver_ref[...], places[:half]), sent_ref[...])
+    core = core if own else 1 - core
+    names = share_names(sublanes(4 * count), 4 * count // band_count, band_count, core)
+    return project(hot_rows(receiver_ref[...], names[far * count : (far + 1) * count]), sent[...])
+
+
+def far_kernel(band_count, receiver_ref, sent_ref, kept_ref):
+    kept_ref[...] = half_sums(band_count, 1, 1, receiver_ref, sent_ref, kept_ref.shape[0])
+
+
+def near_kernel(band_count, receiver_ref, sent_ref, half_ref, weights_ref, biases_ref, given_ref, kept_ref, part_ref):
+    count = kept_ref.shape[0]
+    given_ref[...] = half_sums(band_count, 0, 0, receiver_ref, sent_ref, count).astype(BF16)
+    kept_ref[...] = half_sums(band_count, 1, 0, receiver_ref, sent_ref, count)
     part_ref[...] = project(half_ref[: part_ref.shape[0], :], weights_ref[0]) + biases_ref[4, 0:1, :]
 
 
-def last_kernel(kept_ref, got_ref, half_ref, part_ref, weights_ref, biases_ref, gains_ref, out_ref):
+def last_kernel(kept_ref, paired_ref, got_ref, half_ref, part_ref, weights_ref, biases_ref, gains_ref, out_ref):
     own = half_ref[: out_ref.shape[0], :]
-    total = (kept_ref[...] + got_ref[...].astype(F32)).astype(BF16)
+    total = (kept_ref[...] + paired_ref[...].astype(F32) + got_ref[...].astype(F32)).astype(BF16)
     first = part_ref[...] + project(total, weights_ref[1])
     out_ref[...] = (
         own.astype(F32) + tail(first, weights_ref[2], biases_ref, gains_ref, 4)
@@ -360,6 +365,7 @@
     mcap = senders_all // blk_count
     for count in (blk_count, band_count, cap, mcap):
         assert count & (count - 1) == 0
+    assert band_count >= 4
     exact = blk_count == NEIGH
     unit = 2 * width * width
     piece = shape((cap, width), BF16)
@@ -424,23 +430,20 @@
         unit * (half_rows + medge_rows + 2 * senders_all),
     )
 
-    given, held = call(
-        functools.partial(land_kernel, exact, band_count, half_rows),
-        [shape((half_rows + listed, width), BF16), shape((NEIGH, cap, width), BF16)],
-        (enc_slot_node, other_lists, *landed),
-        (),
-        unit * (half_rows + listed),
-    )
-    kept, kept_listed = call(
-        functools.partial(keep_kernel, band_count),
-        [half_f, shape((listed, width), F32)],
-        (enc_slot_node, lists, held),
-        (),
-        unit * (half_rows + listed),
-    )
+    listed_shape = (listed, width)
+    given, kept_listed, held = call(
+        functools.partial(listed_kernel, exact),
+        [shape(listed_shape, BF16), shape(listed_shape, F32), shape((NEIGH, cap, width), BF16)],
+        (enc_slot_node, lists, other_lists, *landed),
+        (),
+        unit * 2 * listed,
+    )
+    got_listed = swap(given, "band", 1)
+    given = call(functools.partial(land_kernel, band_count, 0), half_bf, (enc_slot_node, held), (), unit * half_rows)
     got = swap(given, "band", 1)
-    half = (kept + got[:half_rows].astype(F32)).astype(BF16)
-    sums = (kept_listed + got[half_rows:].astype(F32)).astype(BF16)
+    kept = call(functools.partial(land_kernel, band_count, 1), half_f, (enc_slot_node, held), (), unit * half_rows)
+    half = (kept + got.astype(F32)).astype(BF16)
+    sums = (kept_listed + got_listed.astype(F32)).astype(BF16)
     count = band_count // 2
     while True:
         count //= 2
@@ -502,9 +505,12 @@
         [pltpu.VMEM((patch_rows, width), BF16)],
         unit * (patch_rows + medge_rows),
     )
+    count = band_count // 4
+    near_rows = count * share_rows
+    quarter_bf, quarter_f = shape((near_rows, width), BF16), shape((near_rows, width), F32)
     given, sent = call(
         functools.partial(process_kernel, band_count, mcap),
-        [half_bf, shape((medge_rows, width), BF16)],
+        [quarter_bf, shape((medge_rows, width), BF16)],
         (
             mesh_sender.reshape(1, medge_rows),
             receivers,
@@ -517,24 +523,28 @@
         (),
         unit * 2 * medge_rows,
     )
-    kept, own_part = call(
-        functools.partial(own_kernel, band_count),
-        [half_f, shape((share_rows, width), F32)],
+    got = swap(given, "band", 1)
+    kept = call(functools.partial(far_kernel, band_count), quarter_f, (receivers, sent), (), unit * near_rows)
+    given = (kept + got.astype(F32)).astype(BF16)
+    got = swap(given, "band", 2 * count)
+    given, kept, own_part = call(
+        functools.partial(near_kernel, band_count),
+        [quarter_bf, quarter_f, shape((share_rows, width), F32)],
         (receivers, sent, half_mid, proc_node_weights, biases),
         (),
         unit * medge_rows,
     )
-    got = swap(given, "band", 1)
-    count = band_count // 2
+    paired = swap(given, "band", 1)
     while count > 1:
-        shares = kept + got.astype(F32)
+        shares = kept + paired.astype(F32) + got.astype(F32)
         count //= 2
         kept, given = shares[: count * share_rows], shares[count * share_rows :].astype(BF16)
+        paired = jnp.zeros_like(given)
         got = swap(given, "band", 2 * count)
     mesh_out = call(
         last_kernel,
         shape((share_rows, width), BF16),
-        (kept, got, half_mid, own_part, proc_node_weights, biases, gains),
+        (kept, paired, got, half_mid, own_part, proc_node_weights, biases, gains),
         (),
         unit * 3 * share_rows,
     )

time: 78.7 us -> 80 us (1.017)
  starting transfers between devices: 35.9 us -> 37 us
    ppermute x25 -> x27, starting transfers between devices: 35.9 us -> 37 us  [swap(): lax.ppermute(rows, axis, [(i, i ^ mask) for i in range(lax.axis_size(axis...]
    ppermute x25 -> x27, waiting for transfers between devices: 22.5 us -> 22.8 us  [swap(): lax.ppermute(rows, axis, [(i, i ^ mask) for i in range(lax.axis_size(axis...]
    pallas_call x13 -> x15, Pallas kernels: 17.3 us -> 17.2 us  [call(): pl.pallas_call(kernel, out_shape=tuple((pltpu.VMEM(out.shape, out.dtype)...]
  transfers between devices with their start and end apart: 25 -> 27, of which waited for: 12 -> 11; matrix products, arithmetic and copies ran while one was open for 1% -> 1% of each run, Pallas kernels for 8% -> 9%
where the time goes in v6:
time: 80 us; the launch traced here: 79.8 us
  starting transfers between devices  37 us (46%)
  waiting for transfers between devices  22.8 us (28%)
  Pallas kernels  17.2 us (22%)
  local copies, waits for them, and re-layouts  1.59 us (2%)
  between operations  1.04 us (1%)
    ppermute x27, starting transfers between devices, swap(): lax.ppermute(rows, axis, [(i, i ^ mask) for i in range(lax.axis_size(axis...  37 us
    ppermute x27, waiting for transfers between devices, swap(): lax.ppermute(rows, axis, [(i, i ^ mask) for i in range(lax.axis_size(axis...  22.8 us
    pallas_call x15, Pallas kernels, call(): pl.pallas_call(kernel, out_shape=tuple((pltpu.VMEM(out.shape, out.dtype)...  17.2 us
  transfers between devices with their start and end apart: 27, of which 11 were waited for; matrix products, arithmetic and copies ran while one was open for 1% of the time, Pallas kernels for 9%

profile of v6, /device:TPU:0, one launch (start us, length us, event | category | flops | bytes accessed | tf_op | source)
XLA Modules:
  0.0 79.8 jit_solution(17115706063849797208)
XLA Ops:
  0.7 2.3 %shard_map.178 = (bf16[64,512]{1,0:T(8,128)(2,1)S(1)}, bf16[64,512]{1,0:T(8,128)(2,1)S(1)}, bf16[64,512]{1,0:T(8,128)(2,1)S(1)}, bf16[64,512]{1,0:T(8,128)(2,1)S...) custom-call(s32[1,512]{1,0:T(1,128)} %node_ref.5, ...), custom_call_target="tpu_custom_call" | custom-call | flops 536870912 | tf_op jit(solution)/shard_map/pallas_call | solution.py:85
  3.0 3.1 %collective-permute-start.1 = (bf16[64,512]{1,0:T(8,128)(2,1)S(1)}, bf16[64,512]{1,0:T(8,128)(2,1)S(1)}, u32[]{:S(2)}, u32[]{:S(2)}) collective-permute-start(bf16[64,512]{1,0:T(8,128)(2,1)S(1)} %get-tuple-element.34), channel_id=1, source_target_pairs={{0,4},{4,0},{8,12},{12,8},{16,20},{20,16},{24,28},{28,24},{1,5},{5... | collective-permute-start | bytes 196616 | tf_op jit(solution)/shard_map/ppermute | solution.py:322
  6.1 1.6 %collective-permute-start.2 = (bf16[64,512]{1,0:T(8,128)(2,1)S(1)}, bf16[64,512]{1,0:T(8,128)(2,1)S(1)}, u32[]{:S(2)}, u32[]{:S(2)}) collective-permute-start(bf16[64,512]{1,0:T(8,128)(2,1)S(1)} %get-tuple-element.35), channel_id=1, source_target_pairs={{0,8},{4,12},{8,0},{12,4},{16,24},{20,28},{24,16},{28,20},{1,9},{5... | collective-permute-start | bytes 196616 | tf_op jit(solution)/shard_map/ppermute | solution.py:322
  9.5 2.6 %collective-permute-start.4 = (bf16[64,512]{1,0:T(8,128)(2,1)S(1)}, bf16[64,512]{1,0:T(8,128)(2,1)S(1)}, u32[]{:S(2)}, u32[]{:S(2)}) collective-permute-start(bf16[64,512]{1,0:T(8,128)(2,1)S(1)} %get-tuple-element.37), channel_id=1, source_target_pairs={{0,16},{4,20},{8,24},{12,28},{16,0},{20,4},{24,8},{28,12},{1,17},{... | collective-permute-start | bytes 196616 | tf_op jit(solution)/shard_map/ppermute | solution.py:322
  12.1 1.6 %collective-permute-start.5 = (bf16[64,512]{1,0:T(8,128)(2,1)S(1)}, bf16[64,512]{1,0:T(8,128)(2,1)S(1)}, u32[]{:S(2)}, u32[]{:S(2)}) collective-permute-start(bf16[64,512]{1,0:T(8,128)(2,1)S(1)} %get-tuple-element.38), channel_id=1, source_target_pairs={{0,20},{4,16},{8,28},{12,24},{16,4},{20,0},{24,12},{28,8},{1,21},{... | collective-permute-start | bytes 196616 | tf_op jit(solution)/shard_map/ppermute | solution.py:322
  13.8 3.3 %collective-permute-start.6 = (bf16[64,512]{1,0:T(8,128)(2,1)S(1)}, bf16[64,512]{1,0:T(8,128)(2,1)S(1)}, u32[]{:S(2)}, u32[]{:S(2)}) collective-permute-start(bf16[64,512]{1,0:T(8,128)(2,1)S(1)} %get-tuple-element.39), channel_id=1, source_target_pairs={{0,24},{4,28},{8,16},{12,20},{16,8},{20,12},{24,0},{28,4},{1,25},{... | collective-permute-start | bytes 196616 | tf_op jit(solution)/shard_map/ppermute | solution.py:322
  17.0 1.5 %collective-permute-start.7 = (bf16[64,512]{1,0:T(8,128)(2,1)S(1)}, bf16[64,512]{1,0:T(8,128)(2,1)S(1)}, u32[]{:S(2)}, u32[]{:S(2)}) collective-permute-start(bf16[64,512]{1,0:T(8,128)(2,1)S(1)} %get-tuple-element.40), channel_id=1, source_target_pairs={{0,28},{4,24},{8,20},{12,16},{16,12},{20,8},{24,4},{28,0},{1,29},{... | collective-permute-start | bytes 196616 | tf_op jit(solution)/shard_map/ppermute | solution.py:322
  18.6 2.8 %shard_map.177.part_ref = f32[1024,512]{1,0:T(8,128)S(1)} custom-call(s32[1,1024]{1,0:T(1,128)S(1)} %bitcast.27, bf16[512,512]{1,0:T(8,128)(2,1)S(1)} %copy-done.8, bf16[4,512,512]{2,1,0:T(8,128)(2,1)S(1)} %copy-done.4, f32[5,2,512]{2,1,0:T(2,128)S(1)} %copy-done.7, bf16[1024,512]{1,0:T(8,128)(2,1)} %edges_hbm.1), custom_call_target="tpu_custom_call" | custom-call | flops 1610612736 | tf_op jit(solution)/shard_map/pallas_call | solution.py:85
  22.1 2.0 %collective-permute-done.7.refs_7_ = bf16[64,512]{1,0:T(8,128)(2,1)S(1)} collective-permute-done((bf16[64,512]{1,0:T(8,128)(2,1)S(1)}, bf16[64,512]{1,0:T(8,128)(2,1)S(1)}, u32[]{:S(2)}, u32[]{:S(2)}) %collective-permute-start.7) | collective-permute-done | bytes 65568 | tf_op jit(solution)/shard_map/ppermute | solution.py:322
  24.1 2.3 %shard_map.179 = (bf16[64,512]{1,0:T(8,128)(2,1)S(1)}, bf16[64,512]{1,0:T(8,128)(2,1)S(1)}, bf16[64,512]{1,0:T(8,128)(2,1)S(1)}, bf16[64,512]{1,0:T(8,128)(2,1)S...) custom-call(s32[1,1024]{1,0:T(1,128)S(1)} %bitcast.28, ...), custom_call_target="tpu_custom_call" | custom-call | flops 1610612736 | tf_op jit(solution)/shard_map/pallas_call | solution.py:85
  28.5 2.5 %collective-permute-start.12 = (bf16[64,512]{1,0:T(8,128)(2,1)S(1)}, bf16[64,512]{1,0:T(8,128)(2,1)S(1)}, u32[]{:S(2)}, u32[]{:S(2)}) collective-permute-start(bf16[64,512]{1,0:T(8,128)(2,1)S(1)} %get-tuple-element.46), channel_id=1, source_target_pairs={{0,16},{4,20},{8,24},{12,28},{16,0},{20,4},{24,8},{28,12},{1,17},{... | collective-permute-start | bytes 196616 | tf_op jit(solution)/shard_map/ppermute | solution.py:322
  32.4 2.0 %collective-permute-start.14 = (bf16[64,512]{1,0:T(8,128)(2,1)S(1)}, bf16[64,512]{1,0:T(8,128)(2,1)S(1)}, u32[]{:S(2)}, u32[]{:S(2)}) collective-permute-start(bf16[64,512]{1,0:T(8,128)(2,1)S(1)} %get-tuple-element.48), channel_id=1, source_target_pairs={{0,24},{4,28},{8,16},{12,20},{16,8},{20,12},{24,0},{28,4},{1,25},{... | collective-permute-start | bytes 196616 | tf_op jit(solution)/shard_map/ppermute | solution.py:322
  34.4 1.8 %collective-permute-start.15 = (bf16[64,512]{1,0:T(8,128)(2,1)S(1)}, bf16[64,512]{1,0:T(8,128)(2,1)S(1)}, u32[]{:S(2)}, u32[]{:S(2)}) collective-permute-start(bf16[64,512]{1,0:T(8,128)(2,1)S(1)} %get-tuple-element.49), channel_id=1, source_target_pairs={{0,28},{4,24},{8,20},{12,16},{16,12},{20,8},{24,4},{28,0},{1,29},{... | collective-permute-start | bytes 196616 | tf_op jit(solution)/shard_map/ppermute | solution.py:322
  36.1 1.5 %collective-permute-start.9 = (bf16[64,512]{1,0:T(8,128)(2,1)S(1)}, bf16[64,512]{1,0:T(8,128)(2,1)S(1)}, u32[]{:S(2)}, u32[]{:S(2)}) collective-permute-start(bf16[64,512]{1,0:T(8,128)(2,1)S(1)} %get-tuple-element.43), channel_id=1, source_target_pairs={{0,4},{4,0},{8,12},{12,8},{16,20},{20,16},{24,28},{28,24},{1,5},{5... | collective-permute-start | bytes 196616 | tf_op jit(solution)/shard_map/ppermute | solution.py:322
  37.7 4.7 %collective-permute-done.13.refs_5_ = bf16[64,512]{1,0:T(8,128)(2,1)S(1)} collective-permute-done((bf16[64,512]{1,0:T(8,128)(2,1)S(1)}, bf16[64,512]{1,0:T(8,128)(2,1)S(1)}, u32[]{:S(2)}, u32[]{:S(2)}) %collective-permute-start.13) | collective-permute-done | bytes 65568 | tf_op jit(solution)/shard_map/ppermute | solution.py:322
  46.2 2.5 %collective-permute-done.20.got_ref = bf16[64,512]{1,0:T(8,128)(2,1)S(1)} collective-permute-done((bf16[64,512]{1,0:T(8,128)(2,1)S(1)}, bf16[64,512]{1,0:T(8,128)(2,1)S(1)}, u32[]{:S(2)}, u32[]{:S(2)}) %collective-permute-start.20) | collective-permute-done | bytes 65568 | tf_op jit(solution)/shard_map/ppermute | solution.py:322
  50.8 2.6 %collective-permute-done.21 = bf16[4,8,512]{2,1,0:T(8,128)(2,1)S(1)} collective-permute-done((bf16[4,8,512]{2,1,0:T(8,128)(2,1)S(1)}, bf16[4,8,512]{2,1,0:T(8,128)(2,1)S(1)}, u32[]{:S(2)}, u32[]{:S(2)}) %collective-permute-start.21) | collective-permute-done | bytes 32800 | tf_op jit(solution)/shard_map/ppermute | solution.py:322
  54.1 2.7 %collective-permute-start.22 = (bf16[2,16,512]{2,1,0:T(8,128)(2,1)S(1)}, bf16[2,16,512]{2,1,0:T(8,128)(2,1)S(1)}, u32[]{:S(2)}, u32[]{:S(2)}) collective-permute-start(bf16[2,16,512]{2,1,0:T(8,128)(2,1)S(1)} %get-tuple-element.69), channel_id=1, source_target_pairs={{0,8},{4,12},{8,0},{12,4},{16,24},{20,28},{24,16},{28,20},{1,9},{5... | collective-permute-start | bytes 98312 | tf_op jit(solution)/shard_map/ppermute | solution.py:322
  56.9 1.9 %collective-permute-done.22 = bf16[2,16,512]{2,1,0:T(8,128)(2,1)S(1)} collective-permute-done((bf16[2,16,512]{2,1,0:T(8,128)(2,1)S(1)}, bf16[2,16,512]{2,1,0:T(8,128)(2,1)S(1)}, u32[]{:S(2)}, u32[]{:S(2)}) %collective-permute-start.22) | collective-permute-done | bytes 32800 | tf_op jit(solution)/shard_map/ppermute | solution.py:322
  58.8 2.3 %collective-permute-done.17.got_ref = bf16[320,512]{1,0:T(8,128)(2,1)S(1)} collective-permute-done((bf16[320,512]{1,0:T(8,128)(2,1)S(1)}, bf16[320,512]{1,0:T(8,128)(2,1)S(1)}, u32[]{:S(2)}, u32[]{:S(2)}) %collective-permute-start.17) | collective-permute-done | bytes 327712 | tf_op jit(solution)/shard_map/ppermute | solution.py:322
  62.0 3.4 %collective-permute-start.23 = (bf16[1,32,512]{2,1,0:T(8,128)(2,1)S(1)}, bf16[1,32,512]{2,1,0:T(8,128)(2,1)S(1)}, u32[]{:S(2)}, u32[]{:S(2)}) collective-permute-start(bf16[1,32,512]{2,1,0:T(8,128)(2,1)S(1)} %get-tuple-element.67), channel_id=1, source_target_pairs={{0,16},{4,20},{8,24},{12,28},{16,0},{20,4},{24,8},{28,12},{1,17},{... | collective-permute-start | bytes 98312 | tf_op jit(solution)/shard_map/ppermute | solution.py:322
  65.4 2.0 %collective-permute-done.23 = bf16[1,32,512]{2,1,0:T(8,128)(2,1)S(1)} collective-permute-done((bf16[1,32,512]{2,1,0:T(8,128)(2,1)S(1)}, bf16[1,32,512]{2,1,0:T(8,128)(2,1)S(1)}, u32[]{:S(2)}, u32[]{:S(2)}) %collective-permute-start.23) | collective-permute-done | bytes 32800 | tf_op jit(solution)/shard_map/ppermute | solution.py:322
  68.7 1.9 %shard_map.187 = (bf16[160,512]{1,0:T(8,128)(2,1)S(1)}, bf16[1024,512]{1,0:T(8,128)(2,1)S(1)}) custom-call(s32[1,1024]{1,0:T(1,128)S(1)} %bitcast.26, s32[1,1024]{1,0:T(1,128)S(1)} %bitcast.22, f32[1024,512]{1,0:T(8,128)S(1)} %shard_map.185.part_ref, bf16[64,512]{1,0:T(8,128)(2,1)S(1)} %bitcast.20, bf16[4,512,512]{2,1,0:T(8,128)(2,1)S(1)} %copy-done, ...), custom_call_target="tpu_custom_call" | custom-call | flops 1073741824 | tf_op jit(solution)/shard_map/pallas_call | solution.py:85
  74.8 3.7 %collective-permute-done.26.got_ref = bf16[160,512]{1,0:T(8,128)(2,1)S(1)} collective-permute-done((bf16[160,512]{1,0:T(8,128)(2,1)S(1)}, bf16[160,512]{1,0:T(8,128)(2,1)S(1)}, u32[]{:S(2)}, u32[]{:S(2)}) %collective-permute-start.26) | collective-permute-done | bytes 163872 | tf_op jit(solution)/shard_map/ppermute | solution.py:322
  (90 shorter events, 20.5 us)
Async XLA Ops:
  3.0 10.7 %collective-permute-start.1 = (bf16[64,512]{1,0:T(8,128)(2,1)S(1)}, bf16[64,512]{1,0:T(8,128)(2,1)S(1)}, u32[]{:S(2)}, u32[]{:S(2)}) collective-permute-start(bf16[64,512]{1,0:T(8,128)(2,1)S(1)} %get-tuple-element.34), channel_id=1, source_target_pairs={{0,4},{4,0},{8,12},{12,8},{16,20},{20,16},{24,28},{28,24},{1,5},{5... | collective-permute-start | bytes 196616 | tf_op jit(solution)/shard_map/ppermute | solution.py:322
  6.1 11.0 %collective-permute-start.2 = (bf16[64,512]{1,0:T(8,128)(2,1)S(1)}, bf16[64,512]{1,0:T(8,128)(2,1)S(1)}, u32[]{:S(2)}, u32[]{:S(2)}) collective-permute-start(bf16[64,512]{1,0:T(8,128)(2,1)S(1)} %get-tuple-element.35), channel_id=1, source_target_pairs={{0,8},{4,12},{8,0},{12,4},{16,24},{20,28},{24,16},{28,20},{1,9},{5... | collective-permute-start | bytes 196616 | tf_op jit(solution)/shard_map/ppermute | solution.py:322
  7.7 4.5 %collective-permute-start = (s32[1,64]{1,0:T(1,128)S(1)}, s32[1,64]{1,0:T(1,128)S(1)}, u32[]{:S(2)}, u32[]{:S(2)}) collective-permute-start(s32[1,64]{1,0:T(1,128)S(1)} %copy-done.13), channel_id=1, source_target_pairs={{0,2},{1,3},{2,0},{3,1},{4,6},{5,7},{6,4},{7,5},{8,10},{9,11},{10,... | collective-permute-start | bytes 776 | tf_op jit(solution)/shard_map/ppermute | solution.py:322
  9.1 12.3 %collective-permute-start.3 = (bf16[64,512]{1,0:T(8,128)(2,1)S(1)}, bf16[64,512]{1,0:T(8,128)(2,1)S(1)}, u32[]{:S(2)}, u32[]{:S(2)}) collective-permute-start(bf16[64,512]{1,0:T(8,128)(2,1)S(1)} %get-tuple-element.36), channel_id=1, source_target_pairs={{0,12},{4,8},{8,4},{12,0},{16,28},{20,24},{24,20},{28,16},{1,13},{... | collective-permute-start | bytes 196616 | tf_op jit(solution)/shard_map/ppermute | solution.py:322
  9.5 11.9 %collective-permute-start.4 = (bf16[64,512]{1,0:T(8,128)(2,1)S(1)}, bf16[64,512]{1,0:T(8,128)(2,1)S(1)}, u32[]{:S(2)}, u32[]{:S(2)}) collective-permute-start(bf16[64,512]{1,0:T(8,128)(2,1)S(1)} %get-tuple-element.37), channel_id=1, source_target_pairs={{0,16},{4,20},{8,24},{12,28},{16,0},{20,4},{24,8},{28,12},{1,17},{... | collective-permute-start | bytes 196616 | tf_op jit(solution)/shard_map/ppermute | solution.py:322
  12.1 10.0 %collective-permute-start.5 = (bf16[64,512]{1,0:T(8,128)(2,1)S(1)}, bf16[64,512]{1,0:T(8,128)(2,1)S(1)}, u32[]{:S(2)}, u32[]{:S(2)}) collective-permute-start(bf16[64,512]{1,0:T(8,128)(2,1)S(1)} %get-tuple-element.38), channel_id=1, source_target_pairs={{0,20},{4,16},{8,28},{12,24},{16,4},{20,0},{24,12},{28,8},{1,21},{... | collective-permute-start | bytes 196616 | tf_op jit(solution)/shard_map/ppermute | solution.py:322
  13.8 8.3 %collective-permute-start.6 = (bf16[64,512]{1,0:T(8,128)(2,1)S(1)}, bf16[64,512]{1,0:T(8,128)(2,1)S(1)}, u32[]{:S(2)}, u32[]{:S(2)}) collective-permute-start(bf16[64,512]{1,0:T(8,128)(2,1)S(1)} %get-tuple-element.39), channel_id=1, source_target_pairs={{0,24},{4,28},{8,16},{12,20},{16,8},{20,12},{24,0},{28,4},{1,25},{... | collective-permute-start | bytes 196616 | tf_op jit(solution)/shard_map/ppermute | solution.py:322
  17.0 7.1 %collective-permute-start.7 = (bf16[64,512]{1,0:T(8,128)(2,1)S(1)}, bf16[64,512]{1,0:T(8,128)(2,1)S(1)}, u32[]{:S(2)}, u32[]{:S(2)}) collective-permute-start(bf16[64,512]{1,0:T(8,128)(2,1)S(1)} %get-tuple-element.40), channel_id=1, source_target_pairs={{0,28},{4,24},{8,20},{12,16},{16,12},{20,8},{24,4},{28,0},{1,29},{... | collective-permute-start | bytes 196616 | tf_op jit(solution)/shard_map/ppermute | solution.py:322
  26.4 7.9 %collective-permute-start.10 = (bf16[64,512]{1,0:T(8,128)(2,1)S(1)}, bf16[64,512]{1,0:T(8,128)(2,1)S(1)}, u32[]{:S(2)}, u32[]{:S(2)}) collective-permute-start(bf16[64,512]{1,0:T(8,128)(2,1)S(1)} %get-tuple-element.44), channel_id=1, source_target_pairs={{0,8},{4,12},{8,0},{12,4},{16,24},{20,28},{24,16},{28,20},{1,9},{5... | collective-permute-start | bytes 196616 | tf_op jit(solution)/shard_map/ppermute | solution.py:322
  27.9 8.3 %collective-permute-start.11 = (bf16[64,512]{1,0:T(8,128)(2,1)S(1)}, bf16[64,512]{1,0:T(8,128)(2,1)S(1)}, u32[]{:S(2)}, u32[]{:S(2)}) collective-permute-start(bf16[64,512]{1,0:T(8,128)(2,1)S(1)} %get-tuple-element.45), channel_id=1, source_target_pairs={{0,12},{4,8},{8,4},{12,0},{16,28},{20,24},{24,20},{28,16},{1,13},{... | collective-permute-start | bytes 196616 | tf_op jit(solution)/shard_map/ppermute | solution.py:322
  28.5 3.9 %collective-permute-start.8 = (s32[2,64]{1,0:T(2,128)S(1)}, s32[2,64]{1,0:T(2,128)S(1)}, u32[]{:S(2)}, u32[]{:S(2)}) collective-permute-start(s32[2,64]{1,0:T(2,128)S(1)} %get-tuple-element.41.own_ref), channel_id=1, source_target_pairs={{0,1},{1,0},{2,3},{3,2},{4,5},{5,4},{6,7},{7,6},{8,9},{9,8},{10,11... | collective-permute-start | bytes 1544 | tf_op jit(solution)/shard_map/ppermute | solution.py:322
  28.5 9.2 %collective-permute-start.12 = (bf16[64,512]{1,0:T(8,128)(2,1)S(1)}, bf16[64,512]{1,0:T(8,128)(2,1)S(1)}, u32[]{:S(2)}, u32[]{:S(2)}) collective-permute-start(bf16[64,512]{1,0:T(8,128)(2,1)S(1)} %get-tuple-element.46), channel_id=1, source_target_pairs={{0,16},{4,20},{8,24},{12,28},{16,0},{20,4},{24,8},{28,12},{1,17},{... | collective-permute-start | bytes 196616 | tf_op jit(solution)/shard_map/ppermute | solution.py:322
  31.0 11.4 %collective-permute-start.13 = (bf16[64,512]{1,0:T(8,128)(2,1)S(1)}, bf16[64,512]{1,0:T(8,128)(2,1)S(1)}, u32[]{:S(2)}, u32[]{:S(2)}) collective-permute-start(bf16[64,512]{1,0:T(8,128)(2,1)S(1)} %get-tuple-element.47), channel_id=1, source_target_pairs={{0,20},{4,16},{8,28},{12,24},{16,4},{20,0},{24,12},{28,8},{1,21},{... | collective-permute-start | bytes 196616 | tf_op jit(solution)/shard_map/ppermute | solution.py:322
  32.4 10.0 %collective-permute-start.14 = (bf16[64,512]{1,0:T(8,128)(2,1)S(1)}, bf16[64,512]{1,0:T(8,128)(2,1)S(1)}, u32[]{:S(2)}, u32[]{:S(2)}) collective-permute-start(bf16[64,512]{1,0:T(8,128)(2,1)S(1)} %get-tuple-element.48), channel_id=1, source_target_pairs={{0,24},{4,28},{8,16},{12,20},{16,8},{20,12},{24,0},{28,4},{1,25},{... | collective-permute-start | bytes 196616 | tf_op jit(solution)/shard_map/ppermute | solution.py:322
  34.4 8.0 %collective-permute-start.15 = (bf16[64,512]{1,0:T(8,128)(2,1)S(1)}, bf16[64,512]{1,0:T(8,128)(2,1)S(1)}, u32[]{:S(2)}, u32[]{:S(2)}) collective-permute-start(bf16[64,512]{1,0:T(8,128)(2,1)S(1)} %get-tuple-element.49), channel_id=1, source_target_pairs={{0,28},{4,24},{8,20},{12,16},{16,12},{20,8},{24,4},{28,0},{1,29},{... | collective-permute-start | bytes 196616 | tf_op jit(solution)/shard_map/ppermute | solution.py:322
  36.1 6.4 %collective-permute-start.9 = (bf16[64,512]{1,0:T(8,128)(2,1)S(1)}, bf16[64,512]{1,0:T(8,128)(2,1)S(1)}, u32[]{:S(2)}, u32[]{:S(2)}) collective-permute-start(bf16[64,512]{1,0:T(8,128)(2,1)S(1)} %get-tuple-element.43), channel_id=1, source_target_pairs={{0,4},{4,0},{8,12},{12,8},{16,20},{20,16},{24,28},{28,24},{1,5},{5... | collective-permute-start | bytes 196616 | tf_op jit(solution)/shard_map/ppermute | solution.py:322
  43.3 10.1 %collective-permute-start.16 = (bf16[320,512]{1,0:T(8,128)(2,1)S(1)}, bf16[320,512]{1,0:T(8,128)(2,1)S(1)}, u32[]{:S(2)}, u32[]{:S(2)}) collective-permute-start(bf16[320,512]{1,0:T(8,128)(2,1)S(1)} %shard_map.182), channel_id=1, source_target_pairs={{0,1},{1,0},{2,3},{3,2},{4,5},{5,4},{6,7},{7,6},{8,9},{9,8},{10,11... | collective-permute-start | bytes 983048 | tf_op jit(solution)/shard_map/ppermute | solution.py:322
  44.3 4.3 %collective-permute-start.20 = (bf16[64,512]{1,0:T(8,128)(2,1)S(1)}, bf16[64,512]{1,0:T(8,128)(2,1)S(1)}, u32[]{:S(2)}, u32[]{:S(2)}) collective-permute-start(bf16[64,512]{1,0:T(8,128)(2,1)S(1)} %get-tuple-element.64), channel_id=1, source_target_pairs={{0,2},{1,3},{2,0},{3,1},{4,6},{5,7},{6,4},{7,5},{8,10},{9,11},{10,... | collective-permute-start | bytes 196616 | tf_op jit(solution)/shard_map/ppermute | solution.py:322
  49.4 4.0 %collective-permute-start.21 = (bf16[4,8,512]{2,1,0:T(8,128)(2,1)S(1)}, bf16[4,8,512]{2,1,0:T(8,128)(2,1)S(1)}, u32[]{:S(2)}, u32[]{:S(2)}) collective-permute-start(bf16[4,8,512]{2,1,0:T(8,128)(2,1)S(1)} %get-tuple-element.58), channel_id=1, source_target_pairs={{0,4},{4,0},{8,12},{12,8},{16,20},{20,16},{24,28},{28,24},{1,5},{5... | collective-permute-start | bytes 98312 | tf_op jit(solution)/shard_map/ppermute | solution.py:322
  53.5 7.5 %collective-permute-start.17 = (bf16[320,512]{1,0:T(8,128)(2,1)S(1)}, bf16[320,512]{1,0:T(8,128)(2,1)S(1)}, u32[]{:S(2)}, u32[]{:S(2)}) collective-permute-start(bf16[320,512]{1,0:T(8,128)(2,1)S(1)} %add_convert_fusion.half_ref), channel_id=1, source_target_pairs={{0,2},{1,3},{2,0},{3,1},{4,6},{5,7},{6,4},{7,5},{8,10},{9,11},{10,... | collective-permute-start | bytes 983048 | tf_op jit(solution)/shard_map/ppermute | solution.py:322
  54.1 4.6 %collective-permute-start.22 = (bf16[2,16,512]{2,1,0:T(8,128)(2,1)S(1)}, bf16[2,16,512]{2,1,0:T(8,128)(2,1)S(1)}, u32[]{:S(2)}, u32[]{:S(2)}) collective-permute-start(bf16[2,16,512]{2,1,0:T(8,128)(2,1)S(1)} %get-tuple-element.69), channel_id=1, source_target_pairs={{0,8},{4,12},{8,0},{12,4},{16,24},{20,28},{24,16},{28,20},{1,9},{5... | collective-permute-start | bytes 98312 | tf_op jit(solution)/shard_map/ppermute | solution.py:322
  61.9 5.5 %collective-permute-start.18 = (bf16[320,512]{1,0:T(8,128)(2,1)S(1)}, bf16[320,512]{1,0:T(8,128)(2,1)S(1)}, u32[]{:S(2)}, u32[]{:S(2)}) collective-permute-start(bf16[320,512]{1,0:T(8,128)(2,1)S(1)} %shard_map.184.own_ref.half_ref), channel_id=1, source_target_pairs={{0,1},{1,0},{2,3},{3,2},{4,5},{5,4},{6,7},{7,6},{8,9},{9,8},{10,11... | collective-permute-start | bytes 983048 | tf_op jit(solution)/shard_map/ppermute | solution.py:322
  62.0 5.3 %collective-permute-start.23 = (bf16[1,32,512]{2,1,0:T(8,128)(2,1)S(1)}, bf16[1,32,512]{2,1,0:T(8,128)(2,1)S(1)}, u32[]{:S(2)}, u32[]{:S(2)}) collective-permute-start(bf16[1,32,512]{2,1,0:T(8,128)(2,1)S(1)} %get-tuple-element.67), channel_id=1, source_target_pairs={{0,16},{4,20},{8,24},{12,28},{16,0},{20,4},{24,8},{28,12},{1,17},{... | collective-permute-start | bytes 98312 | tf_op jit(solution)/shard_map/ppermute | solution.py:322
  72.3 6.2 %collective-permute-start.26 = (bf16[160,512]{1,0:T(8,128)(2,1)S(1)}, bf16[160,512]{1,0:T(8,128)(2,1)S(1)}, u32[]{:S(2)}, u32[]{:S(2)}) collective-permute-start(bf16[160,512]{1,0:T(8,128)(2,1)S(1)} %add_convert_fusion.1), channel_id=1, source_target_pairs={{0,2},{1,3},{2,0},{3,1},{4,6},{5,7},{6,4},{7,5},{8,10},{9,11},{10,... | collective-permute-start | bytes 491528 | tf_op jit(solution)/shard_map/ppermute | solution.py:322
  (19 other events, 209.8 us)

commit v7 on v6

--- a/solution.py
+++ b/solution.py
@@ -262,9 +262,10 @@
     rows = (nodes_ref[...].astype(F32) + change).astype(BF16)
     held[...] = project(rows, w_edges[1]).astype(BF16).reshape(held.shape)
     blk = lax.axis_index("blk")
-    for pair in range(kept_ref.shape[0]):
-        kept_ref[pair] = held[blk ^ (2 * pair)]
-        given_ref[pair] = held[blk ^ (2 * pair + 1)]
+    count = kept_ref.shape[0]
+    for place in range(count):
+        kept_ref[place] = held[blk ^ place]
+        given_ref[place] = held[blk ^ (count + place)]
 
 
 def target_kernel(band_count, receiver_ref, own_ref, other_ref, part_ref, weights_ref, out_ref, table):
@@ -477,12 +478,13 @@
         [pltpu.VMEM((blk_count, mcap, width), BF16)],
         unit * 3 * senders_all,
     )
-    bit = 1
+    bit = blk_count // 2
+    kept, given = kept.reshape(1, bit * mcap, width), given.reshape(1, bit * mcap, width)
     while True:
         got_rows = swap(given, "blk", bit)
-        senders = jnp.stack([kept, got_rows.reshape(kept.shape)], axis=1)
-        bit *= 2
-        if bit == blk_count:
+        senders = jnp.stack([kept, got_rows], axis=1)
+        bit //= 2
+        if bit == 0:
             break
         view = senders.reshape(blk_count // (2 * bit), 2, bit * mcap, width)
         kept, given = view[:, 0], view[:, 1]

time: 80 us -> 77 us (0.963)
  waiting for transfers between devices: 22.8 us -> 20.2 us
    ppermute x27, waiting for transfers between devices: 22.8 us -> 20.2 us  [swap(): lax.ppermute(rows, axis, [(i, i ^ mask) for i in range(lax.axis_size(axis...]
  transfers between devices with their start and end apart: 27 -> 27, of which waited for: 11 -> 11; matrix products, arithmetic and copies ran while one was open for 1% -> 1% of each run, Pallas kernels for 9% -> 10%
where the time goes in v7:
time: 77 us; the launch traced here: 76.8 us
  starting transfers between devices  36.7 us (48%)
  waiting for transfers between devices  20.2 us (26%)
  Pallas kernels  17.1 us (22%)
  local copies, waits for them, and re-layouts  1.57 us (2%)
  between operations  1.02 us (1%)
    ppermute x27, starting transfers between devices, swap(): lax.ppermute(rows, axis, [(i, i ^ mask) for i in range(lax.axis_size(axis...  36.7 us
    ppermute x27, waiting for transfers between devices, swap(): lax.ppermute(rows, axis, [(i, i ^ mask) for i in range(lax.axis_size(axis...  20.2 us
    pallas_call x15, Pallas kernels, call(): pl.pallas_call(kernel, out_shape=tuple((pltpu.VMEM(out.shape, out.dtype)...  17.1 us
    unnamed x35, local copies, waits for them, and re-layouts  1.55 us
  transfers between devices with their start and end apart: 27, of which 11 were waited for; matrix products, arithmetic and copies ran while one was open for 1% of the time, Pallas kernels for 10%

profile of v7, /device:TPU:0, one launch (start us, length us, event | category | flops | bytes accessed | tf_op | source)
XLA Modules:
  0.0 76.8 jit_solution(4153098113957679439)
XLA Ops:
  0.7 2.3 %shard_map.178 = (bf16[64,512]{1,0:T(8,128)(2,1)S(1)}, bf16[64,512]{1,0:T(8,128)(2,1)S(1)}, bf16[64,512]{1,0:T(8,128)(2,1)S(1)}, bf16[64,512]{1,0:T(8,128)(2,1)S...) custom-call(s32[1,512]{1,0:T(1,128)} %node_ref.5, ...), custom_call_target="tpu_custom_call" | custom-call | flops 536870912 | tf_op jit(solution)/shard_map/pallas_call | solution.py:85
  3.0 3.1 %collective-permute-start.1 = (bf16[64,512]{1,0:T(8,128)(2,1)S(1)}, bf16[64,512]{1,0:T(8,128)(2,1)S(1)}, u32[]{:S(2)}, u32[]{:S(2)}) collective-permute-start(bf16[64,512]{1,0:T(8,128)(2,1)S(1)} %get-tuple-element.34), channel_id=1, source_target_pairs={{0,4},{4,0},{8,12},{12,8},{16,20},{20,16},{24,28},{28,24},{1,5},{5... | collective-permute-start | bytes 196616 | tf_op jit(solution)/shard_map/ppermute | solution.py:323
  6.1 1.6 %collective-permute-start.2 = (bf16[64,512]{1,0:T(8,128)(2,1)S(1)}, bf16[64,512]{1,0:T(8,128)(2,1)S(1)}, u32[]{:S(2)}, u32[]{:S(2)}) collective-permute-start(bf16[64,512]{1,0:T(8,128)(2,1)S(1)} %get-tuple-element.35), channel_id=1, source_target_pairs={{0,8},{4,12},{8,0},{12,4},{16,24},{20,28},{24,16},{28,20},{1,9},{5... | collective-permute-start | bytes 196616 | tf_op jit(solution)/shard_map/ppermute | solution.py:323
  7.7 1.5 %collective-permute-start = (s32[1,64]{1,0:T(1,128)S(1)}, s32[1,64]{1,0:T(1,128)S(1)}, u32[]{:S(2)}, u32[]{:S(2)}) collective-permute-start(s32[1,64]{1,0:T(1,128)S(1)} %copy-done.13), channel_id=1, source_target_pairs={{0,2},{1,3},{2,0},{3,1},{4,6},{5,7},{6,4},{7,5},{8,10},{9,11},{10,... | collective-permute-start | bytes 776 | tf_op jit(solution)/shard_map/ppermute | solution.py:323
  9.5 2.6 %collective-permute-start.4 = (bf16[64,512]{1,0:T(8,128)(2,1)S(1)}, bf16[64,512]{1,0:T(8,128)(2,1)S(1)}, u32[]{:S(2)}, u32[]{:S(2)}) collective-permute-start(bf16[64,512]{1,0:T(8,128)(2,1)S(1)} %get-tuple-element.37), channel_id=1, source_target_pairs={{0,16},{4,20},{8,24},{12,28},{16,0},{20,4},{24,8},{28,12},{1,17},{... | collective-permute-start | bytes 196616 | tf_op jit(solution)/shard_map/ppermute | solution.py:323
  12.1 1.6 %collective-permute-start.5 = (bf16[64,512]{1,0:T(8,128)(2,1)S(1)}, bf16[64,512]{1,0:T(8,128)(2,1)S(1)}, u32[]{:S(2)}, u32[]{:S(2)}) collective-permute-start(bf16[64,512]{1,0:T(8,128)(2,1)S(1)} %get-tuple-element.38), channel_id=1, source_target_pairs={{0,20},{4,16},{8,28},{12,24},{16,4},{20,0},{24,12},{28,8},{1,21},{... | collective-permute-start | bytes 196616 | tf_op jit(solution)/shard_map/ppermute | solution.py:323
  13.8 3.3 %collective-permute-start.6 = (bf16[64,512]{1,0:T(8,128)(2,1)S(1)}, bf16[64,512]{1,0:T(8,128)(2,1)S(1)}, u32[]{:S(2)}, u32[]{:S(2)}) collective-permute-start(bf16[64,512]{1,0:T(8,128)(2,1)S(1)} %get-tuple-element.39), channel_id=1, source_target_pairs={{0,24},{4,28},{8,16},{12,20},{16,8},{20,12},{24,0},{28,4},{1,25},{... | collective-permute-start | bytes 196616 | tf_op jit(solution)/shard_map/ppermute | solution.py:323
  17.0 1.5 %collective-permute-start.7 = (bf16[64,512]{1,0:T(8,128)(2,1)S(1)}, bf16[64,512]{1,0:T(8,128)(2,1)S(1)}, u32[]{:S(2)}, u32[]{:S(2)}) collective-permute-start(bf16[64,512]{1,0:T(8,128)(2,1)S(1)} %get-tuple-element.40), channel_id=1, source_target_pairs={{0,28},{4,24},{8,20},{12,16},{16,12},{20,8},{24,4},{28,0},{1,29},{... | collective-permute-start | bytes 196616 | tf_op jit(solution)/shard_map/ppermute | solution.py:323
  18.6 2.8 %shard_map.177.part_ref = f32[1024,512]{1,0:T(8,128)S(1)} custom-call(s32[1,1024]{1,0:T(1,128)S(1)} %bitcast.32, bf16[512,512]{1,0:T(8,128)(2,1)S(1)} %copy-done.8, bf16[4,512,512]{2,1,0:T(8,128)(2,1)S(1)} %copy-done.4, f32[5,2,512]{2,1,0:T(2,128)S(1)} %copy-done.7, bf16[1024,512]{1,0:T(8,128)(2,1)} %edges_hbm.1), custom_call_target="tpu_custom_call" | custom-call | flops 1610612736 | tf_op jit(solution)/shard_map/pallas_call | solution.py:85
  22.1 2.0 %collective-permute-done.7.refs_7_ = bf16[64,512]{1,0:T(8,128)(2,1)S(1)} collective-permute-done((bf16[64,512]{1,0:T(8,128)(2,1)S(1)}, bf16[64,512]{1,0:T(8,128)(2,1)S(1)}, u32[]{:S(2)}, u32[]{:S(2)}) %collective-permute-start.7) | collective-permute-done | bytes 65568 | tf_op jit(solution)/shard_map/ppermute | solution.py:323
  24.1 2.3 %shard_map.179 = (bf16[64,512]{1,0:T(8,128)(2,1)S(1)}, bf16[64,512]{1,0:T(8,128)(2,1)S(1)}, bf16[64,512]{1,0:T(8,128)(2,1)S(1)}, bf16[64,512]{1,0:T(8,128)(2,1)S...) custom-call(s32[1,1024]{1,0:T(1,128)S(1)} %bitcast.33, ...), custom_call_target="tpu_custom_call" | custom-call | flops 1610612736 | tf_op jit(solution)/shard_map/pallas_call | solution.py:85
  26.4 1.4 %collective-permute-start.10 = (bf16[64,512]{1,0:T(8,128)(2,1)S(1)}, bf16[64,512]{1,0:T(8,128)(2,1)S(1)}, u32[]{:S(2)}, u32[]{:S(2)}) collective-permute-start(bf16[64,512]{1,0:T(8,128)(2,1)S(1)} %get-tuple-element.44), channel_id=1, source_target_pairs={{0,8},{4,12},{8,0},{12,4},{16,24},{20,28},{24,16},{28,20},{1,9},{5... | collective-permute-start | bytes 196616 | tf_op jit(solution)/shard_map/ppermute | solution.py:323
  28.4 2.5 %collective-permute-start.12 = (bf16[64,512]{1,0:T(8,128)(2,1)S(1)}, bf16[64,512]{1,0:T(8,128)(2,1)S(1)}, u32[]{:S(2)}, u32[]{:S(2)}) collective-permute-start(bf16[64,512]{1,0:T(8,128)(2,1)S(1)} %get-tuple-element.46), channel_id=1, source_target_pairs={{0,16},{4,20},{8,24},{12,28},{16,0},{20,4},{24,8},{28,12},{1,17},{... | collective-permute-start | bytes 196616 | tf_op jit(solution)/shard_map/ppermute | solution.py:323
  32.3 2.0 %collective-permute-start.14 = (bf16[64,512]{1,0:T(8,128)(2,1)S(1)}, bf16[64,512]{1,0:T(8,128)(2,1)S(1)}, u32[]{:S(2)}, u32[]{:S(2)}) collective-permute-start(bf16[64,512]{1,0:T(8,128)(2,1)S(1)} %get-tuple-element.48), channel_id=1, source_target_pairs={{0,24},{4,28},{8,16},{12,20},{16,8},{20,12},{24,0},{28,4},{1,25},{... | collective-permute-start | bytes 196616 | tf_op jit(solution)/shard_map/ppermute | solution.py:323
  34.3 1.8 %collective-permute-start.15 = (bf16[64,512]{1,0:T(8,128)(2,1)S(1)}, bf16[64,512]{1,0:T(8,128)(2,1)S(1)}, u32[]{:S(2)}, u32[]{:S(2)}) collective-permute-start(bf16[64,512]{1,0:T(8,128)(2,1)S(1)} %get-tuple-element.49), channel_id=1, source_target_pairs={{0,28},{4,24},{8,20},{12,16},{16,12},{20,8},{24,4},{28,0},{1,29},{... | collective-permute-start | bytes 196616 | tf_op jit(solution)/shard_map/ppermute | solution.py:323
  36.1 1.5 %collective-permute-start.9 = (bf16[64,512]{1,0:T(8,128)(2,1)S(1)}, bf16[64,512]{1,0:T(8,128)(2,1)S(1)}, u32[]{:S(2)}, u32[]{:S(2)}) collective-permute-start(bf16[64,512]{1,0:T(8,128)(2,1)S(1)} %get-tuple-element.43), channel_id=1, source_target_pairs={{0,4},{4,0},{8,12},{12,8},{16,20},{20,16},{24,28},{28,24},{1,5},{5... | collective-permute-start | bytes 196616 | tf_op jit(solution)/shard_map/ppermute | solution.py:323
  37.6 4.7 %collective-permute-done.13.refs_5_ = bf16[64,512]{1,0:T(8,128)(2,1)S(1)} collective-permute-done((bf16[64,512]{1,0:T(8,128)(2,1)S(1)}, bf16[64,512]{1,0:T(8,128)(2,1)S(1)}, u32[]{:S(2)}, u32[]{:S(2)}) %collective-permute-start.13) | collective-permute-done | bytes 65568 | tf_op jit(solution)/shard_map/ppermute | solution.py:323
  49.8 3.4 %collective-permute-start.21 = (bf16[1,32,512]{2,1,0:T(8,128)(2,1)S(1)}, bf16[1,32,512]{2,1,0:T(8,128)(2,1)S(1)}, u32[]{:S(2)}, u32[]{:S(2)}) collective-permute-start(bf16[1,32,512]{2,1,0:T(8,128)(2,1)S(1)} %bitcast.31), channel_id=1, source_target_pairs={{0,16},{4,20},{8,24},{12,28},{16,0},{20,4},{24,8},{28,12},{1,17},{... | collective-permute-start | bytes 98312 | tf_op jit(solution)/shard_map/ppermute | solution.py:323
  53.2 1.9 %collective-permute-done.21 = bf16[1,32,512]{2,1,0:T(8,128)(2,1)S(1)} collective-permute-done((bf16[1,32,512]{2,1,0:T(8,128)(2,1)S(1)}, bf16[1,32,512]{2,1,0:T(8,128)(2,1)S(1)}, u32[]{:S(2)}, u32[]{:S(2)}) %collective-permute-start.21) | collective-permute-done | bytes 32800 | tf_op jit(solution)/shard_map/ppermute | solution.py:323
  55.1 2.4 %collective-permute-start.22 = (bf16[2,16,512]{2,1,0:T(8,128)(2,1)S(1)}, bf16[2,16,512]{2,1,0:T(8,128)(2,1)S(1)}, u32[]{:S(2)}, u32[]{:S(2)}) collective-permute-start(bf16[2,16,512]{2,1,0:T(8,128)(2,1)S(1)} %get-tuple-element.69), channel_id=1, source_target_pairs={{0,8},{4,12},{8,0},{12,4},{16,24},{20,28},{24,16},{28,20},{1,9},{5... | collective-permute-start | bytes 98312 | tf_op jit(solution)/shard_map/ppermute | solution.py:323
  57.5 1.9 %collective-permute-done.22 = bf16[2,16,512]{2,1,0:T(8,128)(2,1)S(1)} collective-permute-done((bf16[2,16,512]{2,1,0:T(8,128)(2,1)S(1)}, bf16[2,16,512]{2,1,0:T(8,128)(2,1)S(1)}, u32[]{:S(2)}, u32[]{:S(2)}) %collective-permute-start.22) | collective-permute-done | bytes 32800 | tf_op jit(solution)/shard_map/ppermute | solution.py:323
  60.9 3.4 %collective-permute-done.23 = bf16[4,8,512]{2,1,0:T(8,128)(2,1)S(1)} collective-permute-done((bf16[4,8,512]{2,1,0:T(8,128)(2,1)S(1)}, bf16[4,8,512]{2,1,0:T(8,128)(2,1)S(1)}, u32[]{:S(2)}, u32[]{:S(2)}) %collective-permute-start.23) | collective-permute-done | bytes 32800 | tf_op jit(solution)/shard_map/ppermute | solution.py:323
  65.8 1.9 %shard_map.187 = (bf16[160,512]{1,0:T(8,128)(2,1)S(1)}, bf16[1024,512]{1,0:T(8,128)(2,1)S(1)}) custom-call(s32[1,1024]{1,0:T(1,128)S(1)} %bitcast.30, s32[1,1024]{1,0:T(1,128)S(1)} %bitcast.26, f32[1024,512]{1,0:T(8,128)S(1)} %shard_map.185.part_ref, bf16[64,512]{1,0:T(8,128)(2,1)S(1)} %bitcast.24, bf16[4,512,512]{2,1,0:T(8,128)(2,1)S(1)} %copy-done, ...), custom_call_target="tpu_custom_call" | custom-call | flops 1073741824 | tf_op jit(solution)/shard_map/pallas_call | solution.py:85
  71.6 3.9 %collective-permute-done.26.got_ref = bf16[160,512]{1,0:T(8,128)(2,1)S(1)} collective-permute-done((bf16[160,512]{1,0:T(8,128)(2,1)S(1)}, bf16[160,512]{1,0:T(8,128)(2,1)S(1)}, u32[]{:S(2)}, u32[]{:S(2)}) %collective-permute-start.26) | collective-permute-done | bytes 163872 | tf_op jit(solution)/shard_map/ppermute | solution.py:323
  (88 shorter events, 18.6 us)
Async XLA Ops:
  3.0 10.7 %collective-permute-start.1 = (bf16[64,512]{1,0:T(8,128)(2,1)S(1)}, bf16[64,512]{1,0:T(8,128)(2,1)S(1)}, u32[]{:S(2)}, u32[]{:S(2)}) collective-permute-start(bf16[64,512]{1,0:T(8,128)(2,1)S(1)} %get-tuple-element.34), channel_id=1, source_target_pairs={{0,4},{4,0},{8,12},{12,8},{16,20},{20,16},{24,28},{28,24},{1,5},{5... | collective-permute-start | bytes 196616 | tf_op jit(solution)/shard_map/ppermute | solution.py:323
  6.1 11.0 %collective-permute-start.2 = (bf16[64,512]{1,0:T(8,128)(2,1)S(1)}, bf16[64,512]{1,0:T(8,128)(2,1)S(1)}, u32[]{:S(2)}, u32[]{:S(2)}) collective-permute-start(bf16[64,512]{1,0:T(8,128)(2,1)S(1)} %get-tuple-element.35), channel_id=1, source_target_pairs={{0,8},{4,12},{8,0},{12,4},{16,24},{20,28},{24,16},{28,20},{1,9},{5... | collective-permute-start | bytes 196616 | tf_op jit(solution)/shard_map/ppermute | solution.py:323
  7.7 4.5 %collective-permute-start = (s32[1,64]{1,0:T(1,128)S(1)}, s32[1,64]{1,0:T(1,128)S(1)}, u32[]{:S(2)}, u32[]{:S(2)}) collective-permute-start(s32[1,64]{1,0:T(1,128)S(1)} %copy-done.13), channel_id=1, source_target_pairs={{0,2},{1,3},{2,0},{3,1},{4,6},{5,7},{6,4},{7,5},{8,10},{9,11},{10,... | collective-permute-start | bytes 776 | tf_op jit(solution)/shard_map/ppermute | solution.py:323
  9.1 12.3 %collective-permute-start.3 = (bf16[64,512]{1,0:T(8,128)(2,1)S(1)}, bf16[64,512]{1,0:T(8,128)(2,1)S(1)}, u32[]{:S(2)}, u32[]{:S(2)}) collective-permute-start(bf16[64,512]{1,0:T(8,128)(2,1)S(1)} %get-tuple-element.36), channel_id=1, source_target_pairs={{0,12},{4,8},{8,4},{12,0},{16,28},{20,24},{24,20},{28,16},{1,13},{... | collective-permute-start | bytes 196616 | tf_op jit(solution)/shard_map/ppermute | solution.py:323
  9.5 11.9 %collective-permute-start.4 = (bf16[64,512]{1,0:T(8,128)(2,1)S(1)}, bf16[64,512]{1,0:T(8,128)(2,1)S(1)}, u32[]{:S(2)}, u32[]{:S(2)}) collective-permute-start(bf16[64,512]{1,0:T(8,128)(2,1)S(1)} %get-tuple-element.37), channel_id=1, source_target_pairs={{0,16},{4,20},{8,24},{12,28},{16,0},{20,4},{24,8},{28,12},{1,17},{... | collective-permute-start | bytes 196616 | tf_op jit(solution)/shard_map/ppermute | solution.py:323
  12.1 10.0 %collective-permute-start.5 = (bf16[64,512]{1,0:T(8,128)(2,1)S(1)}, bf16[64,512]{1,0:T(8,128)(2,1)S(1)}, u32[]{:S(2)}, u32[]{:S(2)}) collective-permute-start(bf16[64,512]{1,0:T(8,128)(2,1)S(1)} %get-tuple-element.38), channel_id=1, source_target_pairs={{0,20},{4,16},{8,28},{12,24},{16,4},{20,0},{24,12},{28,8},{1,21},{... | collective-permute-start | bytes 196616 | tf_op jit(solution)/shard_map/ppermute | solution.py:323
  13.8 8.3 %collective-permute-start.6 = (bf16[64,512]{1,0:T(8,128)(2,1)S(1)}, bf16[64,512]{1,0:T(8,128)(2,1)S(1)}, u32[]{:S(2)}, u32[]{:S(2)}) collective-permute-start(bf16[64,512]{1,0:T(8,128)(2,1)S(1)} %get-tuple-element.39), channel_id=1, source_target_pairs={{0,24},{4,28},{8,16},{12,20},{16,8},{20,12},{24,0},{28,4},{1,25},{... | collective-permute-start | bytes 196616 | tf_op jit(solution)/shard_map/ppermute | solution.py:323
  17.0 7.1 %collective-permute-start.7 = (bf16[64,512]{1,0:T(8,128)(2,1)S(1)}, bf16[64,512]{1,0:T(8,128)(2,1)S(1)}, u32[]{:S(2)}, u32[]{:S(2)}) collective-permute-start(bf16[64,512]{1,0:T(8,128)(2,1)S(1)} %get-tuple-element.40), channel_id=1, source_target_pairs={{0,28},{4,24},{8,20},{12,16},{16,12},{20,8},{24,4},{28,0},{1,29},{... | collective-permute-start | bytes 196616 | tf_op jit(solution)/shard_map/ppermute | solution.py:323
  26.4 7.9 %collective-permute-start.10 = (bf16[64,512]{1,0:T(8,128)(2,1)S(1)}, bf16[64,512]{1,0:T(8,128)(2,1)S(1)}, u32[]{:S(2)}, u32[]{:S(2)}) collective-permute-start(bf16[64,512]{1,0:T(8,128)(2,1)S(1)} %get-tuple-element.44), channel_id=1, source_target_pairs={{0,8},{4,12},{8,0},{12,4},{16,24},{20,28},{24,16},{28,20},{1,9},{5... | collective-permute-start | bytes 196616 | tf_op jit(solution)/shard_map/ppermute | solution.py:323
  27.8 8.3 %collective-permute-start.11 = (bf16[64,512]{1,0:T(8,128)(2,1)S(1)}, bf16[64,512]{1,0:T(8,128)(2,1)S(1)}, u32[]{:S(2)}, u32[]{:S(2)}) collective-permute-start(bf16[64,512]{1,0:T(8,128)(2,1)S(1)} %get-tuple-element.45), channel_id=1, source_target_pairs={{0,12},{4,8},{8,4},{12,0},{16,28},{20,24},{24,20},{28,16},{1,13},{... | collective-permute-start | bytes 196616 | tf_op jit(solution)/shard_map/ppermute | solution.py:323
  28.4 3.9 %collective-permute-start.8 = (s32[2,64]{1,0:T(2,128)S(1)}, s32[2,64]{1,0:T(2,128)S(1)}, u32[]{:S(2)}, u32[]{:S(2)}) collective-permute-start(s32[2,64]{1,0:T(2,128)S(1)} %get-tuple-element.41.own_ref), channel_id=1, source_target_pairs={{0,1},{1,0},{2,3},{3,2},{4,5},{5,4},{6,7},{7,6},{8,9},{9,8},{10,11... | collective-permute-start | bytes 1544 | tf_op jit(solution)/shard_map/ppermute | solution.py:323
  28.4 9.2 %collective-permute-start.12 = (bf16[64,512]{1,0:T(8,128)(2,1)S(1)}, bf16[64,512]{1,0:T(8,128)(2,1)S(1)}, u32[]{:S(2)}, u32[]{:S(2)}) collective-permute-start(bf16[64,512]{1,0:T(8,128)(2,1)S(1)} %get-tuple-element.46), channel_id=1, source_target_pairs={{0,16},{4,20},{8,24},{12,28},{16,0},{20,4},{24,8},{28,12},{1,17},{... | collective-permute-start | bytes 196616 | tf_op jit(solution)/shard_map/ppermute | solution.py:323
  30.9 11.3 %collective-permute-start.13 = (bf16[64,512]{1,0:T(8,128)(2,1)S(1)}, bf16[64,512]{1,0:T(8,128)(2,1)S(1)}, u32[]{:S(2)}, u32[]{:S(2)}) collective-permute-start(bf16[64,512]{1,0:T(8,128)(2,1)S(1)} %get-tuple-element.47), channel_id=1, source_target_pairs={{0,20},{4,16},{8,28},{12,24},{16,4},{20,0},{24,12},{28,8},{1,21},{... | collective-permute-start | bytes 196616 | tf_op jit(solution)/shard_map/ppermute | solution.py:323
  32.3 10.0 %collective-permute-start.14 = (bf16[64,512]{1,0:T(8,128)(2,1)S(1)}, bf16[64,512]{1,0:T(8,128)(2,1)S(1)}, u32[]{:S(2)}, u32[]{:S(2)}) collective-permute-start(bf16[64,512]{1,0:T(8,128)(2,1)S(1)} %get-tuple-element.48), channel_id=1, source_target_pairs={{0,24},{4,28},{8,16},{12,20},{16,8},{20,12},{24,0},{28,4},{1,25},{... | collective-permute-start | bytes 196616 | tf_op jit(solution)/shard_map/ppermute | solution.py:323
  34.3 7.9 %collective-permute-start.15 = (bf16[64,512]{1,0:T(8,128)(2,1)S(1)}, bf16[64,512]{1,0:T(8,128)(2,1)S(1)}, u32[]{:S(2)}, u32[]{:S(2)}) collective-permute-start(bf16[64,512]{1,0:T(8,128)(2,1)S(1)} %get-tuple-element.49), channel_id=1, source_target_pairs={{0,28},{4,24},{8,20},{12,16},{16,12},{20,8},{24,4},{28,0},{1,29},{... | collective-permute-start | bytes 196616 | tf_op jit(solution)/shard_map/ppermute | solution.py:323
  36.1 6.4 %collective-permute-start.9 = (bf16[64,512]{1,0:T(8,128)(2,1)S(1)}, bf16[64,512]{1,0:T(8,128)(2,1)S(1)}, u32[]{:S(2)}, u32[]{:S(2)}) collective-permute-start(bf16[64,512]{1,0:T(8,128)(2,1)S(1)} %get-tuple-element.43), channel_id=1, source_target_pairs={{0,4},{4,0},{8,12},{12,8},{16,20},{20,16},{24,28},{28,24},{1,5},{5... | collective-permute-start | bytes 196616 | tf_op jit(solution)/shard_map/ppermute | solution.py:323
  44.3 4.8 %collective-permute-start.20 = (bf16[64,512]{1,0:T(8,128)(2,1)S(1)}, bf16[64,512]{1,0:T(8,128)(2,1)S(1)}, u32[]{:S(2)}, u32[]{:S(2)}) collective-permute-start(bf16[64,512]{1,0:T(8,128)(2,1)S(1)} %get-tuple-element.64), channel_id=1, source_target_pairs={{0,2},{1,3},{2,0},{3,1},{4,6},{5,7},{6,4},{7,5},{8,10},{9,11},{10,... | collective-permute-start | bytes 196616 | tf_op jit(solution)/shard_map/ppermute | solution.py:323
  45.2 14.2 %collective-permute-start.17 = (bf16[320,512]{1,0:T(8,128)(2,1)S(1)}, bf16[320,512]{1,0:T(8,128)(2,1)S(1)}, u32[]{:S(2)}, u32[]{:S(2)}) collective-permute-start(bf16[320,512]{1,0:T(8,128)(2,1)S(1)} %add_convert_fusion.half_ref), channel_id=1, source_target_pairs={{0,2},{1,3},{2,0},{3,1},{4,6},{5,7},{6,4},{7,5},{8,10},{9,11},{10,... | collective-permute-start | bytes 983048 | tf_op jit(solution)/shard_map/ppermute | solution.py:323
  49.8 5.3 %collective-permute-start.21 = (bf16[1,32,512]{2,1,0:T(8,128)(2,1)S(1)}, bf16[1,32,512]{2,1,0:T(8,128)(2,1)S(1)}, u32[]{:S(2)}, u32[]{:S(2)}) collective-permute-start(bf16[1,32,512]{2,1,0:T(8,128)(2,1)S(1)} %bitcast.31), channel_id=1, source_target_pairs={{0,16},{4,20},{8,24},{12,28},{16,0},{20,4},{24,8},{28,12},{1,17},{... | collective-permute-start | bytes 98312 | tf_op jit(solution)/shard_map/ppermute | solution.py:323
  55.1 4.3 %collective-permute-start.22 = (bf16[2,16,512]{2,1,0:T(8,128)(2,1)S(1)}, bf16[2,16,512]{2,1,0:T(8,128)(2,1)S(1)}, u32[]{:S(2)}, u32[]{:S(2)}) collective-permute-start(bf16[2,16,512]{2,1,0:T(8,128)(2,1)S(1)} %get-tuple-element.69), channel_id=1, source_target_pairs={{0,8},{4,12},{8,0},{12,4},{16,24},{20,28},{24,16},{28,20},{1,9},{5... | collective-permute-start | bytes 98312 | tf_op jit(solution)/shard_map/ppermute | solution.py:323
  60.3 4.1 %collective-permute-start.18 = (bf16[320,512]{1,0:T(8,128)(2,1)S(1)}, bf16[320,512]{1,0:T(8,128)(2,1)S(1)}, u32[]{:S(2)}, u32[]{:S(2)}) collective-permute-start(bf16[320,512]{1,0:T(8,128)(2,1)S(1)} %shard_map.184.own_ref.half_ref), channel_id=1, source_target_pairs={{0,1},{1,0},{2,3},{3,2},{4,5},{5,4},{6,7},{7,6},{8,9},{9,8},{10,11... | collective-permute-start | bytes 983048 | tf_op jit(solution)/shard_map/ppermute | solution.py:323
  60.4 4.0 %collective-permute-start.23 = (bf16[4,8,512]{2,1,0:T(8,128)(2,1)S(1)}, bf16[4,8,512]{2,1,0:T(8,128)(2,1)S(1)}, u32[]{:S(2)}, u32[]{:S(2)}) collective-permute-start(bf16[4,8,512]{2,1,0:T(8,128)(2,1)S(1)} %get-tuple-element.67), channel_id=1, source_target_pairs={{0,4},{4,0},{8,12},{12,8},{16,20},{20,16},{24,28},{28,24},{1,5},{5... | collective-permute-start | bytes 98312 | tf_op jit(solution)/shard_map/ppermute | solution.py:323
  68.4 3.2 %collective-permute-start.24 = (bf16[160,512]{1,0:T(8,128)(2,1)S(1)}, bf16[160,512]{1,0:T(8,128)(2,1)S(1)}, u32[]{:S(2)}, u32[]{:S(2)}) collective-permute-start(bf16[160,512]{1,0:T(8,128)(2,1)S(1)} %get-tuple-element.61), channel_id=1, source_target_pairs={{0,1},{1,0},{2,3},{3,2},{4,5},{5,4},{6,7},{7,6},{8,9},{9,8},{10,11... | collective-permute-start | bytes 491528 | tf_op jit(solution)/shard_map/ppermute | solution.py:323
  69.3 6.2 %collective-permute-start.26 = (bf16[160,512]{1,0:T(8,128)(2,1)S(1)}, bf16[160,512]{1,0:T(8,128)(2,1)S(1)}, u32[]{:S(2)}, u32[]{:S(2)}) collective-permute-start(bf16[160,512]{1,0:T(8,128)(2,1)S(1)} %add_convert_fusion.1), channel_id=1, source_target_pairs={{0,2},{1,3},{2,0},{3,1},{4,6},{5,7},{6,4},{7,5},{8,10},{9,11},{10,... | collective-permute-start | bytes 491528 | tf_op jit(solution)/shard_map/ppermute | solution.py:323
  (19 other events, 157.2 us)
